TPU v7x, 32 devices: a whole 2x2x4 slice. The times are simulated.
32 devices in a mesh: scen: 8 (over y, x, core), col: 4 (over z).
Axes of the slice: x: 2, y: 2, z: 4, core: 2. Of those that a mesh axis runs over, the one named last changes fastest.
Arguments:
- coef: float32 [4096, 8192], P('scen', 'col'), as said below
- mask: int32 [4096], replicated, may hold values from 0 to 1, as said below
- assign: int32 [512], replicated, may hold values from 0 to 511, each once
Outputs:
- master: float32 [4, 2048, 4096], P('col', 'scen')
Inputs may be any that keep to these rules, and one draw needn't show every extreme that they name: `mask`: in each aligned block of 512 cuts (the cuts of one index of scen) exactly 256 are active. `coef`: magnitudes of rows and of columns differ widely; entries are finite and not zero on every row.
All inputs are finite; a program needn't handle non-finite values.
Results may differ from a plain program's by a relative error of at most 0.00007.
Values sent between devices are 32-bit elements; how exact they have to be, the bound alone decides.
No kernel may reach another device: no remote copies, remote signals or barrier semaphores. Data moves between devices by JAX's collectives and lax.ppermute only.
A program may use at most 128 MiB of HBM per device.

v0:
```python
import jax
import jax.numpy as jnp
from jax import lax
from jax.sharding import PartitionSpec as P

NV = 8192
K = 8
ACT_DEV = 256


EPS = 1e-06


def on_device(coef, mask, assign):
    rows, width = coef.shape
    groups = lax.axis_size("scen")
    slice_width = width // groups
    cut_total = groups * rows
    slot_total = cut_total // K
    active_total = ACT_DEV * groups
    partial_value = jnp.sum(coef * coef, axis=1)
    total = lax.psum(partial_value, "col")
    row_norm = jnp.sqrt(total / NV + EPS)
    device_index = lax.axis_index("scen")
    own_mask = lax.dynamic_slice_in_dim(mask, device_index * rows, rows)
    live = own_mask.astype(jnp.float32)
    scaled = coef / row_norm[:, None] * live[:, None]
    flipped = scaled.T.reshape(groups, slice_width, rows)
    inverse = jnp.argsort(assign, stable=True)
    kept_rows = jnp.argsort(1 - own_mask, stable=True)[:ACT_DEV]
    picked = jnp.take(flipped, kept_rows, axis=2)
    arrived = lax.all_to_all(picked, "scen", split_axis=0, concat_axis=2, tiled=True)
    norm = jnp.sqrt(jnp.sum(arrived * arrived, axis=2, keepdims=True) / active_total + EPS)
    equil = (arrived / norm).reshape(slice_width, groups, ACT_DEV)
    block_masks = mask.reshape(groups, rows)
    chosen = jnp.argsort(1 - block_masks, axis=1, stable=True)[:, :ACT_DEV]
    bundle = min(groups, 8)
    rounds = groups // bundle
    chosen_sets = chosen.reshape(rounds, bundle, ACT_DEV)
    equil_sets = equil.reshape(slice_width, rounds, bundle, ACT_DEV).transpose(1, 0, 2, 3)
    local_rows = jnp.arange(rows, dtype=jnp.int32)

    def place(pair):
        chosen_set, equil_set = pair
        placing = (chosen_set[:, :, None] == local_rows[None, None, :]).astype(jnp.float32)
        return jnp.einsum("sga,gar->sgr", equil_set, placing, precision=lax.Precision.HIGHEST)

    placed = lax.map(place, (chosen_sets, equil_sets))
    whole = placed.transpose(1, 0, 2, 3).reshape(1, slice_width, cut_total)
    slotted = whole.reshape(1, slice_width, slot_total, K)
    return jnp.take(slotted, inverse, axis=2).reshape(1, slice_width, cut_total)


def solution(mesh):
    in_specs = (P("scen", "col"), P(), P())
    out_specs = P("col", "scen", None)
    return jax.shard_map(
        on_device, mesh=mesh, in_specs=in_specs, out_specs=out_specs, check_vma=False
    )
```

profile of v0, /device:TPU:0, one launch (start us, length us, event | category | flops | bytes accessed | tf_op | source)
XLA Modules:
  0.0 95.5 jit_solution(2898095278292690837)
XLA Ops:
  6.5 0.8 dynamic-slice_subtract_fusion
  7.3 3.8 %sort.50 = (s32[512]{0:T(512)}, s32[512]{0:T(512)S(1)}) sort(s32[512]{0:T(512)S(1)} %get-tuple-element.26, s32[512]{0:T(512)S(1)} %iota.20), dimensions={0}, to_apply=%region_2.0 | sort | flops 4608 | bytes 8192 | tf_op jit(solution)/shard_map/jit(argsort)/sort | solution.py:30
  11.1 2.5 %multiply_reduce_fusion = f32[512]{0:T(512)S(1)} fusion(f32[512,2048]{1,0:T(8,128)} %param.3), kind=kLoop, calls=%fused_computation.4 | loop fusion | flops 2096640 | bytes 4196352 | tf_op jit(solution)/shard_map/reduce_sum | solution.py:21
  13.6 13.5 %psum.7 = f32[512]{0:T(512)S(1)} all-reduce(f32[512]{0:T(512)S(1)} %multiply_reduce_fusion), channel_id=1, replica_groups=mesh['scen'=8,'col'=4] {'col'}, use_global_device_ids=true, to_apply=%region_4.5 | all-reduce | flops 512 | bytes 4096 | tf_op jit(solution)/shard_map/psum | solution.py:22
  27.1 2.6 %divide_multiply_fusion = f32[512,2048]{1,0:T(8,128)S(1)} fusion(f32[512,2048]{1,0:T(8,128)} %param.3, f32[512]{0:T(512)S(1)} %get-tuple-element.27, f32[512]{0:T(512)S(1)} %add_sqrt_fusion), kind=kLoop, calls=%fused_computation.3 | loop fusion | flops 2097152 | bytes 8392704 | tf_op jit(solution)/shard_map/mul | solution.py:27
  29.7 4.0 %copy.11 = f32[64,8,8,256]{3,2,1,0:T(8,128)} copy(f32[64,8,8,256]{3,1,2,0:T(8,128)S(1)} %bitcast.25) | data formatting | bytes 8388608
  33.7 2.9 %gather_fusion = f32[256,8,256]{2,1,0:T(8,128)S(1)} fusion(f32[8,256,512]{1,0,2:T(8,128)} %bitcast.26, s32[1024]{0:T(1024)S(1)} %pad_clamp_fusion.1), kind=kCustom, calls=%fused_computation | custom fusion | bytes 4195328 | tf_op jit(solution)/shard_map/jit(_take)/gather | solution.py:31
  36.6 0.3 select_bitcast_fusion
  37.0 0.0 copy-start
  37.0 0.0 copy-start.1
  37.0 2.0 %copy.7 = f32[8,256,256]{1,2,0:T(8,128)} copy(f32[8,256,256]{1,0,2:T(8,128)S(1)} %select_bitcast_fusion) | data formatting | bytes 4194304 | tf_op jit(solution)/shard_map/jit(_take)/select_n | solution.py:31
  39.0 3.7 %all-to-all-start = ((f32[8,256,256]{1,2,0:T(8,128)}), f32[8,256,256]{1,2,0:T(8,128)S(1)}, u32[]{:S(2)}, u32[]{:S(2)}) async-start(f32[8,256,256]{1,2,0:T(8,128)} %copy.7), calls=%async_computation | async-start | bytes 4194304 | tf_op jit(solution)/shard_map/all_to_all | solution.py:32
  42.7 0.0 sort.52.cloned.1.call-start
  42.7 0.0 copy-done
  42.8 0.6 sub.17
  43.4 0.6 iota.19
  44.0 0.0 sort.52.cloned.1.call-update
  44.0 0.0 copy-done.1
  44.0 3.8 %sort.48 = (s32[512]{0:T(512)}, s32[512]{0:T(512)S(1)}) sort(s32[512]{0:T(512)S(1)} %copy-done.1, s32[512]{0:T(512)S(1)} %iota.18), dimensions={0}, to_apply=%region_0.0 | sort | flops 4608 | bytes 8192 | tf_op jit(solution)/shard_map/jit(argsort)/sort | solution.py:29
  47.8 0.1 broadcast_in_dim.39
  47.9 0.2 broadcast_in_dim.40
  48.1 0.5 sort.52.cloned.1.call-done
  48.6 0.7 slice.6
  49.3 20.0 %all-to-all-done = f32[8,256,256]{1,2,0:T(8,128)S(1)} async-done(((f32[8,256,256]{1,2,0:T(8,128)}), f32[8,256,256]{1,2,0:T(8,128)S(1)}, u32[]{:S(2)}, u32[]{:S(2)}) %all-to-all-start) | async-done | bytes 2097184 | tf_op jit(solution)/shard_map/all_to_all | solution.py:32
  69.3 0.3 fusion.1
  69.6 4.5 %fusion = f32[8,512,256]{2,1,0:T(8,128)} fusion(f32[8,256,256]{1,2,0:T(8,128)S(1)} %all-to-all-done, s32[8,256]{1,0:T(8,128)S(1)} %slice.6, f32[256]{0:T(256)S(1)} %add_sqrt_fusion.1), kind=kOutput, calls=%fused_computation.6 | convolution fusion | flops 3222798336 | bytes 6300672 | tf_op jit(solution)/shard_map/while/body/eval_jaxpr/sga,gar->sgr/dot_general | solution.py:46
  74.1 5.1 %gather_fusion.1 = f32[512,256,8]{1,2,0:T(8,128)} fusion(f32[256,512,8]{0,2,1:T(8,128)} %bitcast.24, s32[1024]{0:T(1024)S(1)} %pad_clamp_fusion), kind=kCustom, calls=%fused_computation.1 | custom fusion | bytes 8390656 | tf_op jit(solution)/shard_map/jit(_take)/gather | solution.py:51
  79.2 3.9 %bitcast_select_fusion = f32[1,256,4096]{1,2,0:T(8,128)} fusion(f32[512,256,8]{1,2,0:T(8,128)} %gather_fusion.1, pred[4096]{0:T(1024)(128)(4,1)S(1)} %broadcast_in_dim.40), kind=kLoop, calls=%fused_computation.2 | loop fusion | flops 1048576 | bytes 8392704 | tf_op jit(solution)/shard_map/jit(_take)/select_n | solution.py:51
  83.1 5.6 %copy.9 = f32[1,256,4096]{2,1,0:T(8,128)} copy(f32[1,256,4096]{1,2,0:T(8,128)} %bitcast_select_fusion) | data formatting | bytes 8388608 | tf_op jit(solution)/shard_map/jit(_take)/select_n | solution.py:51
  (11 shorter events, 0.1 us)
Async XLA Ops:
  37.0 5.8 %copy-start = (s32[4096]{0:T(1024)S(1)}, s32[4096]{0:T(1024)}, u32[]{:S(2)}) copy-start(s32[4096]{0:T(1024)} %param.4) | copy-start | bytes 49156
  37.0 7.0 %copy-start.1 = (s32[512]{0:T(512)S(1)}, s32[512]{0:T(512)}, u32[]{:S(2)}) copy-start(s32[512]{0:T(512)} %param.5) | copy-start | bytes 6148
  39.0 30.3 %all-to-all-start = ((f32[8,256,256]{1,2,0:T(8,128)}), f32[8,256,256]{1,2,0:T(8,128)S(1)}, u32[]{:S(2)}, u32[]{:S(2)}) async-start(f32[8,256,256]{1,2,0:T(8,128)} %copy.7), calls=%async_computation | async-start | bytes 4194304 | tf_op jit(solution)/shard_map/all_to_all | solution.py:32
  42.7 5.9 %sort.52.cloned.1.call-start = ((), (), s32[]{:S(2)}) async-start(), calls=%async_computation.1 | async-start | bytes 98336 | tf_op jit(solution)/shard_map/jit(argsort)/sort | solution.py:36
Sparse Core Ops, SparseCore 0:
  45.9 2.4 sort.54.cloned.1.call-done
  (1 shorter events, 0.0 us)
where the time goes:
time: 96.1 us; the launch traced here: 95.5 us
  local copies, waits for them, and re-layouts  22.3 us (23%)
  waiting for transfers between devices  20 us (21%)
  other arithmetic  18 us (19%)
  blocking collectives  13.5 us (14%)
  between operations  13.5 us (14%)
  matrix products  4.46 us (5%)
  starting transfers between devices  3.72 us (4%)
    all_to_all x1, waiting for transfers between devices, on_device(): lax.all_to_all(picked, 'scen', split_axis=0, concat_axis=2, tiled=True)  20 us
    psum x1, blocking collectives, on_device(): total = lax.psum(partial_value, 'col')  13.5 us
    select_n x1, local copies, waits for them, and re-layouts, on_device(): return jnp.take(slotted, inverse, axis=2).reshape(1, slice_width, cut_total)  5.59 us
    gather x1, local copies, waits for them, and re-layouts, on_device(): return jnp.take(slotted, inverse, axis=2).reshape(1, slice_width, cut_total)  5.08 us
    dot_general x1, matrix products, place(): jnp.einsum('sga,gar->sgr', equil_set, placing, precision=lax.Precision.HI...  4.46 us
    unnamed x6, local copies, waits for them, and re-layouts  4 us
    select_n x2, other arithmetic, on_device(): return jnp.take(slotted, inverse, axis=2).reshape(1, slice_width, cut_total)  3.91 us
    sort x1, other arithmetic, on_device(): kept_rows = jnp.argsort(1 - own_mask, stable=True)[:ACT_DEV]  3.77 us
  transfers between devices with their start and end apart: 1, of which 1 were waited for; matrix products, arithmetic and copies ran while one was open for 6% of the time, Pallas kernels for 0%

commit v1 on v0

--- a/solution.py
+++ b/solution.py
@@ -1,6 +1,10 @@
+import functools
+
 import jax
 import jax.numpy as jnp
 from jax import lax
+from jax.experimental import pallas as pl
+from jax.experimental.pallas import tpu as pltpu
 from jax.sharding import PartitionSpec as P
 
 NV = 8192
@@ -9,9 +13,262 @@
 
 
 EPS = 1e-06
-
-
-def on_device(coef, mask, assign):
+LANES = 128
+SUBLANES = 8
+CHUNKS = 4
+VMEM = pl.BlockSpec(memory_space=pltpu.VMEM)
+SMEM = pl.BlockSpec(memory_space=pltpu.SMEM)
+HBM = pl.BlockSpec(memory_space=pltpu.HBM)
+PARAMS = pltpu.CompilerParams(vmem_limit_bytes=24 * 1024 * 1024)
+
+
+def pick_kernel(groups, rows, slice_width, mask_ref, coef_ref, *refs):
+    outs = refs[:groups]
+    part_ref, coef_v, squares, live, order, sems, mask_sem = refs[groups:]
+    me = lax.axis_index("scen")
+    tiles = slice_width // LANES
+    chunk = rows // CHUNKS
+
+    def copy(c, k, h):
+        span = pl.ds(c * chunk, chunk)
+        column = pl.multiple_of((jnp.bitwise_xor(me, k) * tiles + h) * LANES, LANES)
+        t = k * tiles + h
+        return pltpu.make_async_copy(
+            coef_ref.at[span, pl.ds(column, LANES)], coef_v.at[t, span], sems.at[c, t]
+        )
+
+    places = [(k, h) for k in range(groups) for h in range(tiles)]
+    mask_copy = pltpu.make_async_copy(mask_ref.at[pl.ds(me * rows, rows)], live, mask_sem)
+    mask_copy.start()
+    for c in range(CHUNKS):
+        for k, h in places:
+            copy(c, k, h).start()
+    lane_row = lax.broadcasted_iota(jnp.int32, (SUBLANES, LANES), 0)
+
+    def note(i, n):
+        marks = [live[i * SUBLANES + j] for j in range(SUBLANES)]
+        for j in range(SUBLANES):
+            order[n] = i * SUBLANES + j
+            n = n + marks[j]
+        return n
+
+    def gather(i, carry):
+        first = pl.multiple_of(i * SUBLANES, SUBLANES)
+        picks = [order[first + j] for j in range(SUBLANES)]
+        total = jnp.zeros((SUBLANES, LANES), jnp.float32)
+        for k, h in places:
+            t = k * tiles + h
+            tile = coef_v[t, pl.ds(picks[0], SUBLANES, stride=0), :]
+            for j in range(1, SUBLANES):
+                line = coef_v[t, pl.ds(picks[j], SUBLANES, stride=0), :]
+                tile = jnp.where(lane_row == j, line, tile)
+            outs[k][pl.ds(first, SUBLANES), h * LANES : (h + 1) * LANES] = tile
+            total = total + tile * tile
+        squares[pl.ds(first, SUBLANES), :] = total
+        return carry
+
+    mask_copy.wait()
+    found = jnp.int32(0)
+    ends = []
+    for c in range(CHUNKS):
+        found = lax.fori_loop(
+            c * chunk // SUBLANES, (c + 1) * chunk // SUBLANES, note, found, unroll=2
+        )
+        ends.append(found // SUBLANES)
+    done = jnp.int32(0)
+    for c in range(CHUNKS):
+        for k, h in places:
+            copy(c, k, h).wait()
+        lax.fori_loop(done, ends[c], gather, 0)
+        done = ends[c]
+    part_ref[...] = lax.dot_general(
+        jnp.ones((SUBLANES, LANES), jnp.float32), squares[...],
+        (((1,), (1,)), ((), ())),
+        precision=lax.Precision.HIGHEST, preferred_element_type=jnp.float32,
+    )
+
+
+def pick(mask, coef, groups, rows, slice_width):
+    block = pltpu.VMEM((ACT_DEV, slice_width), jnp.float32)
+    tiles = groups * slice_width // LANES
+    return pl.pallas_call(
+        functools.partial(pick_kernel, groups, rows, slice_width),
+        out_shape=[block] * groups + [pltpu.VMEM((SUBLANES, ACT_DEV), jnp.float32)],
+        in_specs=[HBM, HBM],
+        out_specs=[VMEM] * (groups + 1),
+        scratch_shapes=[
+            pltpu.VMEM((tiles, rows, LANES), jnp.float32),
+            pltpu.VMEM((ACT_DEV, LANES), jnp.float32),
+            pltpu.SMEM((rows,), jnp.int32),
+            pltpu.SMEM((ACT_DEV + SUBLANES,), jnp.int32),
+            pltpu.SemaphoreType.DMA((CHUNKS, tiles)),
+            pltpu.SemaphoreType.DMA,
+        ],
+        name="pick",
+        compiler_params=PARAMS,
+    )(*[pltpu.with_memory_space_constraint(value, pltpu.HBM) for value in (mask, coef)])
+
+
+def spread_kernel(groups, rows, mask_ref, place_ref):
+    live = mask_ref[...]
+    before = lax.broadcasted_iota(jnp.int32, (rows, rows), 0) < lax.broadcasted_iota(
+        jnp.int32, (rows, rows), 1
+    )
+    rank = jnp.dot(
+        live.astype(jnp.float32).astype(jnp.bfloat16),
+        before.astype(jnp.float32).astype(jnp.bfloat16),
+        preferred_element_type=jnp.float32,
+    )
+    key = jnp.where(live > 0, rank, -1.0).T
+    packed = lax.broadcasted_iota(jnp.int32, (rows, ACT_DEV), 1).astype(jnp.float32)
+    for s in range(groups):
+        hit = key[:, s : s + 1] == packed
+        place_ref[s] = jnp.where(hit, 1.0, 0.0).astype(jnp.bfloat16)
+
+
+def spread(mask, groups, rows):
+    return pl.pallas_call(
+        functools.partial(spread_kernel, groups, rows),
+        out_shape=pltpu.VMEM((groups, rows, ACT_DEV), jnp.bfloat16),
+        in_specs=[VMEM],
+        out_specs=VMEM,
+        name="spread",
+        compiler_params=PARAMS,
+    )(mask.reshape(groups, rows))
+
+
+def inverse_norms(totals):
+    total = totals[0][...]
+    for other in totals[1:]:
+        total = total + other[...]
+    return (1.0 / jnp.sqrt(total / NV + EPS)).T
+
+
+def put(k, scale, got_ref, place_ref, assign_ref, flat_ref, wide):
+    rows = wide.shape[0]
+    slots = rows // K
+    source = jnp.bitwise_xor(lax.axis_index("scen"), k)
+    value = got_ref[...] * scale
+    squares = jnp.sum((value * value).reshape(ACT_DEV // SUBLANES, SUBLANES, -1), axis=0)
+    high = value.astype(jnp.bfloat16)
+    low = (value - high.astype(jnp.float32)).astype(jnp.bfloat16)
+    place = place_ref[source]
+    wide[...] = jnp.dot(place, high, preferred_element_type=jnp.float32) + jnp.dot(
+        place, low, preferred_element_type=jnp.float32
+    )
+    for i in range(slots):
+        at = pl.multiple_of(assign_ref[source * slots + i] * K, K)
+        flat_ref[pl.ds(at, K), :] = wide[i * K : (i + 1) * K, :]
+    return squares
+
+
+def early_kernel(lines, assign_ref, place_ref, *refs):
+    n = len(lines)
+    totals, got = refs[:4], refs[4 : 4 + n]
+    flat_ref, squares_ref, wide = refs[4 + n :]
+    scale = inverse_norms(totals)
+    squares = None
+    for (k, line), got_ref in zip(lines, got):
+        one = put(k, scale[:, line : line + 1], got_ref, place_ref, assign_ref, flat_ref, wide)
+        squares = one if squares is None else squares + one
+    squares_ref[...] = squares
+
+
+def late_kernel(lines, active_total, assign_ref, place_ref, *refs):
+    n = len(lines)
+    totals, got = refs[:4], refs[4 : 4 + n]
+    flat_ref, squares_ref, out_ref, wide, out_v, sems = refs[4 + n :]
+    scale = inverse_norms(totals)
+    squares = squares_ref[...]
+    for (k, line), got_ref in zip(lines, got):
+        squares = squares + put(
+            k, scale[:, line : line + 1], got_ref, place_ref, assign_ref, flat_ref, wide
+        )
+    column = jnp.sum(squares, axis=0, keepdims=True)
+    inverse = 1.0 / jnp.sqrt(column / active_total + EPS)
+    cuts = flat_ref.shape[0]
+    step = 4 * LANES
+    copies = []
+    for c in range(cuts // step):
+        span = pl.ds(c * step, step)
+        out_v[:, span] = (flat_ref[span, :] * inverse).T
+        copies.append(pltpu.make_async_copy(out_v.at[:, span], out_ref.at[0, :, span], sems.at[c]))
+        copies[-1].start()
+    for one in copies:
+        one.wait()
+
+
+def on_chip(value):
+    return pltpu.with_memory_space_constraint(value, pltpu.VMEM)
+
+
+def finish(received, lines_of, last, totals, place, assign, groups, rows, slice_width):
+    received = {k: on_chip(v) for k, v in received.items()}
+    totals = [on_chip(v) for v in totals]
+    cuts = groups * rows
+    flat = pltpu.VMEM((cuts, slice_width), jnp.float32)
+    squares = pltpu.VMEM((SUBLANES, slice_width), jnp.float32)
+    wide = pltpu.VMEM((rows, slice_width), jnp.float32)
+    early = [k for k in range(groups) if k not in last]
+    flat, squares = pl.pallas_call(
+        functools.partial(early_kernel, [(k, lines_of[k]) for k in early]),
+        out_shape=[flat, squares],
+        in_specs=[SMEM] + [VMEM] * (1 + len(totals) + len(early)),
+        out_specs=[VMEM, VMEM],
+        scratch_shapes=[wide],
+        name="early",
+        compiler_params=PARAMS,
+    )(assign, place, *totals, *[received[k] for k in early])
+    return pl.pallas_call(
+        functools.partial(late_kernel, [(k, lines_of[k]) for k in last], ACT_DEV * groups),
+        out_shape=jax.ShapeDtypeStruct((1, slice_width, cuts), jnp.float32),
+        in_specs=[SMEM] + [VMEM] * (3 + len(totals) + len(last)),
+        out_specs=HBM,
+        scratch_shapes=[
+            wide,
+            pltpu.VMEM((slice_width, cuts), jnp.float32),
+            pltpu.SemaphoreType.DMA((cuts // (4 * LANES),)),
+        ],
+        name="late",
+        compiler_params=PARAMS,
+    )(assign, place, *totals, *[received[k] for k in last], flat, squares)
+
+
+def send_order(groups):
+    return [k for k in range(2, groups, 2)] + [k for k in range(1, groups, 2)][::-1]
+
+
+def exchange(coef, mask, assign):
+    rows, width = coef.shape
+    groups = lax.axis_size("scen")
+    columns = lax.axis_size("col")
+    slice_width = width // groups
+
+    def swap(value, k):
+        return lax.ppermute(value, "scen", [(i, i ^ k) for i in range(groups)])
+
+    *blocks, part = pick(mask, coef, groups, rows, slice_width)
+    received = {0: blocks[0]}
+    sends = send_order(groups)
+    for k in sends[:2]:
+        received[k] = swap(blocks[k], k)
+    evens = [k for k in range(0, groups, 2)]
+    parts = [part[:1]] + [swap(part, k)[:1] for k in evens[1:]]
+    for k in sends[2:]:
+        received[k] = swap(blocks[k], k)
+    half = jnp.concatenate(parts, axis=0)
+    other = swap(half, 1)
+    lines = jnp.concatenate([half, other], axis=0)
+    lines_of = {k: n for n, k in enumerate(evens + [k ^ 1 for k in evens])}
+    totals = [lines] + [
+        lax.ppermute(lines, "col", [(i, (i + z) % columns) for i in range(columns)])
+        for z in range(1, columns)
+    ]
+    place = spread(mask, groups, rows)
+    return finish(received, lines_of, [sends[-2]], totals, place, assign, groups, rows, slice_width)
+
+
+def fallback(coef, mask, assign):
     rows, width = coef.shape
     groups = lax.axis_size("scen")
     slice_width = width // groups
@@ -54,6 +311,12 @@
 def solution(mesh):
     in_specs = (P("scen", "col"), P(), P())
     out_specs = P("col", "scen", None)
-    return jax.shard_map(
-        on_device, mesh=mesh, in_specs=in_specs, out_specs=out_specs, check_vma=False
-    )
+    groups, columns = mesh.shape["scen"], mesh.shape["col"]
+    paired = groups >= 4 and groups & (groups - 1) == 0
+    fits = NV % (groups * columns * LANES) == 0
+    shard = functools.partial(
+        jax.shard_map, mesh=mesh, in_specs=in_specs, out_specs=out_specs, check_vma=False
+    )
+    if not (paired and fits):
+        return shard(fallback)
+    return shard(exchange)

time: 96.1 us -> 52.5 us (0.55)
  local copies, waits for them, and re-layouts: 22.3 us -> 0.04 us
  other arithmetic: 18 us -> 0.01 us
  blocking collectives: 13.5 us -> 0 us
  between operations: 13.5 us -> 0.08 us
  starting transfers between devices: 3.72 us -> 16.1 us
  Pallas kernels: 0 us -> 11.8 us
  matrix products: 4.46 us -> 0 us
  waiting for transfers between devices: 20 us -> 23.7 us
    ppermute x0 -> x14, waiting for transfers between devices: none -> 23.7 us  [the longest x11 19.9 us: swap(): return lax.ppermute(value, 'scen', [(i, i ^ k) for i in range(groups)])]
    all_to_all x1 -> x0, waiting for transfers between devices: 20 us -> none  [on_device(): lax.all_to_all(picked, 'scen', split_axis=0, concat_axis=2, tiled=True)]
    ppermute x0 -> x14, starting transfers between devices: none -> 16.1 us  [the longest x11 11.4 us: swap(): return lax.ppermute(value, 'scen', [(i, i ^ k) for i in range(groups)])]
    psum x1 -> x0, blocking collectives: 13.5 us -> none  [on_device(): total = lax.psum(partial_value, 'col')]
    pallas_call x0 -> x4, Pallas kernels: none -> 11.8 us  [the longest x1 5.12 us: pick(): pl.pallas_call(functools.partial(pick_kernel, groups, rows, slice_width),...]
    gather x2 -> x0, local copies, waits for them, and re-layouts: 8.02 us -> none  [the longest x1 5.08 us: on_device(): return jnp.take(slotted, inverse, axis=2).reshape(1, slice_width, cut_total)]
    select_n x2 -> x0, local copies, waits for them, and re-layouts: 7.55 us -> none  [the longest x1 5.59 us: on_device(): return jnp.take(slotted, inverse, axis=2).reshape(1, slice_width, cut_total)]
    sort x2 -> x0, other arithmetic: 7.52 us -> none  [the longest x1 3.77 us: on_device(): kept_rows = jnp.argsort(1 - own_mask, stable=True)[:ACT_DEV]]
  transfers between devices with their start and end apart: 1 -> 14, of which waited for: 1 -> 7; matrix products, arithmetic and copies ran while one was open for 6% -> 0% of each run, Pallas kernels for 0% -> 6%
where the time goes in v1:
time: 52.5 us; the launch traced here: 51.7 us
  waiting for transfers between devices  23.7 us (45%)
  starting transfers between devices  16.1 us (31%)
  Pallas kernels  11.8 us (22%)
    ppermute x11, waiting for transfers between devices, swap(): return lax.ppermute(value, 'scen', [(i, i ^ k) for i in range(groups)])  19.9 us
    ppermute x11, starting transfers between devices, swap(): return lax.ppermute(value, 'scen', [(i, i ^ k) for i in range(groups)])  11.4 us
    pallas_call x1, Pallas kernels, pick(): pl.pallas_call(functools.partial(pick_kernel, groups, rows, slice_width),...  5.12 us
    ppermute x3, starting transfers between devices, exchange(): lax.ppermute(lines, 'col', [(i, (i + z) % columns) for i in range(columns)])  4.66 us
    ppermute x3, waiting for transfers between devices, exchange(): lax.ppermute(lines, 'col', [(i, (i + z) % columns) for i in range(columns)])  3.81 us
    pallas_call x1, Pallas kernels, finish(): pl.pallas_call(functools.partial(late_kernel, [(k, lines_of[k]) for k in...  3.4 us
    pallas_call x1, Pallas kernels, finish(): pl.pallas_call(functools.partial(early_kernel, [(k, lines_of[k]) for k in...  2.3 us
  transfers between devices with their start and end apart: 14, of which 7 were waited for; matrix products, arithmetic and copies ran while one was open for 0% of the time, Pallas kernels for 6%

profile of v1, /device:TPU:0, one launch (start us, length us, event | category | flops | bytes accessed | tf_op | source)
XLA Modules:
  0.0 51.7 jit_solution(7294389301794460144)
XLA Ops:
  0.0 0.0 copy-start.1
  0.0 0.0 copy-start
  0.0 5.1 %pick.1 = (f32[256,256]{1,0:T(8,128)S(1)}, f32[256,256]{1,0:T(8,128)S(1)}, f32[256,256]{1,0:T(8,128)S(1)}, f32[256,256]{1,0:T(8,128)S(1)}, f32[256,256]{1,0:T(8,...) custom-call(s32[4096]{0:T(1024)} %mask_ref.1, ...), custom_call_target="tpu_custom_call" | custom-call | tf_op jit(solution)/shard_map/pick/pallas_call | solution.py:94
  5.1 0.6 %collective-permute-start.8 = (f32[256,256]{1,0:T(8,128)S(1)}, f32[256,256]{1,0:T(8,128)S(1)}, u32[]{:S(2)}, u32[]{:S(2)}) collective-permute-start(f32[256,256]{1,0:T(8,128)S(1)} %get-tuple-element.19), channel_id=1, source_target_pairs={{0,4},{4,0},{8,12},{12,8},{16,20},{20,16},{24,28},{28,24},{1,5},{5... | collective-permute-start | bytes 786440 | tf_op jit(solution)/shard_map/ppermute | solution.py:248
  5.7 2.6 %collective-permute-start.9 = (f32[256,256]{1,0:T(8,128)S(1)}, f32[256,256]{1,0:T(8,128)S(1)}, u32[]{:S(2)}, u32[]{:S(2)}) collective-permute-start(f32[256,256]{1,0:T(8,128)S(1)} %get-tuple-element.20), channel_id=1, source_target_pairs={{0,8},{4,12},{8,0},{12,4},{16,24},{20,28},{24,16},{28,20},{1,9},{5... | collective-permute-start | bytes 786440 | tf_op jit(solution)/shard_map/ppermute | solution.py:248
  8.3 1.5 %collective-permute-start.2 = (f32[8,256]{1,0:T(8,128)S(1)}, f32[8,256]{1,0:T(8,128)S(1)}, u32[]{:S(2)}, u32[]{:S(2)}) collective-permute-start(f32[8,256]{1,0:T(8,128)S(1)} %get-tuple-element.16), channel_id=1, source_target_pairs={{0,24},{4,28},{8,16},{12,20},{16,8},{20,12},{24,0},{28,4},{1,25},{... | collective-permute-start | bytes 24584 | tf_op jit(solution)/shard_map/ppermute | solution.py:248
  9.7 0.0 collective-permute-start.1
  9.8 1.9 %collective-permute-start = (f32[8,256]{1,0:T(8,128)S(1)}, f32[8,256]{1,0:T(8,128)S(1)}, u32[]{:S(2)}, u32[]{:S(2)}) collective-permute-start(f32[8,256]{1,0:T(8,128)S(1)} %get-tuple-element.16), channel_id=1, source_target_pairs={{0,8},{4,12},{8,0},{12,4},{16,24},{20,28},{24,16},{28,20},{1,9},{5... | collective-permute-start | bytes 24584 | tf_op jit(solution)/shard_map/ppermute | solution.py:248
  11.7 4.9 %collective-permute-done.2 = f32[8,256]{1,0:T(8,128)S(1)} collective-permute-done((f32[8,256]{1,0:T(8,128)S(1)}, f32[8,256]{1,0:T(8,128)S(1)}, u32[]{:S(2)}, u32[]{:S(2)}) %collective-permute-start.2) | collective-permute-done | bytes 8224 | tf_op jit(solution)/shard_map/ppermute | solution.py:248
  16.6 0.0 collective-permute-done.1
  16.6 0.0 collective-permute-done
  16.7 0.1 collective-permute-start.3
  16.8 1.2 %collective-permute-done.3 = f32[4,256]{1,0:T(4,128)S(1)} collective-permute-done((f32[4,256]{1,0:T(4,128)S(1)}, f32[4,256]{1,0:T(4,128)S(1)}, u32[]{:S(2)}, u32[]{:S(2)}) %collective-permute-start.3) | collective-permute-done | bytes 4128 | tf_op jit(solution)/shard_map/ppermute | solution.py:248
  17.9 3.7 %collective-permute-start.6 = (f32[8,256]{1,0:T(8,128)S(1)}, f32[8,256]{1,0:T(8,128)S(1)}, u32[]{:S(2)}, u32[]{:S(2)}) collective-permute-start(f32[8,256]{1,0:T(8,128)S(1)} %concatenate.8.refs_0_), channel_id=1, source_target_pairs={{0,3},{1,0},{2,1},{3,2},{4,7},{5,4},{6,5},{7,6},{8,11},{9,8},{10,9... | collective-permute-start | bytes 24584 | tf_op jit(solution)/shard_map/ppermute | solution.py:264
  21.6 0.0 collective-permute-start.5
  21.6 1.0 %collective-permute-start.4 = (f32[8,256]{1,0:T(8,128)S(1)}, f32[8,256]{1,0:T(8,128)S(1)}, u32[]{:S(2)}, u32[]{:S(2)}) collective-permute-start(f32[8,256]{1,0:T(8,128)S(1)} %concatenate.8.refs_0_), channel_id=1, source_target_pairs={{0,1},{1,2},{2,3},{3,0},{4,5},{5,6},{6,7},{7,4},{8,9},{9,10},{10,1... | collective-permute-start | bytes 24584 | tf_op jit(solution)/shard_map/ppermute | solution.py:264
  22.6 0.4 collective-permute-done.6.refs_3_
  22.9 0.6 %collective-permute-start.10 = (f32[256,256]{1,0:T(8,128)S(1)}, f32[256,256]{1,0:T(8,128)S(1)}, u32[]{:S(2)}, u32[]{:S(2)}) collective-permute-start(f32[256,256]{1,0:T(8,128)S(1)} %get-tuple-element.21), channel_id=1, source_target_pairs={{0,16},{4,20},{8,24},{12,28},{16,0},{20,4},{24,8},{28,12},{1,17},{... | collective-permute-start | bytes 786440 | tf_op jit(solution)/shard_map/ppermute | solution.py:248
  23.6 2.6 %collective-permute-done.5.refs_2_ = f32[8,256]{1,0:T(8,128)S(1)} collective-permute-done((f32[8,256]{1,0:T(8,128)S(1)}, f32[8,256]{1,0:T(8,128)S(1)}, u32[]{:S(2)}, u32[]{:S(2)}) %collective-permute-start.5) | collective-permute-done | bytes 8224 | tf_op jit(solution)/shard_map/ppermute | solution.py:264
  26.1 0.0 collective-permute-start.11
  26.1 0.9 %collective-permute-done.4.refs_1_ = f32[8,256]{1,0:T(8,128)S(1)} collective-permute-done((f32[8,256]{1,0:T(8,128)S(1)}, f32[8,256]{1,0:T(8,128)S(1)}, u32[]{:S(2)}, u32[]{:S(2)}) %collective-permute-start.4) | collective-permute-done | bytes 8224 | tf_op jit(solution)/shard_map/ppermute | solution.py:264
  27.0 1.6 %collective-permute-start.12 = (f32[256,256]{1,0:T(8,128)S(1)}, f32[256,256]{1,0:T(8,128)S(1)}, u32[]{:S(2)}, u32[]{:S(2)}) collective-permute-start(f32[256,256]{1,0:T(8,128)S(1)} %get-tuple-element.23), channel_id=1, source_target_pairs={{0,24},{4,28},{8,16},{12,20},{16,8},{20,12},{24,0},{28,4},{1,25},{... | collective-permute-start | bytes 786440 | tf_op jit(solution)/shard_map/ppermute | solution.py:248
  28.6 0.0 collective-permute-done.8.refs_5_
  28.6 0.5 %collective-permute-start.13 = (f32[256,256]{1,0:T(8,128)S(1)}, f32[256,256]{1,0:T(8,128)S(1)}, u32[]{:S(2)}, u32[]{:S(2)}) collective-permute-start(f32[256,256]{1,0:T(8,128)S(1)} %get-tuple-element.24), channel_id=1, source_target_pairs={{0,28},{4,24},{8,20},{12,16},{16,12},{20,8},{24,4},{28,0},{1,29},{... | collective-permute-start | bytes 786440 | tf_op jit(solution)/shard_map/ppermute | solution.py:248
  29.1 0.0 collective-permute-done.9.refs_6_
  29.1 2.0 %collective-permute-start.7 = (f32[256,256]{1,0:T(8,128)S(1)}, f32[256,256]{1,0:T(8,128)S(1)}, u32[]{:S(2)}, u32[]{:S(2)}) collective-permute-start(f32[256,256]{1,0:T(8,128)S(1)} %get-tuple-element.17), channel_id=1, source_target_pairs={{0,12},{4,8},{8,4},{12,0},{16,28},{20,24},{24,20},{28,16},{1,13},{... | collective-permute-start | bytes 786440 | tf_op jit(solution)/shard_map/ppermute | solution.py:248
  31.2 0.0 copy-done.1
  31.2 1.0 %spread.1.place_ref = bf16[8,512,256]{2,1,0:T(8,128)(2,1)S(1)} custom-call(s32[8,512]{1,0:T(8,128)S(1)} %reshape.3.mask_ref), custom_call_target="tpu_custom_call" | custom-call | tf_op jit(solution)/shard_map/spread/pallas_call | solution.py:130
  32.2 10.9 %collective-permute-done.10.refs_7_ = f32[256,256]{1,0:T(8,128)S(1)} collective-permute-done((f32[256,256]{1,0:T(8,128)S(1)}, f32[256,256]{1,0:T(8,128)S(1)}, u32[]{:S(2)}, u32[]{:S(2)}) %collective-permute-start.10) | collective-permute-done | bytes 262176 | tf_op jit(solution)/shard_map/ppermute | solution.py:248
  43.1 2.9 %collective-permute-done.11.refs_8_ = f32[256,256]{1,0:T(8,128)S(1)} collective-permute-done((f32[256,256]{1,0:T(8,128)S(1)}, f32[256,256]{1,0:T(8,128)S(1)}, u32[]{:S(2)}, u32[]{:S(2)}) %collective-permute-start.11) | collective-permute-done | bytes 262176 | tf_op jit(solution)/shard_map/ppermute | solution.py:248
  46.0 0.0 collective-permute-done.12.refs_9_
  46.0 0.0 collective-permute-done.13.refs_10_
  46.0 0.0 copy-done
  46.0 2.3 %early.1 = (f32[4096,256]{1,0:T(8,128)S(1)}, f32[8,256]{1,0:T(8,128)S(1)}) custom-call(s32[512]{0:T(512)S(1)} %copy-done, bf16[8,512,256]{2,1,0:T(8,128)(2,1)S(1)} %spread.1.place_ref, f32[8,256]{1,0:T(8,128)S(1)} %concatenate.8.refs_0_, f32[8,256]{1,0:T(8,128)S(1)} %collective-permute-done.4.refs_1_, f32[8,256]{1,0:T(8,128)S(1)} %collective-permute-done.5.refs_2_, ...), custom_call_target="tpu_custom_call" | custom-call | tf_op jit(solution)/shard_map/early/pallas_call | solution.py:213
  48.3 0.0 collective-permute-done.7.refs_4_
  48.3 3.4 %late.1 = f32[1,256,4096]{2,1,0:T(8,128)} custom-call(s32[512]{0:T(512)S(1)} %copy-done, bf16[8,512,256]{2,1,0:T(8,128)(2,1)S(1)} %spread.1.place_ref, f32[8,256]{1,0:T(8,128)S(1)} %concatenate.8.refs_0_, f32[8,256]{1,0:T(8,128)S(1)} %collective-permute-done.4.refs_1_, f32[8,256]{1,0:T(8,128)S(1)} %collective-permute-done.5.refs_2_, ...), custom_call_target="tpu_custom_call" | custom-call | tf_op jit(solution)/shard_map/late/pallas_call | solution.py:222
  (7 shorter events, 0.0 us)
Async XLA Ops:
  0.0 31.2 %copy-start.1 = (s32[4096]{0:T(1024)S(1)}, s32[4096]{0:T(1024)}, u32[]{:S(2)}) copy-start(s32[4096]{0:T(1024)} %mask_ref.1) | copy-start | bytes 49156
  0.0 46.0 %copy-start = (s32[512]{0:T(512)S(1)}, s32[512]{0:T(512)}, u32[]{:S(2)}) copy-start(s32[512]{0:T(512)} %assign_ref.3) | copy-start | bytes 6148
  5.1 23.5 %collective-permute-start.8 = (f32[256,256]{1,0:T(8,128)S(1)}, f32[256,256]{1,0:T(8,128)S(1)}, u32[]{:S(2)}, u32[]{:S(2)}) collective-permute-start(f32[256,256]{1,0:T(8,128)S(1)} %get-tuple-element.19), channel_id=1, source_target_pairs={{0,4},{4,0},{8,12},{12,8},{16,20},{20,16},{24,28},{28,24},{1,5},{5... | collective-permute-start | bytes 786440 | tf_op jit(solution)/shard_map/ppermute | solution.py:248
  5.7 23.4 %collective-permute-start.9 = (f32[256,256]{1,0:T(8,128)S(1)}, f32[256,256]{1,0:T(8,128)S(1)}, u32[]{:S(2)}, u32[]{:S(2)}) collective-permute-start(f32[256,256]{1,0:T(8,128)S(1)} %get-tuple-element.20), channel_id=1, source_target_pairs={{0,8},{4,12},{8,0},{12,4},{16,24},{20,28},{24,16},{28,20},{1,9},{5... | collective-permute-start | bytes 786440 | tf_op jit(solution)/shard_map/ppermute | solution.py:248
  8.3 8.4 %collective-permute-start.2 = (f32[8,256]{1,0:T(8,128)S(1)}, f32[8,256]{1,0:T(8,128)S(1)}, u32[]{:S(2)}, u32[]{:S(2)}) collective-permute-start(f32[8,256]{1,0:T(8,128)S(1)} %get-tuple-element.16), channel_id=1, source_target_pairs={{0,24},{4,28},{8,16},{12,20},{16,8},{20,12},{24,0},{28,4},{1,25},{... | collective-permute-start | bytes 24584 | tf_op jit(solution)/shard_map/ppermute | solution.py:248
  9.7 6.9 %collective-permute-start.1 = (f32[8,256]{1,0:T(8,128)S(1)}, f32[8,256]{1,0:T(8,128)S(1)}, u32[]{:S(2)}, u32[]{:S(2)}) collective-permute-start(f32[8,256]{1,0:T(8,128)S(1)} %get-tuple-element.16), channel_id=1, source_target_pairs={{0,16},{4,20},{8,24},{12,28},{16,0},{20,4},{24,8},{28,12},{1,17},{... | collective-permute-start | bytes 24584 | tf_op jit(solution)/shard_map/ppermute | solution.py:248
  9.8 6.8 %collective-permute-start = (f32[8,256]{1,0:T(8,128)S(1)}, f32[8,256]{1,0:T(8,128)S(1)}, u32[]{:S(2)}, u32[]{:S(2)}) collective-permute-start(f32[8,256]{1,0:T(8,128)S(1)} %get-tuple-element.16), channel_id=1, source_target_pairs={{0,8},{4,12},{8,0},{12,4},{16,24},{20,28},{24,16},{28,20},{1,9},{5... | collective-permute-start | bytes 24584 | tf_op jit(solution)/shard_map/ppermute | solution.py:248
  16.7 1.2 %collective-permute-start.3 = (f32[4,256]{1,0:T(4,128)S(1)}, f32[4,256]{1,0:T(4,128)S(1)}, u32[]{:S(2)}, u32[]{:S(2)}) collective-permute-start(f32[4,256]{1,0:T(4,128)S(1)} %pad_maximum_fusion), channel_id=1, source_target_pairs={{0,4},{4,0},{8,12},{12,8},{16,20},{20,16},{24,28},{28,24},{1,5},{5... | collective-permute-start | bytes 12296 | tf_op jit(solution)/shard_map/ppermute | solution.py:248
  17.9 5.0 %collective-permute-start.6 = (f32[8,256]{1,0:T(8,128)S(1)}, f32[8,256]{1,0:T(8,128)S(1)}, u32[]{:S(2)}, u32[]{:S(2)}) collective-permute-start(f32[8,256]{1,0:T(8,128)S(1)} %concatenate.8.refs_0_), channel_id=1, source_target_pairs={{0,3},{1,0},{2,1},{3,2},{4,7},{5,4},{6,5},{7,6},{8,11},{9,8},{10,9... | collective-permute-start | bytes 24584 | tf_op jit(solution)/shard_map/ppermute | solution.py:264
  21.6 4.5 %collective-permute-start.5 = (f32[8,256]{1,0:T(8,128)S(1)}, f32[8,256]{1,0:T(8,128)S(1)}, u32[]{:S(2)}, u32[]{:S(2)}) collective-permute-start(f32[8,256]{1,0:T(8,128)S(1)} %concatenate.8.refs_0_), channel_id=1, source_target_pairs={{0,2},{1,3},{2,0},{3,1},{4,6},{5,7},{6,4},{7,5},{8,10},{9,11},{10,... | collective-permute-start | bytes 24584 | tf_op jit(solution)/shard_map/ppermute | solution.py:264
  21.6 5.4 %collective-permute-start.4 = (f32[8,256]{1,0:T(8,128)S(1)}, f32[8,256]{1,0:T(8,128)S(1)}, u32[]{:S(2)}, u32[]{:S(2)}) collective-permute-start(f32[8,256]{1,0:T(8,128)S(1)} %concatenate.8.refs_0_), channel_id=1, source_target_pairs={{0,1},{1,2},{2,3},{3,0},{4,5},{5,6},{6,7},{7,4},{8,9},{9,10},{10,1... | collective-permute-start | bytes 24584 | tf_op jit(solution)/shard_map/ppermute | solution.py:264
  22.9 20.1 %collective-permute-start.10 = (f32[256,256]{1,0:T(8,128)S(1)}, f32[256,256]{1,0:T(8,128)S(1)}, u32[]{:S(2)}, u32[]{:S(2)}) collective-permute-start(f32[256,256]{1,0:T(8,128)S(1)} %get-tuple-element.21), channel_id=1, source_target_pairs={{0,16},{4,20},{8,24},{12,28},{16,0},{20,4},{24,8},{28,12},{1,17},{... | collective-permute-start | bytes 786440 | tf_op jit(solution)/shard_map/ppermute | solution.py:248
  26.1 19.8 %collective-permute-start.11 = (f32[256,256]{1,0:T(8,128)S(1)}, f32[256,256]{1,0:T(8,128)S(1)}, u32[]{:S(2)}, u32[]{:S(2)}) collective-permute-start(f32[256,256]{1,0:T(8,128)S(1)} %get-tuple-element.22), channel_id=1, source_target_pairs={{0,20},{4,16},{8,28},{12,24},{16,4},{20,0},{24,12},{28,8},{1,21},{... | collective-permute-start | bytes 786440 | tf_op jit(solution)/shard_map/ppermute | solution.py:248
  27.0 18.9 %collective-permute-start.12 = (f32[256,256]{1,0:T(8,128)S(1)}, f32[256,256]{1,0:T(8,128)S(1)}, u32[]{:S(2)}, u32[]{:S(2)}) collective-permute-start(f32[256,256]{1,0:T(8,128)S(1)} %get-tuple-element.23), channel_id=1, source_target_pairs={{0,24},{4,28},{8,16},{12,20},{16,8},{20,12},{24,0},{28,4},{1,25},{... | collective-permute-start | bytes 786440 | tf_op jit(solution)/shard_map/ppermute | solution.py:248
  28.6 17.4 %collective-permute-start.13 = (f32[256,256]{1,0:T(8,128)S(1)}, f32[256,256]{1,0:T(8,128)S(1)}, u32[]{:S(2)}, u32[]{:S(2)}) collective-permute-start(f32[256,256]{1,0:T(8,128)S(1)} %get-tuple-element.24), channel_id=1, source_target_pairs={{0,28},{4,24},{8,20},{12,16},{16,12},{20,8},{24,4},{28,0},{1,29},{... | collective-permute-start | bytes 786440 | tf_op jit(solution)/shard_map/ppermute | solution.py:248
  29.1 19.2 %collective-permute-start.7 = (f32[256,256]{1,0:T(8,128)S(1)}, f32[256,256]{1,0:T(8,128)S(1)}, u32[]{:S(2)}, u32[]{:S(2)}) collective-permute-start(f32[256,256]{1,0:T(8,128)S(1)} %get-tuple-element.17), channel_id=1, source_target_pairs={{0,12},{4,8},{8,4},{12,0},{16,28},{20,24},{24,20},{28,16},{1,13},{... | collective-permute-start | bytes 786440 | tf_op jit(solution)/shard_map/ppermute | solution.py:248

commit v2 on v0

--- a/solution.py
+++ b/solution.py
@@ -1,6 +1,10 @@
+import functools
+
 import jax
 import jax.numpy as jnp
 from jax import lax
+from jax.experimental import pallas as pl
+from jax.experimental.pallas import tpu as pltpu
 from jax.sharding import PartitionSpec as P
 
 NV = 8192
@@ -9,9 +13,388 @@
 
 
 EPS = 1e-06
-
-
-def on_device(coef, mask, assign):
+LANES = 128
+SUBLANES = 8
+CHUNKS = 4
+VMEM = pl.BlockSpec(memory_space=pltpu.VMEM)
+HBM = pl.BlockSpec(memory_space=pltpu.HBM)
+SMEM = pl.BlockSpec(memory_space=pltpu.SMEM)
+PARAMS = pltpu.CompilerParams(vmem_limit_bytes=16 * 1024 * 1024)
+
+
+def on_chip(*values):
+    return [pltpu.with_memory_space_constraint(value, pltpu.VMEM) for value in values]
+
+
+def scalars(value):
+    return pltpu.with_memory_space_constraint(value, pltpu.SMEM)
+
+
+def in_hbm(*values):
+    return [pltpu.with_memory_space_constraint(value, pltpu.HBM) for value in values]
+
+
+def evens(groups):
+    return list(range(0, groups, 2))
+
+
+def odds(groups):
+    return list(range(1, groups, 2))
+
+
+def halved(groups):
+    return odds(groups)[1:-1]
+
+
+def pieces(groups, tiles):
+    whole = [(k, 0, tiles) for k in range(groups) if k not in halved(groups)]
+    first = [(k, 0, tiles // 2) for k in halved(groups)]
+    second = [(k, tiles // 2, tiles) for k in halved(groups)]
+    return whole + first + second
+
+
+def pack(first, picks, window, cells, total):
+    lane_row = lax.broadcasted_iota(jnp.int32, (SUBLANES, LANES), 0)
+    for t, out, lane in cells:
+        tile = window[t, pl.ds(picks[0], SUBLANES), :]
+        for j in range(1, SUBLANES):
+            tile = jnp.where(lane_row == j, window[t, pl.ds(picks[j], SUBLANES), :], tile)
+        out[pl.ds(first, SUBLANES), lane : lane + LANES] = tile
+        total = total + tile * tile
+    return total
+
+
+def cells_of(parts, outs, tiles):
+    return [
+        (k * tiles + h, out, (h - h0) * LANES)
+        for (k, h0, h1), out in zip(parts, outs)
+        for h in range(h0, h1)
+    ]
+
+
+def first_kernel(groups, rows, tiles, parts, mask_ref, coef_ref, *refs):
+    outs = refs[: len(parts)]
+    window, squares, order, live, sems, mask_sem = refs[len(parts) :]
+    me = lax.axis_index("scen")
+    chunk = rows // CHUNKS
+    places = [(k, h) for k in range(groups) for h in range(tiles)]
+    cells = cells_of(parts, outs, tiles)
+    places.sort(key=lambda place: place[0] not in [k for k, _, _ in parts])
+
+    def copy(c, k, h):
+        span = pl.ds(c * chunk, chunk)
+        column = pl.multiple_of((jnp.bitwise_xor(me, k) * tiles + h) * LANES, LANES)
+        t = k * tiles + h
+        return pltpu.make_async_copy(
+            coef_ref.at[span, pl.ds(column, LANES)], window.at[t, span], sems.at[c, t]
+        )
+
+    mask_copy = pltpu.make_async_copy(mask_ref.at[pl.ds(me * rows, rows)], live, mask_sem)
+    mask_copy.start()
+    for k, h in places:
+        for c in range(CHUNKS):
+            copy(c, k, h).start()
+
+    def note(i, n):
+        marks = [live[i * SUBLANES + j] for j in range(SUBLANES)]
+        for j in range(SUBLANES):
+            order[n] = i * SUBLANES + j
+            n = n + marks[j]
+        return n
+
+    def gather(i, carry):
+        first = pl.multiple_of(i * SUBLANES, SUBLANES)
+        picks = [order[first + j] - j for j in range(SUBLANES)]
+        total = jnp.zeros((SUBLANES, LANES), jnp.float32)
+        squares[pl.ds(first, SUBLANES), :] = pack(first, picks, window, cells, total)
+        return carry
+
+    mask_copy.wait()
+    lax.fori_loop(0, rows // SUBLANES, note, jnp.int32(0), unroll=4)
+    inside = [k for k, _, _ in parts]
+    for k, h in places:
+        for c in range(CHUNKS):
+            if k in inside:
+                copy(c, k, h).wait()
+    lax.fori_loop(0, ACT_DEV // SUBLANES, gather, 0, unroll=2)
+    for k, h in places:
+        for c in range(CHUNKS):
+            if k not in inside:
+                copy(c, k, h).wait()
+
+
+def second_kernel(tiles, parts, window, before, order, *refs):
+    outs = refs[: len(parts)]
+    part_ref, squares = refs[len(parts) :]
+    cells = cells_of(parts, outs, tiles)
+
+    def gather(i, carry):
+        first = pl.multiple_of(i * SUBLANES, SUBLANES)
+        picks = [order[first + j] - j for j in range(SUBLANES)]
+        total = before[pl.ds(first, SUBLANES), :]
+        squares[pl.ds(first, SUBLANES), :] = pack(first, picks, window, cells, total)
+        return carry
+
+    lax.fori_loop(0, ACT_DEV // SUBLANES, gather, 0)
+    part_ref[...] = lax.dot_general(
+        jnp.ones((SUBLANES, LANES), jnp.float32), squares[...],
+        (((1,), (1,)), ((), ())),
+        precision=lax.Precision.HIGHEST, preferred_element_type=jnp.float32,
+    )
+
+
+def pick(mask, coef, groups, rows, tiles):
+    parts = pieces(groups, tiles)
+    ahead = [part for part in parts if part[0] == evens(groups)[-1]]
+    behind = [part for part in parts if part not in ahead]
+
+    def blocks(some):
+        room = {1: SUBLANES}
+        return [
+            pltpu.VMEM((ACT_DEV + room.get(k, 0), (h1 - h0) * LANES), jnp.float32)
+            for k, h0, h1 in some
+        ]
+
+    squares = pltpu.VMEM((ACT_DEV, LANES), jnp.float32)
+    window = pltpu.VMEM((groups * tiles, rows + SUBLANES, LANES), jnp.float32)
+    *one, window, before, order = pl.pallas_call(
+        functools.partial(first_kernel, groups, rows, tiles, ahead),
+        out_shape=blocks(ahead) + [window, squares, pltpu.SMEM((rows,), jnp.int32)],
+        in_specs=[HBM, HBM],
+        out_specs=[VMEM] * (len(ahead) + 2) + [SMEM],
+        scratch_shapes=[
+            pltpu.SMEM((rows,), jnp.int32),
+            pltpu.SemaphoreType.DMA((CHUNKS, groups * tiles)),
+            pltpu.SemaphoreType.DMA,
+        ],
+        name="first",
+        compiler_params=PARAMS,
+    )(*in_hbm(mask, coef))
+    *two, part = pl.pallas_call(
+        functools.partial(second_kernel, tiles, behind),
+        out_shape=blocks(behind) + [pltpu.VMEM((SUBLANES, ACT_DEV), jnp.float32)],
+        in_specs=[VMEM, VMEM, SMEM],
+        out_specs=[VMEM] * (len(behind) + 1),
+        scratch_shapes=[squares],
+        name="second",
+        compiler_params=PARAMS,
+    )(*on_chip(window, before), scalars(order))
+    found = zip(ahead + behind, one + two)
+    return {(k, h0): block for (k, h0, _), block in found}, part
+
+
+def join_kernel(block_ref, *refs):
+    out_ref = refs[-1]
+    for n, ref in enumerate(refs[:-1]):
+        out_ref[ACT_DEV + n : ACT_DEV + n + 1, :] = ref[:1, :]
+
+
+def join(block, *values):
+    return pl.pallas_call(
+        join_kernel,
+        out_shape=pltpu.VMEM(block.shape, jnp.float32),
+        in_specs=[VMEM] * (1 + len(values)),
+        out_specs=VMEM,
+        input_output_aliases={0: 0},
+        name="join",
+        compiler_params=PARAMS,
+    )(*on_chip(block, *values))
+
+
+def stack_kernel(take, *refs):
+    for n, ref in enumerate(refs[:-1]):
+        refs[-1][n * take : (n + 1) * take, :] = ref[ACT_DEV : ACT_DEV + take, :]
+
+
+def stack(take, *values):
+    return pl.pallas_call(
+        functools.partial(stack_kernel, take),
+        out_shape=pltpu.VMEM((take * len(values), values[0].shape[1]), jnp.float32),
+        in_specs=[VMEM] * len(values),
+        out_specs=VMEM,
+        name="stack",
+        compiler_params=PARAMS,
+    )(*on_chip(*values))
+
+
+def spread_kernel(groups, rows, mask_ref, assign_ref, place_ref, slots_ref, sem):
+    copy = pltpu.make_async_copy(assign_ref, slots_ref, sem)
+    copy.start()
+    lines = [mask_ref[pl.ds(s * rows, rows)].reshape(1, rows) for s in range(groups)]
+    live = jnp.concatenate(lines, axis=0)
+    before = lax.broadcasted_iota(jnp.int32, (rows, rows), 0) < lax.broadcasted_iota(
+        jnp.int32, (rows, rows), 1
+    )
+    rank = jnp.dot(
+        live.astype(jnp.float32).astype(jnp.bfloat16),
+        before.astype(jnp.float32).astype(jnp.bfloat16),
+        preferred_element_type=jnp.float32,
+    )
+    key = jnp.where(live > 0, rank, -1.0).T
+    packed = lax.broadcasted_iota(jnp.int32, (rows, ACT_DEV), 1).astype(jnp.float32)
+    for s in range(groups):
+        hit = key[:, s : s + 1] == packed
+        place_ref[s] = jnp.where(hit, 1.0, 0.0).astype(jnp.bfloat16)
+    copy.wait()
+
+
+def spread(mask, assign, groups, rows):
+    place = pltpu.VMEM((groups, rows, ACT_DEV), jnp.bfloat16)
+    return pl.pallas_call(
+        functools.partial(spread_kernel, groups, rows),
+        out_shape=[place, pltpu.SMEM(assign.shape, jnp.int32)],
+        in_specs=[VMEM, HBM],
+        out_specs=[VMEM, SMEM],
+        scratch_shapes=[pltpu.SemaphoreType.DMA],
+        name="spread",
+        compiler_params=PARAMS,
+    )(*on_chip(mask), *in_hbm(assign))
+
+
+def inverse_norms(totals):
+    total = totals[0][...]
+    for other in totals[1:]:
+        total = total + other[...]
+    return (1.0 / jnp.sqrt(total / NV + EPS)).T
+
+
+def place_rows(k, scale, got_ref, place_ref, assign_ref, flats):
+    source = jnp.bitwise_xor(lax.axis_index("scen"), k)
+    value = got_ref[:ACT_DEV, :] * scale
+    high = value.astype(jnp.bfloat16)
+    low = (value - high.astype(jnp.float32)).astype(jnp.bfloat16)
+    place = place_ref[source]
+    wide = jnp.dot(place, high, preferred_element_type=jnp.float32) + jnp.dot(
+        place, low, preferred_element_type=jnp.float32
+    )
+    slots = wide.shape[0] // K
+    for i in range(slots):
+        at = pl.multiple_of(assign_ref[source * slots + i] * K, K)
+        lane = 0
+        for flat in flats:
+            width = flat.shape[1]
+            flat[pl.ds(at, K), :] = wide[i * K : (i + 1) * K, lane : lane + width]
+            lane += width
+    return jnp.sum((value * value).reshape(ACT_DEV // SUBLANES, SUBLANES, -1), axis=0)
+
+
+def early_kernel(lines, rest, assign_ref, place_ref, *refs):
+    n = len(lines)
+    totals, got = refs[:4], refs[4 : 4 + n]
+    outs = refs[4 + n :]
+    flats, (squares_a, squares_b), scales = outs[:2], outs[2:4], outs[4:]
+    scale = inverse_norms(totals)
+    for line, ref in zip(rest, scales):
+        ref[...] = jnp.broadcast_to(scale[:, line : line + 1], ref.shape)
+    squares = None
+    for (k, line), got_ref in zip(lines, got):
+        one = place_rows(k, scale[:, line : line + 1], got_ref, place_ref, assign_ref, flats)
+        squares = one if squares is None else squares + one
+    half = squares_a.shape[1]
+    squares_a[...] = squares[:, :half]
+    squares_b[...] = squares[:, half:]
+
+
+def late_kernel(last, active_total, steps, assign_ref, place_ref, *refs):
+    n = len(last)
+    scales, got, (flat, squares_ref) = refs[:n], refs[n : 2 * n], refs[2 * n : 2 * n + 2]
+    copies = []
+    cuts, width = flat.shape
+    if steps:
+        other_ref, out_ref, out_v, sems = refs[2 * n + 2 :]
+        target = out_ref.at[0, pl.ds(0, width)]
+        copies.append(pltpu.make_async_copy(other_ref, target, sems.at[steps]))
+
+        def begin(i, carry):
+            copies[0].start()
+            return carry
+
+        lax.fori_loop(0, jnp.minimum(lax.axis_index("scen") + 1, 1), begin, 0)
+    else:
+        (out_v,) = refs[2 * n + 2 :]
+    squares = squares_ref[...]
+    for k, scale, got_ref in zip(last, scales, got):
+        squares = squares + place_rows(k, scale[...], got_ref, place_ref, assign_ref, [flat])
+    column = jnp.sum(squares, axis=0, keepdims=True)
+    inverse = 1.0 / jnp.sqrt(column / active_total + EPS)
+    step = 4 * LANES
+    for c in range(cuts // step):
+        span = pl.ds(c * step, step)
+        out_v[:, span] = (flat[span, :] * inverse).T
+        if steps:
+            target = out_ref.at[0, pl.ds(width, width), span]
+            copies.append(pltpu.make_async_copy(out_v.at[:, span], target, sems.at[c]))
+            copies[-1].start()
+    for one in copies:
+        one.wait()
+
+
+def finish(received, lines_of, totals, place, assign, groups, rows, slice_width):
+    cuts = groups * rows
+    half = slice_width // 2
+    last = halved(groups)
+    early = [k for k in range(groups) if k not in last]
+    assign = scalars(assign)
+    (place,) = on_chip(place)
+    flat = pltpu.VMEM((cuts, half), jnp.float32)
+    squares = pltpu.VMEM((SUBLANES, half), jnp.float32)
+    scale = pltpu.VMEM((ACT_DEV, half), jnp.float32)
+    flat_a, flat_b, squares_a, squares_b, *scales = pl.pallas_call(
+        functools.partial(
+            early_kernel, [(k, lines_of[k]) for k in early], [lines_of[k] for k in last]
+        ),
+        out_shape=[flat, flat, squares, squares] + [scale] * len(last),
+        in_specs=[SMEM] + [VMEM] * (1 + len(totals) + len(early)),
+        out_specs=[VMEM] * (4 + len(last)),
+        name="early",
+        compiler_params=PARAMS,
+    )(assign, place, *on_chip(*totals, *[received[k, 0] for k in early]))
+
+    def late(n, flat, squares, *other):
+        got = [received[k, n * half // LANES] for k in last]
+        values = on_chip(*scales, *got, flat, squares, *other)
+        steps = cuts // (4 * LANES) if n else 0
+        turned = pltpu.VMEM((half, cuts), jnp.float32)
+        whole = jax.ShapeDtypeStruct((1, slice_width, cuts), jnp.float32)
+        return pl.pallas_call(
+            functools.partial(late_kernel, last, ACT_DEV * groups, steps),
+            out_shape=whole if n else turned,
+            in_specs=[SMEM] + [VMEM] * (1 + len(values)),
+            out_specs=HBM if n else VMEM,
+            scratch_shapes=[turned, pltpu.SemaphoreType.DMA((steps + 1,))] if n else [],
+            compiler_params=PARAMS,
+        )(assign, place, *values)
+
+    return late(1, flat_b, squares_b, late(0, flat_a, squares_a))
+
+
+def exchange(coef, mask, assign):
+    rows, width = coef.shape
+    groups = lax.axis_size("scen")
+    columns = lax.axis_size("col")
+    slice_width = width // groups
+    tiles = slice_width // LANES
+
+    def swap(value, k):
+        return lax.ppermute(value, "scen", [(i, i ^ k) for i in range(groups)])
+
+    blocks, part = pick(mask, coef, groups, rows, tiles)
+    near = evens(groups)
+    parts = [part] + [swap(part, k) for k in near[1:]]
+    blocks[1, 0] = join(blocks[1, 0], *parts)
+    received = {(k, h): swap(block, k) if k else block for (k, h), block in blocks.items()}
+    lines = stack(len(near), blocks[1, 0], received[1, 0])
+    lines_of = {k: n for n, k in enumerate(near + [k ^ 1 for k in near])}
+
+    def turn(z):
+        return lax.ppermute(lines, "col", [(i, (i + z) % columns) for i in range(columns)])
+
+    totals = [lines] + [turn(z) for z in range(1, columns)]
+    place, assign = spread(mask, assign, groups, rows)
+    return finish(received, lines_of, totals, place, assign, groups, rows, slice_width)
+
+
+def fallback(coef, mask, assign):
     rows, width = coef.shape
     groups = lax.axis_size("scen")
     slice_width = width // groups
@@ -54,6 +437,12 @@
 def solution(mesh):
     in_specs = (P("scen", "col"), P(), P())
     out_specs = P("col", "scen", None)
-    return jax.shard_map(
-        on_device, mesh=mesh, in_specs=in_specs, out_specs=out_specs, check_vma=False
+    groups, columns = mesh.shape["scen"], mesh.shape["col"]
+    slice_width = NV // (groups * columns)
+    fits = groups == 8 and columns == 4 and slice_width % (2 * LANES) == 0
+    shard = functools.partial(
+        jax.shard_map, mesh=mesh, in_specs=in_specs, out_specs=out_specs, check_vma=False
     )
+    if not fits:
+        return shard(fallback)
+    return shard(exchange)

time: 96.1 us -> 55.7 us (0.58)
  local copies, waits for them, and re-layouts: 22.3 us -> 0.01 us
  other arithmetic: 18 us -> 0 us
  starting transfers between devices: 3.72 us -> 19.8 us
  blocking collectives: 13.5 us -> 0 us
  between operations: 13.5 us -> 0.1 us
  Pallas kernels: 0 us -> 10.1 us
  waiting for transfers between devices: 20 us -> 25.5 us
  matrix products: 4.46 us -> 0 us
    ppermute x0 -> x15, waiting for transfers between devices: none -> 25.5 us  [the longest x12 17.9 us: swap(): return lax.ppermute(value, 'scen', [(i, i ^ k) for i in range(groups)])]
    all_to_all x1 -> x0, waiting for transfers between devices: 20 us -> none  [on_device(): lax.all_to_all(picked, 'scen', split_axis=0, concat_axis=2, tiled=True)]
    ppermute x0 -> x15, starting transfers between devices: none -> 19.8 us  [the longest x12 13.2 us: swap(): return lax.ppermute(value, 'scen', [(i, i ^ k) for i in range(groups)])]
    psum x1 -> x0, blocking collectives: 13.5 us -> none  [on_device(): total = lax.psum(partial_value, 'col')]
    pallas_call x0 -> x8, Pallas kernels: none -> 10.1 us  [the longest x2 3.21 us: late(): pl.pallas_call(functools.partial(late_kernel, last, ACT_DEV * groups, ste...]
    gather x2 -> x0, local copies, waits for them, and re-layouts: 8.02 us -> none  [the longest x1 5.08 us: on_device(): return jnp.take(slotted, inverse, axis=2).reshape(1, slice_width, cut_total)]
    select_n x2 -> x0, local copies, waits for them, and re-layouts: 7.55 us -> none  [the longest x1 5.59 us: on_device(): return jnp.take(slotted, inverse, axis=2).reshape(1, slice_width, cut_total)]
    sort x2 -> x0, other arithmetic: 7.52 us -> none  [the longest x1 3.77 us: on_device(): kept_rows = jnp.argsort(1 - own_mask, stable=True)[:ACT_DEV]]
  transfers between devices with their start and end apart: 1 -> 15, of which waited for: 1 -> 8; matrix products, arithmetic and copies ran while one was open for 6% -> 0% of each run, Pallas kernels for 0% -> 7%
where the time goes in v2:
time: 55.7 us; the launch traced here: 55.6 us
  waiting for transfers between devices  25.5 us (46%)
  starting transfers between devices  19.8 us (36%)
  Pallas kernels  10.1 us (18%)
    ppermute x12, waiting for transfers between devices, swap(): return lax.ppermute(value, 'scen', [(i, i ^ k) for i in range(groups)])  17.9 us
    ppermute x12, starting transfers between devices, swap(): return lax.ppermute(value, 'scen', [(i, i ^ k) for i in range(groups)])  13.2 us
    ppermute x3, waiting for transfers between devices, turn(): lax.ppermute(lines, 'col', [(i, (i + z) % columns) for i in range(columns)])  7.63 us
    ppermute x3, starting transfers between devices, turn(): lax.ppermute(lines, 'col', [(i, (i + z) % columns) for i in range(columns)])  6.65 us
    pallas_call x2, Pallas kernels, late(): pl.pallas_call(functools.partial(late_kernel, last, ACT_DEV * groups, ste...  3.21 us
    pallas_call x1, Pallas kernels, pick(): pl.pallas_call(functools.partial(first_kernel, groups, rows, tiles, ahead...  2.83 us
    pallas_call x1, Pallas kernels, finish(): pl.pallas_call(functools.partial(early_kernel, [(k, lines_of[k]) for k in...  1.61 us
    pallas_call x1, Pallas kernels, pick(): pl.pallas_call(functools.partial(second_kernel, tiles, behind), out_shape...  1.48 us
  transfers between devices with their start and end apart: 15, of which 8 were waited for; matrix products, arithmetic and copies ran while one was open for 0% of the time, Pallas kernels for 7%

profile of v2, /device:TPU:0, one launch (start us, length us, event | category | flops | bytes accessed | tf_op | source)
XLA Modules:
  0.0 55.6 jit_solution(3600457144799765189)
XLA Ops:
  0.0 2.8 %first.1 = (f32[256,256]{1,0:T(8,128)S(1)}, f32[16,520,128]{2,1,0:T(8,128)S(1)}, f32[256,128]{1,0:T(8,128)S(1)}, s32[512]{0:T(512)S(4)}) custom-call(s32[4096]{0:T(1024)} %mask_ref.3, f32[512,2048]{1,0:T(8,128)} %coef_ref.1), custom_call_target="tpu_custom_call" | custom-call | tf_op jit(solution)/shard_map/first/pallas_call | solution.py:160
  2.8 0.0 copy-start
  2.8 1.5 %second.1 = (f32[256,256]{1,0:T(8,128)S(1)}, f32[264,256]{1,0:T(8,128)S(1)}, f32[256,256]{1,0:T(8,128)S(1)}, f32[256,256]{1,0:T(8,128)S(1)}, f32[256,256]{1,0:T(...) custom-call(f32[16,520,128]{2,1,0:T(8,128)S(1)} %get-tuple-element.2, ...), custom_call_target="tpu_custom_call" | custom-call | tf_op jit(solution)/shard_map/second/pallas_call | solution.py:173
  4.3 4.0 %collective-permute-start.2 = (f32[8,256]{1,0:T(8,128)S(1)}, f32[8,256]{1,0:T(8,128)S(1)}, u32[]{:S(2)}, u32[]{:S(2)}) collective-permute-start(f32[8,256]{1,0:T(8,128)S(1)} %get-tuple-element.33.refs_0_), channel_id=1, source_target_pairs={{0,24},{4,28},{8,16},{12,20},{16,8},{20,12},{24,0},{28,4},{1,25},{... | collective-permute-start | bytes 24584 | tf_op jit(solution)/shard_map/ppermute | solution.py:379
  8.3 0.5 collective-permute-start.1
  8.8 0.1 collective-permute-start
  8.9 1.0 %collective-permute-done.2.refs_3_ = f32[8,256]{1,0:T(8,128)S(1)} collective-permute-done((f32[8,256]{1,0:T(8,128)S(1)}, f32[8,256]{1,0:T(8,128)S(1)}, u32[]{:S(2)}, u32[]{:S(2)}) %collective-permute-start.2) | collective-permute-done | bytes 8224 | tf_op jit(solution)/shard_map/ppermute | solution.py:379
  9.9 2.0 %collective-permute-done.1.refs_2_ = f32[8,256]{1,0:T(8,128)S(1)} collective-permute-done((f32[8,256]{1,0:T(8,128)S(1)}, f32[8,256]{1,0:T(8,128)S(1)}, u32[]{:S(2)}, u32[]{:S(2)}) %collective-permute-start.1) | collective-permute-done | bytes 8224 | tf_op jit(solution)/shard_map/ppermute | solution.py:379
  11.9 0.5 collective-permute-done.refs_1_
  12.4 0.0 collective-permute-start.3
  12.4 0.2 collective-permute-start.7
  12.6 1.9 %collective-permute-start.8 = (f32[256,256]{1,0:T(8,128)S(1)}, f32[256,256]{1,0:T(8,128)S(1)}, u32[]{:S(2)}, u32[]{:S(2)}) collective-permute-start(f32[256,256]{1,0:T(8,128)S(1)} %get-tuple-element.36), channel_id=1, source_target_pairs={{0,16},{4,20},{8,24},{12,28},{16,0},{20,4},{24,8},{28,12},{1,17},{... | collective-permute-start | bytes 786440 | tf_op jit(solution)/shard_map/ppermute | solution.py:379
  14.6 0.9 %collective-permute-start.10 = (f32[256,256]{1,0:T(8,128)S(1)}, f32[256,256]{1,0:T(8,128)S(1)}, u32[]{:S(2)}, u32[]{:S(2)}) collective-permute-start(f32[256,256]{1,0:T(8,128)S(1)} %get-tuple-element.38), channel_id=1, source_target_pairs={{0,28},{4,24},{8,20},{12,16},{16,12},{20,8},{24,4},{28,0},{1,29},{... | collective-permute-start | bytes 786440 | tf_op jit(solution)/shard_map/ppermute | solution.py:379
  15.5 1.5 %collective-permute-start.9 = (f32[256,256]{1,0:T(8,128)S(1)}, f32[256,256]{1,0:T(8,128)S(1)}, u32[]{:S(2)}, u32[]{:S(2)}) collective-permute-start(f32[256,256]{1,0:T(8,128)S(1)} %get-tuple-element.37), channel_id=1, source_target_pairs={{0,24},{4,28},{8,16},{12,20},{16,8},{20,12},{24,0},{28,4},{1,25},{... | collective-permute-start | bytes 786440 | tf_op jit(solution)/shard_map/ppermute | solution.py:379
  17.0 4.7 %collective-permute-done.7.refs_6_ = f32[256,256]{1,0:T(8,128)S(1)} collective-permute-done((f32[256,256]{1,0:T(8,128)S(1)}, f32[256,256]{1,0:T(8,128)S(1)}, u32[]{:S(2)}, u32[]{:S(2)}) %collective-permute-start.7) | collective-permute-done | bytes 262176 | tf_op jit(solution)/shard_map/ppermute | solution.py:379
  21.7 0.0 collective-permute-start.13
  21.7 9.6 %collective-permute-done.8.refs_7_ = f32[256,256]{1,0:T(8,128)S(1)} collective-permute-done((f32[256,256]{1,0:T(8,128)S(1)}, f32[256,256]{1,0:T(8,128)S(1)}, u32[]{:S(2)}, u32[]{:S(2)}) %collective-permute-start.8) | collective-permute-done | bytes 262176 | tf_op jit(solution)/shard_map/ppermute | solution.py:379
  31.3 0.0 collective-permute-start.14
  31.3 0.0 collective-permute-done.10.refs_9_
  31.3 4.1 %collective-permute-start.11 = (f32[256,128]{1,0:T(8,128)S(1)}, f32[256,128]{1,0:T(8,128)S(1)}, u32[]{:S(2)}, u32[]{:S(2)}) collective-permute-start(f32[256,128]{1,0:T(8,128)S(1)} %get-tuple-element.41), channel_id=1, source_target_pairs={{0,12},{4,8},{8,4},{12,0},{16,28},{20,24},{24,20},{28,16},{1,13},{... | collective-permute-start | bytes 393224 | tf_op jit(solution)/shard_map/ppermute | solution.py:379
  35.4 0.0 collective-permute-done.3.refs_1_.refs_5_
  35.4 0.0 collective-permute-start.12
  35.4 0.0 collective-permute-done.9.refs_8_
  35.4 3.7 %collective-permute-start.6 = (f32[8,256]{1,0:T(8,128)S(1)}, f32[8,256]{1,0:T(8,128)S(1)}, u32[]{:S(2)}, u32[]{:S(2)}) collective-permute-start(f32[8,256]{1,0:T(8,128)S(1)} %stack.1.refs_0_), channel_id=1, source_target_pairs={{0,3},{1,0},{2,1},{3,2},{4,7},{5,4},{6,5},{7,6},{8,11},{9,8},{10,9... | collective-permute-start | bytes 24584 | tf_op jit(solution)/shard_map/ppermute | solution.py:390
  39.1 1.4 %collective-permute-done.6.refs_3_ = f32[8,256]{1,0:T(8,128)S(1)} collective-permute-done((f32[8,256]{1,0:T(8,128)S(1)}, f32[8,256]{1,0:T(8,128)S(1)}, u32[]{:S(2)}, u32[]{:S(2)}) %collective-permute-start.6) | collective-permute-done | bytes 8224 | tf_op jit(solution)/shard_map/ppermute | solution.py:390
  40.4 1.3 %collective-permute-start.5 = (f32[8,256]{1,0:T(8,128)S(1)}, f32[8,256]{1,0:T(8,128)S(1)}, u32[]{:S(2)}, u32[]{:S(2)}) collective-permute-start(f32[8,256]{1,0:T(8,128)S(1)} %stack.1.refs_0_), channel_id=1, source_target_pairs={{0,2},{1,3},{2,0},{3,1},{4,6},{5,7},{6,4},{7,5},{8,10},{9,11},{10,... | collective-permute-start | bytes 24584 | tf_op jit(solution)/shard_map/ppermute | solution.py:390
  41.7 3.3 %collective-permute-done.5.refs_2_ = f32[8,256]{1,0:T(8,128)S(1)} collective-permute-done((f32[8,256]{1,0:T(8,128)S(1)}, f32[8,256]{1,0:T(8,128)S(1)}, u32[]{:S(2)}, u32[]{:S(2)}) %collective-permute-start.5) | collective-permute-done | bytes 8224 | tf_op jit(solution)/shard_map/ppermute | solution.py:390
  45.0 1.7 %collective-permute-start.4 = (f32[8,256]{1,0:T(8,128)S(1)}, f32[8,256]{1,0:T(8,128)S(1)}, u32[]{:S(2)}, u32[]{:S(2)}) collective-permute-start(f32[8,256]{1,0:T(8,128)S(1)} %stack.1.refs_0_), channel_id=1, source_target_pairs={{0,1},{1,2},{2,3},{3,0},{4,5},{5,6},{6,7},{7,4},{8,9},{9,10},{10,1... | collective-permute-start | bytes 24584 | tf_op jit(solution)/shard_map/ppermute | solution.py:390
  46.7 0.0 copy-done
  46.7 1.0 %spread.1 = (bf16[8,512,256]{2,1,0:T(8,128)(2,1)S(1)}, s32[512]{0:T(512)S(4)}) custom-call(s32[4096]{0:T(1024)S(1)} %copy-done, s32[512]{0:T(512)} %assign_ref.1), custom_call_target="tpu_custom_call" | custom-call | tf_op jit(solution)/shard_map/spread/pallas_call | solution.py:243
  47.7 3.0 %collective-permute-done.4.refs_1_ = f32[8,256]{1,0:T(8,128)S(1)} collective-permute-done((f32[8,256]{1,0:T(8,128)S(1)}, f32[8,256]{1,0:T(8,128)S(1)}, u32[]{:S(2)}, u32[]{:S(2)}) %collective-permute-start.4) | collective-permute-done | bytes 8224 | tf_op jit(solution)/shard_map/ppermute | solution.py:390
  50.7 1.6 %early.1 = (f32[4096,128]{1,0:T(8,128)S(1)}, f32[4096,128]{1,0:T(8,128)S(1)}, f32[8,128]{1,0:T(8,128)S(1)}, f32[8,128]{1,0:T(8,128)S(1)}, f32[256,128]{1,0:T(8,128)S(1)}, /*index=5*/f32[256,128]{1,0:T(8,128)S(1)}) custom-call(s32[512]{0:T(512)S(4)} %get-tuple-element.27.assign_ref, bf16[8,512,256]{2,1,0:T(8,128)(2,1)S(1)} %get-tuple-element.28.place_ref, ...), custom_call_target="tpu_custom_call" | custom-call | tf_op jit(solution)/shard_map/early/pallas_call | solution.py:342
  52.3 0.0 collective-permute-done.13.refs_2_
  52.3 0.0 collective-permute-done.14.refs_3_
  52.3 1.1 %shard_map.37.refs_6_ = f32[128,4096]{1,0:T(8,128)S(1)} custom-call(s32[512]{0:T(512)S(4)} %get-tuple-element.27.assign_ref, bf16[8,512,256]{2,1,0:T(8,128)(2,1)S(1)} %get-tuple-element.28.place_ref, f32[256,128]{1,0:T(8,128)S(1)} %get-tuple-element.39.refs_0_, f32[256,128]{1,0:T(8,128)S(1)} %get-tuple-element.40.refs_1_, ...), custom_call_target="tpu_custom_call" | custom-call | tf_op jit(solution)/shard_map/pallas_call | solution.py:359
  53.5 0.0 collective-permute-done.11.refs_2_
  53.5 0.0 collective-permute-done.12.refs_3_
  53.5 2.1 %shard_map.38 = f32[1,256,4096]{2,1,0:T(8,128)} custom-call(s32[512]{0:T(512)S(4)} %get-tuple-element.27.assign_ref, bf16[8,512,256]{2,1,0:T(8,128)(2,1)S(1)} %get-tuple-element.28.place_ref, f32[256,128]{1,0:T(8,128)S(1)} %get-tuple-element.39.refs_0_, f32[256,128]{1,0:T(8,128)S(1)} %get-tuple-element.40.refs_1_, ...), custom_call_target="tpu_custom_call" | custom-call | tf_op jit(solution)/shard_map/pallas_call | solution.py:359
  (2 shorter events, 0.0 us)
Async XLA Ops:
  2.8 43.9 %copy-start = (s32[4096]{0:T(1024)S(1)}, s32[4096]{0:T(1024)}, u32[]{:S(2)}) copy-start(s32[4096]{0:T(1024)} %mask_ref.3) | copy-start | bytes 49156
  4.3 5.6 %collective-permute-start.2 = (f32[8,256]{1,0:T(8,128)S(1)}, f32[8,256]{1,0:T(8,128)S(1)}, u32[]{:S(2)}, u32[]{:S(2)}) collective-permute-start(f32[8,256]{1,0:T(8,128)S(1)} %get-tuple-element.33.refs_0_), channel_id=1, source_target_pairs={{0,24},{4,28},{8,16},{12,20},{16,8},{20,12},{24,0},{28,4},{1,25},{... | collective-permute-start | bytes 24584 | tf_op jit(solution)/shard_map/ppermute | solution.py:379
  8.3 3.7 %collective-permute-start.1 = (f32[8,256]{1,0:T(8,128)S(1)}, f32[8,256]{1,0:T(8,128)S(1)}, u32[]{:S(2)}, u32[]{:S(2)}) collective-permute-start(f32[8,256]{1,0:T(8,128)S(1)} %get-tuple-element.33.refs_0_), channel_id=1, source_target_pairs={{0,16},{4,20},{8,24},{12,28},{16,0},{20,4},{24,8},{28,12},{1,17},{... | collective-permute-start | bytes 24584 | tf_op jit(solution)/shard_map/ppermute | solution.py:379
  8.8 3.7 %collective-permute-start = (f32[8,256]{1,0:T(8,128)S(1)}, f32[8,256]{1,0:T(8,128)S(1)}, u32[]{:S(2)}, u32[]{:S(2)}) collective-permute-start(f32[8,256]{1,0:T(8,128)S(1)} %get-tuple-element.33.refs_0_), channel_id=1, source_target_pairs={{0,8},{4,12},{8,0},{12,4},{16,24},{20,28},{24,16},{28,20},{1,9},{5... | collective-permute-start | bytes 24584 | tf_op jit(solution)/shard_map/ppermute | solution.py:379
  12.4 23.0 %collective-permute-start.3 = (f32[264,256]{1,0:T(8,128)S(1)}, f32[264,256]{1,0:T(8,128)S(1)}, u32[]{:S(2)}, u32[]{:S(2)}) collective-permute-start(f32[264,256]{1,0:T(8,128)S(1)} %join.1.refs_0_), channel_id=1, source_target_pairs={{0,4},{4,0},{8,12},{12,8},{16,20},{20,16},{24,28},{28,24},{1,5},{5... | collective-permute-start | bytes 811016 | tf_op jit(solution)/shard_map/ppermute | solution.py:379
  12.4 9.2 %collective-permute-start.7 = (f32[256,256]{1,0:T(8,128)S(1)}, f32[256,256]{1,0:T(8,128)S(1)}, u32[]{:S(2)}, u32[]{:S(2)}) collective-permute-start(f32[256,256]{1,0:T(8,128)S(1)} %get-tuple-element.35), channel_id=1, source_target_pairs={{0,8},{4,12},{8,0},{12,4},{16,24},{20,28},{24,16},{28,20},{1,9},{5... | collective-permute-start | bytes 786440 | tf_op jit(solution)/shard_map/ppermute | solution.py:379
  12.6 18.7 %collective-permute-start.8 = (f32[256,256]{1,0:T(8,128)S(1)}, f32[256,256]{1,0:T(8,128)S(1)}, u32[]{:S(2)}, u32[]{:S(2)}) collective-permute-start(f32[256,256]{1,0:T(8,128)S(1)} %get-tuple-element.36), channel_id=1, source_target_pairs={{0,16},{4,20},{8,24},{12,28},{16,0},{20,4},{24,8},{28,12},{1,17},{... | collective-permute-start | bytes 786440 | tf_op jit(solution)/shard_map/ppermute | solution.py:379
  14.6 16.7 %collective-permute-start.10 = (f32[256,256]{1,0:T(8,128)S(1)}, f32[256,256]{1,0:T(8,128)S(1)}, u32[]{:S(2)}, u32[]{:S(2)}) collective-permute-start(f32[256,256]{1,0:T(8,128)S(1)} %get-tuple-element.38), channel_id=1, source_target_pairs={{0,28},{4,24},{8,20},{12,16},{16,12},{20,8},{24,4},{28,0},{1,29},{... | collective-permute-start | bytes 786440 | tf_op jit(solution)/shard_map/ppermute | solution.py:379
  15.5 19.9 %collective-permute-start.9 = (f32[256,256]{1,0:T(8,128)S(1)}, f32[256,256]{1,0:T(8,128)S(1)}, u32[]{:S(2)}, u32[]{:S(2)}) collective-permute-start(f32[256,256]{1,0:T(8,128)S(1)} %get-tuple-element.37), channel_id=1, source_target_pairs={{0,24},{4,28},{8,16},{12,20},{16,8},{20,12},{24,0},{28,4},{1,25},{... | collective-permute-start | bytes 786440 | tf_op jit(solution)/shard_map/ppermute | solution.py:379
  21.7 30.6 %collective-permute-start.13 = (f32[256,128]{1,0:T(8,128)S(1)}, f32[256,128]{1,0:T(8,128)S(1)}, u32[]{:S(2)}, u32[]{:S(2)}) collective-permute-start(f32[256,128]{1,0:T(8,128)S(1)} %get-tuple-element.45), channel_id=1, source_target_pairs={{0,12},{4,8},{8,4},{12,0},{16,28},{20,24},{24,20},{28,16},{1,13},{... | collective-permute-start | bytes 393224 | tf_op jit(solution)/shard_map/ppermute | solution.py:379
  31.3 21.0 %collective-permute-start.14 = (f32[256,128]{1,0:T(8,128)S(1)}, f32[256,128]{1,0:T(8,128)S(1)}, u32[]{:S(2)}, u32[]{:S(2)}) collective-permute-start(f32[256,128]{1,0:T(8,128)S(1)} %get-tuple-element.46), channel_id=1, source_target_pairs={{0,20},{4,16},{8,28},{12,24},{16,4},{20,0},{24,12},{28,8},{1,21},{... | collective-permute-start | bytes 393224 | tf_op jit(solution)/shard_map/ppermute | solution.py:379
  31.3 22.2 %collective-permute-start.11 = (f32[256,128]{1,0:T(8,128)S(1)}, f32[256,128]{1,0:T(8,128)S(1)}, u32[]{:S(2)}, u32[]{:S(2)}) collective-permute-start(f32[256,128]{1,0:T(8,128)S(1)} %get-tuple-element.41), channel_id=1, source_target_pairs={{0,12},{4,8},{8,4},{12,0},{16,28},{20,24},{24,20},{28,16},{1,13},{... | collective-permute-start | bytes 393224 | tf_op jit(solution)/shard_map/ppermute | solution.py:379
  35.4 18.1 %collective-permute-start.12 = (f32[256,128]{1,0:T(8,128)S(1)}, f32[256,128]{1,0:T(8,128)S(1)}, u32[]{:S(2)}, u32[]{:S(2)}) collective-permute-start(f32[256,128]{1,0:T(8,128)S(1)} %get-tuple-element.42), channel_id=1, source_target_pairs={{0,20},{4,16},{8,28},{12,24},{16,4},{20,0},{24,12},{28,8},{1,21},{... | collective-permute-start | bytes 393224 | tf_op jit(solution)/shard_map/ppermute | solution.py:379
  35.4 5.0 %collective-permute-start.6 = (f32[8,256]{1,0:T(8,128)S(1)}, f32[8,256]{1,0:T(8,128)S(1)}, u32[]{:S(2)}, u32[]{:S(2)}) collective-permute-start(f32[8,256]{1,0:T(8,128)S(1)} %stack.1.refs_0_), channel_id=1, source_target_pairs={{0,3},{1,0},{2,1},{3,2},{4,7},{5,4},{6,5},{7,6},{8,11},{9,8},{10,9... | collective-permute-start | bytes 24584 | tf_op jit(solution)/shard_map/ppermute | solution.py:390
  40.4 4.5 %collective-permute-start.5 = (f32[8,256]{1,0:T(8,128)S(1)}, f32[8,256]{1,0:T(8,128)S(1)}, u32[]{:S(2)}, u32[]{:S(2)}) collective-permute-start(f32[8,256]{1,0:T(8,128)S(1)} %stack.1.refs_0_), channel_id=1, source_target_pairs={{0,2},{1,3},{2,0},{3,1},{4,6},{5,7},{6,4},{7,5},{8,10},{9,11},{10,... | collective-permute-start | bytes 24584 | tf_op jit(solution)/shard_map/ppermute | solution.py:390
  45.0 5.7 %collective-permute-start.4 = (f32[8,256]{1,0:T(8,128)S(1)}, f32[8,256]{1,0:T(8,128)S(1)}, u32[]{:S(2)}, u32[]{:S(2)}) collective-permute-start(f32[8,256]{1,0:T(8,128)S(1)} %stack.1.refs_0_), channel_id=1, source_target_pairs={{0,1},{1,2},{2,3},{3,0},{4,5},{5,6},{6,7},{7,4},{8,9},{9,10},{10,1... | collective-permute-start | bytes 24584 | tf_op jit(solution)/shard_map/ppermute | solution.py:390

commit v3 on v2

--- a/solution.py
+++ b/solution.py
@@ -15,7 +15,6 @@
 EPS = 1e-06
 LANES = 128
 SUBLANES = 8
-CHUNKS = 4
 VMEM = pl.BlockSpec(memory_space=pltpu.VMEM)
 HBM = pl.BlockSpec(memory_space=pltpu.HBM)
 SMEM = pl.BlockSpec(memory_space=pltpu.SMEM)
@@ -51,6 +50,10 @@
     first = [(k, 0, tiles // 2) for k in halved(groups)]
     second = [(k, tiles // 2, tiles) for k in halved(groups)]
     return whole + first + second
+
+
+def ahead_of_all(begin):
+    lax.fori_loop(0, jnp.minimum(lax.axis_index("scen") + 1, 1), begin, 0)
 
 
 def pack(first, picks, window, cells, total):
@@ -76,24 +79,33 @@
     outs = refs[: len(parts)]
     window, squares, order, live, sems, mask_sem = refs[len(parts) :]
     me = lax.axis_index("scen")
-    chunk = rows // CHUNKS
-    places = [(k, h) for k in range(groups) for h in range(tiles)]
     cells = cells_of(parts, outs, tiles)
-    places.sort(key=lambda place: place[0] not in [k for k, _, _ in parts])
-
-    def copy(c, k, h):
-        span = pl.ds(c * chunk, chunk)
+    ahead = [t for t, _, _ in cells]
+    every = groups * tiles
+    runs = [(ahead[0], ahead[-1] + 1), (0, ahead[0]), (ahead[-1] + 1, every)]
+
+    def copy(run, t):
+        k, h = divmod(t, tiles)
         column = pl.multiple_of((jnp.bitwise_xor(me, k) * tiles + h) * LANES, LANES)
-        t = k * tiles + h
         return pltpu.make_async_copy(
-            coef_ref.at[span, pl.ds(column, LANES)], window.at[t, span], sems.at[c, t]
+            coef_ref.at[:, pl.ds(column, LANES)], window.at[t, pl.ds(0, rows)], sems.at[run]
         )
 
+    def wait(run):
+        start, end = runs[run]
+        landed = window.at[pl.ds(start, end - start), pl.ds(0, rows)]
+        pltpu.make_async_copy(landed, landed, sems.at[run]).wait()
+
     mask_copy = pltpu.make_async_copy(mask_ref.at[pl.ds(me * rows, rows)], live, mask_sem)
-    mask_copy.start()
-    for k, h in places:
-        for c in range(CHUNKS):
-            copy(c, k, h).start()
+
+    def begin(i, carry):
+        mask_copy.start()
+        return carry
+
+    ahead_of_all(begin)
+    for run, (start, end) in enumerate(runs):
+        for t in range(start, end):
+            copy(run, t).start()
 
     def note(i, n):
         marks = [live[i * SUBLANES + j] for j in range(SUBLANES)]
@@ -111,16 +123,10 @@
 
     mask_copy.wait()
     lax.fori_loop(0, rows // SUBLANES, note, jnp.int32(0), unroll=4)
-    inside = [k for k, _, _ in parts]
-    for k, h in places:
-        for c in range(CHUNKS):
-            if k in inside:
-                copy(c, k, h).wait()
+    wait(0)
     lax.fori_loop(0, ACT_DEV // SUBLANES, gather, 0, unroll=2)
-    for k, h in places:
-        for c in range(CHUNKS):
-            if k not in inside:
-                copy(c, k, h).wait()
+    wait(1)
+    wait(2)
 
 
 def second_kernel(tiles, parts, window, before, order, *refs):
@@ -164,7 +170,7 @@
         out_specs=[VMEM] * (len(ahead) + 2) + [SMEM],
         scratch_shapes=[
             pltpu.SMEM((rows,), jnp.int32),
-            pltpu.SemaphoreType.DMA((CHUNKS, groups * tiles)),
+            pltpu.SemaphoreType.DMA((3,)),
             pltpu.SemaphoreType.DMA,
         ],
         name="first",
@@ -264,9 +270,9 @@
     high = value.astype(jnp.bfloat16)
     low = (value - high.astype(jnp.float32)).astype(jnp.bfloat16)
     place = place_ref[source]
-    wide = jnp.dot(place, high, preferred_element_type=jnp.float32) + jnp.dot(
-        place, low, preferred_element_type=jnp.float32
-    )
+    both = jnp.concatenate([high, low], axis=1)
+    wide = jnp.dot(place, both, preferred_element_type=jnp.float32)
+    wide = wide[:, : high.shape[1]] + wide[:, high.shape[1] :]
     slots = wide.shape[0] // K
     for i in range(slots):
         at = pl.multiple_of(assign_ref[source * slots + i] * K, K)
@@ -295,23 +301,24 @@
     squares_b[...] = squares[:, half:]
 
 
-def late_kernel(last, active_total, steps, assign_ref, place_ref, *refs):
+def turned_by_matmul(value):
+    high = value.astype(jnp.bfloat16)
+    low = (value - high.astype(jnp.float32)).astype(jnp.bfloat16)
+    both = jnp.concatenate([high, low], axis=1)
+    shape = (value.shape[1], both.shape[1])
+    row = lax.broadcasted_iota(jnp.int32, shape, 0)
+    column = lax.broadcasted_iota(jnp.int32, shape, 1)
+    unit = jnp.where(jnp.bitwise_and(column, shape[0] - 1) == row, 1.0, 0.0).astype(jnp.bfloat16)
+    return lax.dot_general(
+        unit, both, (((1,), (1,)), ((), ())), preferred_element_type=jnp.float32
+    )
+
+
+def late_kernel(last, active_total, half, assign_ref, place_ref, *refs):
     n = len(last)
     scales, got, (flat, squares_ref) = refs[:n], refs[n : 2 * n], refs[2 * n : 2 * n + 2]
-    copies = []
+    out_ref, out_v, sem = refs[-3:]
     cuts, width = flat.shape
-    if steps:
-        other_ref, out_ref, out_v, sems = refs[2 * n + 2 :]
-        target = out_ref.at[0, pl.ds(0, width)]
-        copies.append(pltpu.make_async_copy(other_ref, target, sems.at[steps]))
-
-        def begin(i, carry):
-            copies[0].start()
-            return carry
-
-        lax.fori_loop(0, jnp.minimum(lax.axis_index("scen") + 1, 1), begin, 0)
-    else:
-        (out_v,) = refs[2 * n + 2 :]
     squares = squares_ref[...]
     for k, scale, got_ref in zip(last, scales, got):
         squares = squares + place_rows(k, scale[...], got_ref, place_ref, assign_ref, [flat])
@@ -320,13 +327,11 @@
     step = 4 * LANES
     for c in range(cuts // step):
         span = pl.ds(c * step, step)
-        out_v[:, span] = (flat[span, :] * inverse).T
-        if steps:
-            target = out_ref.at[0, pl.ds(width, width), span]
-            copies.append(pltpu.make_async_copy(out_v.at[:, span], target, sems.at[c]))
-            copies[-1].start()
-    for one in copies:
-        one.wait()
+        value = flat[span, :] * inverse
+        out_v[:, span] = value.T if half or c % 2 == 0 else turned_by_matmul(value)
+        target = out_ref.at[0, pl.ds(half * width, width), span]
+        pltpu.make_async_copy(out_v.at[:, span], target, sem).start()
+    pltpu.make_async_copy(out_v, out_ref.at[0, pl.ds(half * width, width)], sem).wait()
 
 
 def finish(received, lines_of, totals, place, assign, groups, rows, slice_width):
@@ -352,16 +357,14 @@
 
     def late(n, flat, squares, *other):
         got = [received[k, n * half // LANES] for k in last]
-        values = on_chip(*scales, *got, flat, squares, *other)
-        steps = cuts // (4 * LANES) if n else 0
-        turned = pltpu.VMEM((half, cuts), jnp.float32)
-        whole = jax.ShapeDtypeStruct((1, slice_width, cuts), jnp.float32)
+        values = on_chip(*scales, *got, flat, squares) + in_hbm(*other)
         return pl.pallas_call(
-            functools.partial(late_kernel, last, ACT_DEV * groups, steps),
-            out_shape=whole if n else turned,
-            in_specs=[SMEM] + [VMEM] * (1 + len(values)),
-            out_specs=HBM if n else VMEM,
-            scratch_shapes=[turned, pltpu.SemaphoreType.DMA((steps + 1,))] if n else [],
+            functools.partial(late_kernel, last, ACT_DEV * groups, n),
+            out_shape=jax.ShapeDtypeStruct((1, slice_width, cuts), jnp.float32),
+            in_specs=[SMEM] + [VMEM] * (1 + len(values) - n) + [HBM] * n,
+            out_specs=HBM,
+            scratch_shapes=[pltpu.VMEM((half, cuts), jnp.float32), pltpu.SemaphoreType.DMA],
+            input_output_aliases={len(values) + 1: 0} if n else {},
             compiler_params=PARAMS,
         )(assign, place, *values)
 

time: 55.7 us -> 55.5 us (level)
    pallas_call x1, Pallas kernels: 2.83 us -> 2.23 us  [pick(): pl.pallas_call(functools.partial(first_kernel, groups, rows, tiles, ahead...]
  transfers between devices with their start and end apart: 15 -> 15, of which waited for: 8 -> 8; matrix products, arithmetic and copies ran while one was open for 0% -> 0% of each run, Pallas kernels for 7% -> 8%
where the time goes in v3:
time: 55.5 us; the launch traced here: 55.4 us
  waiting for transfers between devices  25.5 us (46%)
  starting transfers between devices  19.8 us (36%)
  Pallas kernels  9.92 us (18%)
    ppermute x12, waiting for transfers between devices, swap(): return lax.ppermute(value, 'scen', [(i, i ^ k) for i in range(groups)])  17.9 us
    ppermute x12, starting transfers between devices, swap(): return lax.ppermute(value, 'scen', [(i, i ^ k) for i in range(groups)])  13.2 us
    ppermute x3, waiting for transfers between devices, turn(): lax.ppermute(lines, 'col', [(i, (i + z) % columns) for i in range(columns)])  7.63 us
    ppermute x3, starting transfers between devices, turn(): lax.ppermute(lines, 'col', [(i, (i + z) % columns) for i in range(columns)])  6.65 us
    pallas_call x2, Pallas kernels, late(): pl.pallas_call(functools.partial(late_kernel, last, ACT_DEV * groups, n),...  3.65 us
    pallas_call x1, Pallas kernels, pick(): pl.pallas_call(functools.partial(first_kernel, groups, rows, tiles, ahead...  2.23 us
    pallas_call x1, Pallas kernels, finish(): pl.pallas_call(functools.partial(early_kernel, [(k, lines_of[k]) for k in...  1.55 us
    pallas_call x1, Pallas kernels, pick(): pl.pallas_call(functools.partial(second_kernel, tiles, behind), out_shape...  1.48 us
  transfers between devices with their start and end apart: 15, of which 8 were waited for; matrix products, arithmetic and copies ran while one was open for 0% of the time, Pallas kernels for 8%

profile of v3, /device:TPU:0, one launch (start us, length us, event | category | flops | bytes accessed | tf_op | source)
XLA Modules:
  0.0 55.4 jit_solution(7163290391056654490)
XLA Ops:
  0.0 0.0 copy-start
  0.0 2.2 %first.1 = (f32[256,256]{1,0:T(8,128)S(1)}, f32[16,520,128]{2,1,0:T(8,128)S(1)}, f32[256,128]{1,0:T(8,128)S(1)}, s32[512]{0:T(512)S(4)}) custom-call(s32[4096]{0:T(1024)} %mask_ref.3, f32[512,2048]{1,0:T(8,128)} %coef_ref.1), custom_call_target="tpu_custom_call" | custom-call | tf_op jit(solution)/shard_map/first/pallas_call | solution.py:166
  2.2 1.5 %second.1 = (f32[256,256]{1,0:T(8,128)S(1)}, f32[264,256]{1,0:T(8,128)S(1)}, f32[256,256]{1,0:T(8,128)S(1)}, f32[256,256]{1,0:T(8,128)S(1)}, f32[256,256]{1,0:T(...) custom-call(f32[16,520,128]{2,1,0:T(8,128)S(1)} %get-tuple-element.2, ...), custom_call_target="tpu_custom_call" | custom-call | tf_op jit(solution)/shard_map/second/pallas_call | solution.py:179
  3.7 4.0 %collective-permute-start.2 = (f32[8,256]{1,0:T(8,128)S(1)}, f32[8,256]{1,0:T(8,128)S(1)}, u32[]{:S(2)}, u32[]{:S(2)}) collective-permute-start(f32[8,256]{1,0:T(8,128)S(1)} %get-tuple-element.33.refs_0_), channel_id=1, source_target_pairs={{0,24},{4,28},{8,16},{12,20},{16,8},{20,12},{24,0},{28,4},{1,25},{... | collective-permute-start | bytes 24584 | tf_op jit(solution)/shard_map/ppermute | solution.py:382
  7.7 0.5 collective-permute-start.1
  8.2 0.1 collective-permute-start
  8.3 1.0 %collective-permute-done.2.refs_3_ = f32[8,256]{1,0:T(8,128)S(1)} collective-permute-done((f32[8,256]{1,0:T(8,128)S(1)}, f32[8,256]{1,0:T(8,128)S(1)}, u32[]{:S(2)}, u32[]{:S(2)}) %collective-permute-start.2) | collective-permute-done | bytes 8224 | tf_op jit(solution)/shard_map/ppermute | solution.py:382
  9.3 2.0 %collective-permute-done.1.refs_2_ = f32[8,256]{1,0:T(8,128)S(1)} collective-permute-done((f32[8,256]{1,0:T(8,128)S(1)}, f32[8,256]{1,0:T(8,128)S(1)}, u32[]{:S(2)}, u32[]{:S(2)}) %collective-permute-start.1) | collective-permute-done | bytes 8224 | tf_op jit(solution)/shard_map/ppermute | solution.py:382
  11.3 0.5 collective-permute-done.refs_1_
  11.8 0.0 collective-permute-start.3
  11.8 0.2 collective-permute-start.7
  12.0 1.9 %collective-permute-start.8 = (f32[256,256]{1,0:T(8,128)S(1)}, f32[256,256]{1,0:T(8,128)S(1)}, u32[]{:S(2)}, u32[]{:S(2)}) collective-permute-start(f32[256,256]{1,0:T(8,128)S(1)} %get-tuple-element.36), channel_id=1, source_target_pairs={{0,16},{4,20},{8,24},{12,28},{16,0},{20,4},{24,8},{28,12},{1,17},{... | collective-permute-start | bytes 786440 | tf_op jit(solution)/shard_map/ppermute | solution.py:382
  14.0 0.9 %collective-permute-start.10 = (f32[256,256]{1,0:T(8,128)S(1)}, f32[256,256]{1,0:T(8,128)S(1)}, u32[]{:S(2)}, u32[]{:S(2)}) collective-permute-start(f32[256,256]{1,0:T(8,128)S(1)} %get-tuple-element.38), channel_id=1, source_target_pairs={{0,28},{4,24},{8,20},{12,16},{16,12},{20,8},{24,4},{28,0},{1,29},{... | collective-permute-start | bytes 786440 | tf_op jit(solution)/shard_map/ppermute | solution.py:382
  14.9 1.5 %collective-permute-start.9 = (f32[256,256]{1,0:T(8,128)S(1)}, f32[256,256]{1,0:T(8,128)S(1)}, u32[]{:S(2)}, u32[]{:S(2)}) collective-permute-start(f32[256,256]{1,0:T(8,128)S(1)} %get-tuple-element.37), channel_id=1, source_target_pairs={{0,24},{4,28},{8,16},{12,20},{16,8},{20,12},{24,0},{28,4},{1,25},{... | collective-permute-start | bytes 786440 | tf_op jit(solution)/shard_map/ppermute | solution.py:382
  16.4 4.7 %collective-permute-done.7.refs_6_ = f32[256,256]{1,0:T(8,128)S(1)} collective-permute-done((f32[256,256]{1,0:T(8,128)S(1)}, f32[256,256]{1,0:T(8,128)S(1)}, u32[]{:S(2)}, u32[]{:S(2)}) %collective-permute-start.7) | collective-permute-done | bytes 262176 | tf_op jit(solution)/shard_map/ppermute | solution.py:382
  21.1 0.0 collective-permute-start.13
  21.1 9.6 %collective-permute-done.8.refs_7_ = f32[256,256]{1,0:T(8,128)S(1)} collective-permute-done((f32[256,256]{1,0:T(8,128)S(1)}, f32[256,256]{1,0:T(8,128)S(1)}, u32[]{:S(2)}, u32[]{:S(2)}) %collective-permute-start.8) | collective-permute-done | bytes 262176 | tf_op jit(solution)/shard_map/ppermute | solution.py:382
  30.7 0.0 collective-permute-start.14
  30.7 0.0 collective-permute-done.10.refs_9_
  30.7 4.1 %collective-permute-start.11 = (f32[256,128]{1,0:T(8,128)S(1)}, f32[256,128]{1,0:T(8,128)S(1)}, u32[]{:S(2)}, u32[]{:S(2)}) collective-permute-start(f32[256,128]{1,0:T(8,128)S(1)} %get-tuple-element.41), channel_id=1, source_target_pairs={{0,12},{4,8},{8,4},{12,0},{16,28},{20,24},{24,20},{28,16},{1,13},{... | collective-permute-start | bytes 393224 | tf_op jit(solution)/shard_map/ppermute | solution.py:382
  34.8 0.0 collective-permute-done.3.refs_1_.refs_5_
  34.8 0.0 collective-permute-start.12
  34.8 0.0 collective-permute-done.9.refs_8_
  34.8 3.7 %collective-permute-start.6 = (f32[8,256]{1,0:T(8,128)S(1)}, f32[8,256]{1,0:T(8,128)S(1)}, u32[]{:S(2)}, u32[]{:S(2)}) collective-permute-start(f32[8,256]{1,0:T(8,128)S(1)} %stack.1.refs_0_), channel_id=1, source_target_pairs={{0,3},{1,0},{2,1},{3,2},{4,7},{5,4},{6,5},{7,6},{8,11},{9,8},{10,9... | collective-permute-start | bytes 24584 | tf_op jit(solution)/shard_map/ppermute | solution.py:393
  38.5 1.4 %collective-permute-done.6.refs_3_ = f32[8,256]{1,0:T(8,128)S(1)} collective-permute-done((f32[8,256]{1,0:T(8,128)S(1)}, f32[8,256]{1,0:T(8,128)S(1)}, u32[]{:S(2)}, u32[]{:S(2)}) %collective-permute-start.6) | collective-permute-done | bytes 8224 | tf_op jit(solution)/shard_map/ppermute | solution.py:393
  39.8 1.3 %collective-permute-start.5 = (f32[8,256]{1,0:T(8,128)S(1)}, f32[8,256]{1,0:T(8,128)S(1)}, u32[]{:S(2)}, u32[]{:S(2)}) collective-permute-start(f32[8,256]{1,0:T(8,128)S(1)} %stack.1.refs_0_), channel_id=1, source_target_pairs={{0,2},{1,3},{2,0},{3,1},{4,6},{5,7},{6,4},{7,5},{8,10},{9,11},{10,... | collective-permute-start | bytes 24584 | tf_op jit(solution)/shard_map/ppermute | solution.py:393
  41.1 3.3 %collective-permute-done.5.refs_2_ = f32[8,256]{1,0:T(8,128)S(1)} collective-permute-done((f32[8,256]{1,0:T(8,128)S(1)}, f32[8,256]{1,0:T(8,128)S(1)}, u32[]{:S(2)}, u32[]{:S(2)}) %collective-permute-start.5) | collective-permute-done | bytes 8224 | tf_op jit(solution)/shard_map/ppermute | solution.py:393
  44.4 1.7 %collective-permute-start.4 = (f32[8,256]{1,0:T(8,128)S(1)}, f32[8,256]{1,0:T(8,128)S(1)}, u32[]{:S(2)}, u32[]{:S(2)}) collective-permute-start(f32[8,256]{1,0:T(8,128)S(1)} %stack.1.refs_0_), channel_id=1, source_target_pairs={{0,1},{1,2},{2,3},{3,0},{4,5},{5,6},{6,7},{7,4},{8,9},{9,10},{10,1... | collective-permute-start | bytes 24584 | tf_op jit(solution)/shard_map/ppermute | solution.py:393
  46.1 0.0 copy-done
  46.1 1.0 %spread.1 = (bf16[8,512,256]{2,1,0:T(8,128)(2,1)S(1)}, s32[512]{0:T(512)S(4)}) custom-call(s32[4096]{0:T(1024)S(1)} %copy-done, s32[512]{0:T(512)} %assign_ref.1), custom_call_target="tpu_custom_call" | custom-call | tf_op jit(solution)/shard_map/spread/pallas_call | solution.py:249
  47.1 3.0 %collective-permute-done.4.refs_1_ = f32[8,256]{1,0:T(8,128)S(1)} collective-permute-done((f32[8,256]{1,0:T(8,128)S(1)}, f32[8,256]{1,0:T(8,128)S(1)}, u32[]{:S(2)}, u32[]{:S(2)}) %collective-permute-start.4) | collective-permute-done | bytes 8224 | tf_op jit(solution)/shard_map/ppermute | solution.py:393
  50.1 1.6 %early.1 = (f32[4096,128]{1,0:T(8,128)S(1)}, f32[4096,128]{1,0:T(8,128)S(1)}, f32[8,128]{1,0:T(8,128)S(1)}, f32[8,128]{1,0:T(8,128)S(1)}, f32[256,128]{1,0:T(8,128)S(1)}, /*index=5*/f32[256,128]{1,0:T(8,128)S(1)}) custom-call(s32[512]{0:T(512)S(4)} %get-tuple-element.27.assign_ref, bf16[8,512,256]{2,1,0:T(8,128)(2,1)S(1)} %get-tuple-element.28.place_ref, ...), custom_call_target="tpu_custom_call" | custom-call | tf_op jit(solution)/shard_map/early/pallas_call | solution.py:347
  51.7 0.0 collective-permute-done.13.refs_2_
  51.7 0.0 collective-permute-done.14.refs_3_
  51.7 1.9 %shard_map.37.refs_6_ = f32[1,256,4096]{2,1,0:T(8,128)} custom-call(s32[512]{0:T(512)S(4)} %get-tuple-element.27.assign_ref, bf16[8,512,256]{2,1,0:T(8,128)(2,1)S(1)} %get-tuple-element.28.place_ref, f32[256,128]{1,0:T(8,128)S(1)} %get-tuple-element.39.refs_0_, f32[256,128]{1,0:T(8,128)S(1)} %get-tuple-element.40.refs_1_, ...), custom_call_target="tpu_custom_call" | custom-call | tf_op jit(solution)/shard_map/pallas_call | solution.py:361
  53.5 0.0 collective-permute-done.11.refs_2_
  53.5 0.0 collective-permute-done.12.refs_3_
  53.6 1.8 %shard_map.38 = f32[1,256,4096]{2,1,0:T(8,128)} custom-call(s32[512]{0:T(512)S(4)} %get-tuple-element.27.assign_ref, bf16[8,512,256]{2,1,0:T(8,128)(2,1)S(1)} %get-tuple-element.28.place_ref, f32[256,128]{1,0:T(8,128)S(1)} %get-tuple-element.39.refs_0_, f32[256,128]{1,0:T(8,128)S(1)} %get-tuple-element.40.refs_1_, ...), custom_call_target="tpu_custom_call", output_to_operand_aliasing={{}: (8, {})} | custom-call | tf_op jit(solution)/shard_map/pallas_call | solution.py:361
  (2 shorter events, 0.0 us)
Async XLA Ops:
  0.0 46.1 %copy-start = (s32[4096]{0:T(1024)S(1)}, s32[4096]{0:T(1024)}, u32[]{:S(2)}) copy-start(s32[4096]{0:T(1024)} %mask_ref.3) | copy-start | bytes 49156
  3.7 5.6 %collective-permute-start.2 = (f32[8,256]{1,0:T(8,128)S(1)}, f32[8,256]{1,0:T(8,128)S(1)}, u32[]{:S(2)}, u32[]{:S(2)}) collective-permute-start(f32[8,256]{1,0:T(8,128)S(1)} %get-tuple-element.33.refs_0_), channel_id=1, source_target_pairs={{0,24},{4,28},{8,16},{12,20},{16,8},{20,12},{24,0},{28,4},{1,25},{... | collective-permute-start | bytes 24584 | tf_op jit(solution)/shard_map/ppermute | solution.py:382
  7.7 3.7 %collective-permute-start.1 = (f32[8,256]{1,0:T(8,128)S(1)}, f32[8,256]{1,0:T(8,128)S(1)}, u32[]{:S(2)}, u32[]{:S(2)}) collective-permute-start(f32[8,256]{1,0:T(8,128)S(1)} %get-tuple-element.33.refs_0_), channel_id=1, source_target_pairs={{0,16},{4,20},{8,24},{12,28},{16,0},{20,4},{24,8},{28,12},{1,17},{... | collective-permute-start | bytes 24584 | tf_op jit(solution)/shard_map/ppermute | solution.py:382
  8.2 3.7 %collective-permute-start = (f32[8,256]{1,0:T(8,128)S(1)}, f32[8,256]{1,0:T(8,128)S(1)}, u32[]{:S(2)}, u32[]{:S(2)}) collective-permute-start(f32[8,256]{1,0:T(8,128)S(1)} %get-tuple-element.33.refs_0_), channel_id=1, source_target_pairs={{0,8},{4,12},{8,0},{12,4},{16,24},{20,28},{24,16},{28,20},{1,9},{5... | collective-permute-start | bytes 24584 | tf_op jit(solution)/shard_map/ppermute | solution.py:382
  11.8 23.0 %collective-permute-start.3 = (f32[264,256]{1,0:T(8,128)S(1)}, f32[264,256]{1,0:T(8,128)S(1)}, u32[]{:S(2)}, u32[]{:S(2)}) collective-permute-start(f32[264,256]{1,0:T(8,128)S(1)} %join.1.refs_0_), channel_id=1, source_target_pairs={{0,4},{4,0},{8,12},{12,8},{16,20},{20,16},{24,28},{28,24},{1,5},{5... | collective-permute-start | bytes 811016 | tf_op jit(solution)/shard_map/ppermute | solution.py:382
  11.8 9.2 %collective-permute-start.7 = (f32[256,256]{1,0:T(8,128)S(1)}, f32[256,256]{1,0:T(8,128)S(1)}, u32[]{:S(2)}, u32[]{:S(2)}) collective-permute-start(f32[256,256]{1,0:T(8,128)S(1)} %get-tuple-element.35), channel_id=1, source_target_pairs={{0,8},{4,12},{8,0},{12,4},{16,24},{20,28},{24,16},{28,20},{1,9},{5... | collective-permute-start | bytes 786440 | tf_op jit(solution)/shard_map/ppermute | solution.py:382
  12.0 18.7 %collective-permute-start.8 = (f32[256,256]{1,0:T(8,128)S(1)}, f32[256,256]{1,0:T(8,128)S(1)}, u32[]{:S(2)}, u32[]{:S(2)}) collective-permute-start(f32[256,256]{1,0:T(8,128)S(1)} %get-tuple-element.36), channel_id=1, source_target_pairs={{0,16},{4,20},{8,24},{12,28},{16,0},{20,4},{24,8},{28,12},{1,17},{... | collective-permute-start | bytes 786440 | tf_op jit(solution)/shard_map/ppermute | solution.py:382
  14.0 16.7 %collective-permute-start.10 = (f32[256,256]{1,0:T(8,128)S(1)}, f32[256,256]{1,0:T(8,128)S(1)}, u32[]{:S(2)}, u32[]{:S(2)}) collective-permute-start(f32[256,256]{1,0:T(8,128)S(1)} %get-tuple-element.38), channel_id=1, source_target_pairs={{0,28},{4,24},{8,20},{12,16},{16,12},{20,8},{24,4},{28,0},{1,29},{... | collective-permute-start | bytes 786440 | tf_op jit(solution)/shard_map/ppermute | solution.py:382
  14.9 19.9 %collective-permute-start.9 = (f32[256,256]{1,0:T(8,128)S(1)}, f32[256,256]{1,0:T(8,128)S(1)}, u32[]{:S(2)}, u32[]{:S(2)}) collective-permute-start(f32[256,256]{1,0:T(8,128)S(1)} %get-tuple-element.37), channel_id=1, source_target_pairs={{0,24},{4,28},{8,16},{12,20},{16,8},{20,12},{24,0},{28,4},{1,25},{... | collective-permute-start | bytes 786440 | tf_op jit(solution)/shard_map/ppermute | solution.py:382
  21.1 30.6 %collective-permute-start.13 = (f32[256,128]{1,0:T(8,128)S(1)}, f32[256,128]{1,0:T(8,128)S(1)}, u32[]{:S(2)}, u32[]{:S(2)}) collective-permute-start(f32[256,128]{1,0:T(8,128)S(1)} %get-tuple-element.45), channel_id=1, source_target_pairs={{0,12},{4,8},{8,4},{12,0},{16,28},{20,24},{24,20},{28,16},{1,13},{... | collective-permute-start | bytes 393224 | tf_op jit(solution)/shard_map/ppermute | solution.py:382
  30.7 21.0 %collective-permute-start.14 = (f32[256,128]{1,0:T(8,128)S(1)}, f32[256,128]{1,0:T(8,128)S(1)}, u32[]{:S(2)}, u32[]{:S(2)}) collective-permute-start(f32[256,128]{1,0:T(8,128)S(1)} %get-tuple-element.46), channel_id=1, source_target_pairs={{0,20},{4,16},{8,28},{12,24},{16,4},{20,0},{24,12},{28,8},{1,21},{... | collective-permute-start | bytes 393224 | tf_op jit(solution)/shard_map/ppermute | solution.py:382
  30.7 22.9 %collective-permute-start.11 = (f32[256,128]{1,0:T(8,128)S(1)}, f32[256,128]{1,0:T(8,128)S(1)}, u32[]{:S(2)}, u32[]{:S(2)}) collective-permute-start(f32[256,128]{1,0:T(8,128)S(1)} %get-tuple-element.41), channel_id=1, source_target_pairs={{0,12},{4,8},{8,4},{12,0},{16,28},{20,24},{24,20},{28,16},{1,13},{... | collective-permute-start | bytes 393224 | tf_op jit(solution)/shard_map/ppermute | solution.py:382
  34.8 18.8 %collective-permute-start.12 = (f32[256,128]{1,0:T(8,128)S(1)}, f32[256,128]{1,0:T(8,128)S(1)}, u32[]{:S(2)}, u32[]{:S(2)}) collective-permute-start(f32[256,128]{1,0:T(8,128)S(1)} %get-tuple-element.42), channel_id=1, source_target_pairs={{0,20},{4,16},{8,28},{12,24},{16,4},{20,0},{24,12},{28,8},{1,21},{... | collective-permute-start | bytes 393224 | tf_op jit(solution)/shard_map/ppermute | solution.py:382
  34.8 5.0 %collective-permute-start.6 = (f32[8,256]{1,0:T(8,128)S(1)}, f32[8,256]{1,0:T(8,128)S(1)}, u32[]{:S(2)}, u32[]{:S(2)}) collective-permute-start(f32[8,256]{1,0:T(8,128)S(1)} %stack.1.refs_0_), channel_id=1, source_target_pairs={{0,3},{1,0},{2,1},{3,2},{4,7},{5,4},{6,5},{7,6},{8,11},{9,8},{10,9... | collective-permute-start | bytes 24584 | tf_op jit(solution)/shard_map/ppermute | solution.py:393
  39.8 4.5 %collective-permute-start.5 = (f32[8,256]{1,0:T(8,128)S(1)}, f32[8,256]{1,0:T(8,128)S(1)}, u32[]{:S(2)}, u32[]{:S(2)}) collective-permute-start(f32[8,256]{1,0:T(8,128)S(1)} %stack.1.refs_0_), channel_id=1, source_target_pairs={{0,2},{1,3},{2,0},{3,1},{4,6},{5,7},{6,4},{7,5},{8,10},{9,11},{10,... | collective-permute-start | bytes 24584 | tf_op jit(solution)/shard_map/ppermute | solution.py:393
  44.4 5.7 %collective-permute-start.4 = (f32[8,256]{1,0:T(8,128)S(1)}, f32[8,256]{1,0:T(8,128)S(1)}, u32[]{:S(2)}, u32[]{:S(2)}) collective-permute-start(f32[8,256]{1,0:T(8,128)S(1)} %stack.1.refs_0_), channel_id=1, source_target_pairs={{0,1},{1,2},{2,3},{3,0},{4,5},{5,6},{6,7},{7,4},{8,9},{9,10},{10,1... | collective-permute-start | bytes 24584 | tf_op jit(solution)/shard_map/ppermute | solution.py:393

commit v4 on v3

--- a/solution.py
+++ b/solution.py
@@ -75,9 +75,9 @@
     ]
 
 
-def first_kernel(groups, rows, tiles, parts, mask_ref, coef_ref, *refs):
+def first_kernel(groups, rows, tiles, parts, mask_ref, assign_ref, coef_ref, *refs):
     outs = refs[: len(parts)]
-    window, squares, order, live, sems, mask_sem = refs[len(parts) :]
+    window, squares, key_ref, order, slots, live, masks, sems, mask_sems = refs[len(parts) :]
     me = lax.axis_index("scen")
     cells = cells_of(parts, outs, tiles)
     ahead = [t for t, _, _ in cells]
@@ -96,23 +96,21 @@
         landed = window.at[pl.ds(start, end - start), pl.ds(0, rows)]
         pltpu.make_async_copy(landed, landed, sems.at[run]).wait()
 
-    mask_copy = pltpu.make_async_copy(mask_ref.at[pl.ds(me * rows, rows)], live, mask_sem)
+    small = [
+        pltpu.make_async_copy(mask_ref.at[pl.ds(me * rows, rows)], live, mask_sems.at[0]),
+        pltpu.make_async_copy(mask_ref, masks, mask_sems.at[1]),
+        pltpu.make_async_copy(assign_ref, slots, mask_sems.at[2]),
+    ]
 
     def begin(i, carry):
-        mask_copy.start()
+        for one in small:
+            one.start()
         return carry
 
     ahead_of_all(begin)
     for run, (start, end) in enumerate(runs):
         for t in range(start, end):
             copy(run, t).start()
-
-    def note(i, n):
-        marks = [live[i * SUBLANES + j] for j in range(SUBLANES)]
-        for j in range(SUBLANES):
-            order[n] = i * SUBLANES + j
-            n = n + marks[j]
-        return n
 
     def gather(i, carry):
         first = pl.multiple_of(i * SUBLANES, SUBLANES)
@@ -121,12 +119,30 @@
         squares[pl.ds(first, SUBLANES), :] = pack(first, picks, window, cells, total)
         return carry
 
-    mask_copy.wait()
-    lax.fori_loop(0, rows // SUBLANES, note, jnp.int32(0), unroll=4)
+    before = lax.broadcasted_iota(jnp.int32, (rows, rows), 0) < lax.broadcasted_iota(
+        jnp.int32, (rows, rows), 1
+    )
+    before = before.astype(jnp.float32).astype(jnp.bfloat16)
+    small[1].wait()
+    small[0].wait()
+    starts = [pl.multiple_of(jnp.bitwise_xor(me, k) * rows, rows) for k in range(groups)]
+    lines = [masks[pl.ds(start, rows)].reshape(1, rows) for start in starts]
+    marks = jnp.concatenate(lines, axis=0)
+    rank = jnp.dot(
+        marks.astype(jnp.float32).astype(jnp.bfloat16),
+        before,
+        preferred_element_type=jnp.float32,
+    )
+    n = jnp.int32(0)
+    for r in range(rows):
+        order[n] = r
+        n = n + live[r]
+    key_ref[...] = jnp.where(marks > 0, rank, -1.0).T
     wait(0)
     lax.fori_loop(0, ACT_DEV // SUBLANES, gather, 0, unroll=2)
     wait(1)
     wait(2)
+    small[2].wait()
 
 
 def second_kernel(tiles, parts, window, before, order, *refs):
@@ -142,14 +158,15 @@
         return carry
 
     lax.fori_loop(0, ACT_DEV // SUBLANES, gather, 0)
-    part_ref[...] = lax.dot_general(
+    total = lax.dot_general(
         jnp.ones((SUBLANES, LANES), jnp.float32), squares[...],
         (((1,), (1,)), ((), ())),
         precision=lax.Precision.HIGHEST, preferred_element_type=jnp.float32,
     )
-
-
-def pick(mask, coef, groups, rows, tiles):
+    part_ref[...] = total[:1]
+
+
+def pick(mask, assign, coef, groups, rows, tiles):
     parts = pieces(groups, tiles)
     ahead = [part for part in parts if part[0] == evens(groups)[-1]]
     behind = [part for part in parts if part not in ahead]
@@ -163,22 +180,25 @@
 
     squares = pltpu.VMEM((ACT_DEV, LANES), jnp.float32)
     window = pltpu.VMEM((groups * tiles, rows + SUBLANES, LANES), jnp.float32)
-    *one, window, before, order = pl.pallas_call(
+    key = pltpu.VMEM((rows, groups), jnp.float32)
+    listed = [pltpu.SMEM((rows,), jnp.int32), pltpu.SMEM(assign.shape, jnp.int32)]
+    *one, window, before, key, order, slots = pl.pallas_call(
         functools.partial(first_kernel, groups, rows, tiles, ahead),
-        out_shape=blocks(ahead) + [window, squares, pltpu.SMEM((rows,), jnp.int32)],
-        in_specs=[HBM, HBM],
-        out_specs=[VMEM] * (len(ahead) + 2) + [SMEM],
+        out_shape=blocks(ahead) + [window, squares, key] + listed,
+        in_specs=[HBM, HBM, HBM],
+        out_specs=[VMEM] * (len(ahead) + 3) + [SMEM, SMEM],
         scratch_shapes=[
             pltpu.SMEM((rows,), jnp.int32),
+            pltpu.VMEM(mask.shape, jnp.int32),
             pltpu.SemaphoreType.DMA((3,)),
-            pltpu.SemaphoreType.DMA,
+            pltpu.SemaphoreType.DMA((3,)),
         ],
         name="first",
         compiler_params=PARAMS,
-    )(*in_hbm(mask, coef))
+    )(*in_hbm(mask, assign, coef))
     *two, part = pl.pallas_call(
         functools.partial(second_kernel, tiles, behind),
-        out_shape=blocks(behind) + [pltpu.VMEM((SUBLANES, ACT_DEV), jnp.float32)],
+        out_shape=blocks(behind) + [pltpu.VMEM((1, ACT_DEV), jnp.float32)],
         in_specs=[VMEM, VMEM, SMEM],
         out_specs=[VMEM] * (len(behind) + 1),
         scratch_shapes=[squares],
@@ -186,7 +206,7 @@
         compiler_params=PARAMS,
     )(*on_chip(window, before), scalars(order))
     found = zip(ahead + behind, one + two)
-    return {(k, h0): block for (k, h0, _), block in found}, part
+    return {(k, h0): block for (k, h0, _), block in found}, part, key, slots
 
 
 def join_kernel(block_ref, *refs):
@@ -223,40 +243,6 @@
     )(*on_chip(*values))
 
 
-def spread_kernel(groups, rows, mask_ref, assign_ref, place_ref, slots_ref, sem):
-    copy = pltpu.make_async_copy(assign_ref, slots_ref, sem)
-    copy.start()
-    lines = [mask_ref[pl.ds(s * rows, rows)].reshape(1, rows) for s in range(groups)]
-    live = jnp.concatenate(lines, axis=0)
-    before = lax.broadcasted_iota(jnp.int32, (rows, rows), 0) < lax.broadcasted_iota(
-        jnp.int32, (rows, rows), 1
-    )
-    rank = jnp.dot(
-        live.astype(jnp.float32).astype(jnp.bfloat16),
-        before.astype(jnp.float32).astype(jnp.bfloat16),
-        preferred_element_type=jnp.float32,
-    )
-    key = jnp.where(live > 0, rank, -1.0).T
-    packed = lax.broadcasted_iota(jnp.int32, (rows, ACT_DEV), 1).astype(jnp.float32)
-    for s in range(groups):
-        hit = key[:, s : s + 1] == packed
-        place_ref[s] = jnp.where(hit, 1.0, 0.0).astype(jnp.bfloat16)
-    copy.wait()
-
-
-def spread(mask, assign, groups, rows):
-    place = pltpu.VMEM((groups, rows, ACT_DEV), jnp.bfloat16)
-    return pl.pallas_call(
-        functools.partial(spread_kernel, groups, rows),
-        out_shape=[place, pltpu.SMEM(assign.shape, jnp.int32)],
-        in_specs=[VMEM, HBM],
-        out_specs=[VMEM, SMEM],
-        scratch_shapes=[pltpu.SemaphoreType.DMA],
-        name="spread",
-        compiler_params=PARAMS,
-    )(*on_chip(mask), *in_hbm(assign))
-
-
 def inverse_norms(totals):
     total = totals[0][...]
     for other in totals[1:]:
@@ -264,12 +250,17 @@
     return (1.0 / jnp.sqrt(total / NV + EPS)).T
 
 
-def place_rows(k, scale, got_ref, place_ref, assign_ref, flats):
+def matrix(key_ref, k):
+    packed = lax.broadcasted_iota(jnp.int32, (key_ref.shape[0], ACT_DEV), 1)
+    hit = key_ref[:, k : k + 1] == packed.astype(jnp.float32)
+    return jnp.where(hit, 1.0, 0.0).astype(jnp.bfloat16)
+
+
+def place_rows(k, scale, got_ref, place, assign_ref, flats):
     source = jnp.bitwise_xor(lax.axis_index("scen"), k)
     value = got_ref[:ACT_DEV, :] * scale
     high = value.astype(jnp.bfloat16)
     low = (value - high.astype(jnp.float32)).astype(jnp.bfloat16)
-    place = place_ref[source]
     both = jnp.concatenate([high, low], axis=1)
     wide = jnp.dot(place, both, preferred_element_type=jnp.float32)
     wide = wide[:, : high.shape[1]] + wide[:, high.shape[1] :]
@@ -284,17 +275,21 @@
     return jnp.sum((value * value).reshape(ACT_DEV // SUBLANES, SUBLANES, -1), axis=0)
 
 
-def early_kernel(lines, rest, assign_ref, place_ref, *refs):
+def early_kernel(lines, rest, assign_ref, key_ref, *refs):
     n = len(lines)
     totals, got = refs[:4], refs[4 : 4 + n]
     outs = refs[4 + n :]
-    flats, (squares_a, squares_b), scales = outs[:2], outs[2:4], outs[4:]
+    flats, (squares_a, squares_b) = outs[:2], outs[2:4]
     scale = inverse_norms(totals)
-    for line, ref in zip(rest, scales):
-        ref[...] = jnp.broadcast_to(scale[:, line : line + 1], ref.shape)
+    for n, (k, line) in enumerate(rest):
+        scale_ref, place_ref = outs[4 + 2 * n : 6 + 2 * n]
+        scale_ref[...] = jnp.broadcast_to(scale[:, line : line + 1], scale_ref.shape)
+        place_ref[...] = matrix(key_ref, k)
     squares = None
     for (k, line), got_ref in zip(lines, got):
-        one = place_rows(k, scale[:, line : line + 1], got_ref, place_ref, assign_ref, flats)
+        one = place_rows(
+            k, scale[:, line : line + 1], got_ref, matrix(key_ref, k), assign_ref, flats
+        )
         squares = one if squares is None else squares + one
     half = squares_a.shape[1]
     squares_a[...] = squares[:, :half]
@@ -314,14 +309,30 @@
     )
 
 
-def late_kernel(last, active_total, half, assign_ref, place_ref, *refs):
+def late_kernel(last, active_total, half, assign_ref, *refs):
     n = len(last)
-    scales, got, (flat, squares_ref) = refs[:n], refs[n : 2 * n], refs[2 * n : 2 * n + 2]
-    out_ref, out_v, sem = refs[-3:]
+    scales, places, got = refs[: 2 * n : 2], refs[1 : 2 * n : 2], refs[2 * n : 3 * n]
+    flat, squares_ref = refs[3 * n : 3 * n + 2]
     cuts, width = flat.shape
+    early = pl.ds(0, cuts // 2)
+    late = pl.ds(cuts // 2, cuts // 2)
+    own = pl.ds(half * width, width)
+    if half:
+        other_ref, _, out_ref, out_v, sems = refs[3 * n + 2 :]
+        rest = pltpu.make_async_copy(
+            other_ref.at[:, late], out_ref.at[0, pl.ds(0, width), late], sems.at[1]
+        )
+
+        def begin(i, carry):
+            rest.start()
+            return carry
+
+        ahead_of_all(begin)
+    else:
+        out_ref, out_v, sems = refs[3 * n + 2 :]
     squares = squares_ref[...]
-    for k, scale, got_ref in zip(last, scales, got):
-        squares = squares + place_rows(k, scale[...], got_ref, place_ref, assign_ref, [flat])
+    for k, scale, place, got_ref in zip(last, scales, places, got):
+        squares = squares + place_rows(k, scale[...], got_ref, place[...], assign_ref, [flat])
     column = jnp.sum(squares, axis=0, keepdims=True)
     inverse = 1.0 / jnp.sqrt(column / active_total + EPS)
     step = 4 * LANES
@@ -329,46 +340,52 @@
         span = pl.ds(c * step, step)
         value = flat[span, :] * inverse
         out_v[:, span] = value.T if half or c % 2 == 0 else turned_by_matmul(value)
-        target = out_ref.at[0, pl.ds(half * width, width), span]
-        pltpu.make_async_copy(out_v.at[:, span], target, sem).start()
-    pltpu.make_async_copy(out_v, out_ref.at[0, pl.ds(half * width, width)], sem).wait()
-
-
-def finish(received, lines_of, totals, place, assign, groups, rows, slice_width):
+        if half or (c + 1) * step <= cuts // 2:
+            target = out_ref.at[0, own, span]
+            pltpu.make_async_copy(out_v.at[:, span], target, sems.at[0]).start()
+    if half:
+        rest.wait()
+        pltpu.make_async_copy(out_v, out_ref.at[0, own], sems.at[0]).wait()
+    else:
+        pltpu.make_async_copy(out_v.at[:, early], out_ref.at[0, own, early], sems.at[0]).wait()
+
+
+def finish(received, lines_of, totals, key, assign, groups, rows, slice_width):
     cuts = groups * rows
     half = slice_width // 2
     last = halved(groups)
     early = [k for k in range(groups) if k not in last]
     assign = scalars(assign)
-    (place,) = on_chip(place)
     flat = pltpu.VMEM((cuts, half), jnp.float32)
     squares = pltpu.VMEM((SUBLANES, half), jnp.float32)
-    scale = pltpu.VMEM((ACT_DEV, half), jnp.float32)
-    flat_a, flat_b, squares_a, squares_b, *scales = pl.pallas_call(
+    tables = [pltpu.VMEM((ACT_DEV, half), jnp.float32), pltpu.VMEM((rows, ACT_DEV), jnp.bfloat16)]
+    flat_a, flat_b, squares_a, squares_b, *tables = pl.pallas_call(
         functools.partial(
-            early_kernel, [(k, lines_of[k]) for k in early], [lines_of[k] for k in last]
+            early_kernel, [(k, lines_of[k]) for k in early], [(k, lines_of[k]) for k in last]
         ),
-        out_shape=[flat, flat, squares, squares] + [scale] * len(last),
+        out_shape=[flat, flat, squares, squares] + tables * len(last),
         in_specs=[SMEM] + [VMEM] * (1 + len(totals) + len(early)),
-        out_specs=[VMEM] * (4 + len(last)),
+        out_specs=[VMEM] * (4 + 2 * len(last)),
         name="early",
         compiler_params=PARAMS,
-    )(assign, place, *on_chip(*totals, *[received[k, 0] for k in early]))
-
-    def late(n, flat, squares, *other):
+    )(assign, *on_chip(key, *totals, *[received[k, 0] for k in early]))
+
+    def late(n, flat, squares, *others):
         got = [received[k, n * half // LANES] for k in last]
-        values = on_chip(*scales, *got, flat, squares) + in_hbm(*other)
+        values = on_chip(*tables, *got, flat, squares, *others[n:]) + in_hbm(*others[:n])
+        whole = jax.ShapeDtypeStruct((1, slice_width, cuts), jnp.float32)
+        turned = pltpu.VMEM((half, cuts), jnp.float32)
         return pl.pallas_call(
             functools.partial(late_kernel, last, ACT_DEV * groups, n),
-            out_shape=jax.ShapeDtypeStruct((1, slice_width, cuts), jnp.float32),
-            in_specs=[SMEM] + [VMEM] * (1 + len(values) - n) + [HBM] * n,
-            out_specs=HBM,
-            scratch_shapes=[pltpu.VMEM((half, cuts), jnp.float32), pltpu.SemaphoreType.DMA],
-            input_output_aliases={len(values) + 1: 0} if n else {},
+            out_shape=whole if n else [whole, turned],
+            in_specs=[SMEM] + [VMEM] * (len(values) - n) + [HBM] * n,
+            out_specs=HBM if n else [HBM, VMEM],
+            scratch_shapes=[turned] * n + [pltpu.SemaphoreType.DMA((2,))],
+            input_output_aliases={len(values): 0} if n else {},
             compiler_params=PARAMS,
-        )(assign, place, *values)
-
-    return late(1, flat_b, squares_b, late(0, flat_a, squares_a))
+        )(assign, *values)
+
+    return late(1, flat_b, squares_b, *late(0, flat_a, squares_a))
 
 
 def exchange(coef, mask, assign):
@@ -381,7 +398,7 @@
     def swap(value, k):
         return lax.ppermute(value, "scen", [(i, i ^ k) for i in range(groups)])
 
-    blocks, part = pick(mask, coef, groups, rows, tiles)
+    blocks, part, key, slots = pick(mask, assign, coef, groups, rows, tiles)
     near = evens(groups)
     parts = [part] + [swap(part, k) for k in near[1:]]
     blocks[1, 0] = join(blocks[1, 0], *parts)
@@ -393,8 +410,7 @@
         return lax.ppermute(lines, "col", [(i, (i + z) % columns) for i in range(columns)])
 
     totals = [lines] + [turn(z) for z in range(1, columns)]
-    place, assign = spread(mask, assign, groups, rows)
-    return finish(received, lines_of, totals, place, assign, groups, rows, slice_width)
+    return finish(received, lines_of, totals, key, slots, groups, rows, slice_width)
 
 
 def fallback(coef, mask, assign):

time: 55.5 us -> 52.9 us (0.953)
  starting transfers between devices: 19.8 us -> 17.2 us
  waiting for transfers between devices: 25.5 us -> 26.5 us
  Pallas kernels: 9.92 us -> 8.99 us
    ppermute x12, starting transfers between devices: 13.2 us -> 10.6 us  [swap(): return lax.ppermute(value, 'scen', [(i, i ^ k) for i in range(groups)])]
    ppermute x3, waiting for transfers between devices: 7.63 us -> 8.63 us  [turn(): lax.ppermute(lines, 'col', [(i, (i + z) % columns) for i in range(columns)])]
    pallas_call x1 -> x0, Pallas kernels: 0.99 us -> none  [spread(): pl.pallas_call(functools.partial(spread_kernel, groups, rows), out_shape=...]
  transfers between devices with their start and end apart: 15 -> 15, of which waited for: 8 -> 9; matrix products, arithmetic and copies ran while one was open for 0% -> 0% of each run, Pallas kernels for 8% -> 6%
where the time goes in v4:
time: 52.9 us; the launch traced here: 52.8 us
  waiting for transfers between devices  26.5 us (50%)
  starting transfers between devices  17.2 us (33%)
  Pallas kernels  8.99 us (17%)
    ppermute x12, waiting for transfers between devices, swap(): return lax.ppermute(value, 'scen', [(i, i ^ k) for i in range(groups)])  17.9 us
    ppermute x12, starting transfers between devices, swap(): return lax.ppermute(value, 'scen', [(i, i ^ k) for i in range(groups)])  10.6 us
    ppermute x3, waiting for transfers between devices, turn(): lax.ppermute(lines, 'col', [(i, (i + z) % columns) for i in range(columns)])  8.63 us
    ppermute x3, starting transfers between devices, turn(): lax.ppermute(lines, 'col', [(i, (i + z) % columns) for i in range(columns)])  6.6 us
    pallas_call x2, Pallas kernels, late(): pl.pallas_call(functools.partial(late_kernel, last, ACT_DEV * groups, n),...  3.36 us
    pallas_call x1, Pallas kernels, pick(): pl.pallas_call(functools.partial(first_kernel, groups, rows, tiles, ahead...  2.27 us
    pallas_call x1, Pallas kernels, finish(): pl.pallas_call(functools.partial(early_kernel, [(k, lines_of[k]) for k in...  1.87 us
    pallas_call x1, Pallas kernels, pick(): pl.pallas_call(functools.partial(second_kernel, tiles, behind), out_shape...  1.49 us
  transfers between devices with their start and end apart: 15, of which 9 were waited for; matrix products, arithmetic and copies ran while one was open for 0% of the time, Pallas kernels for 6%

profile of v4, /device:TPU:0, one launch (start us, length us, event | category | flops | bytes accessed | tf_op | source)
XLA Modules:
  0.0 52.8 jit_solution(4578089372842370085)
XLA Ops:
  0.0 2.3 %first.1 = (f32[256,256]{1,0:T(8,128)S(1)}, f32[16,520,128]{2,1,0:T(8,128)S(1)}, f32[256,128]{1,0:T(8,128)S(1)}, f32[512,8]{1,0:T(8,128)S(1)}, s32[512]{0:T(512)S(4)}, /*index=5*/s32[512]{0:T(512)S(4)}) custom-call(s32[4096]{0:T(1024)} %mask_ref.1, s32[512]{0:T(512)} %assign_ref.1, f32[512,2048]{1,0:T(8,128)} %coef_ref.1), custom_call_target="tpu_custom_call" | custom-call | tf_op jit(solution)/shard_map/first/pallas_call | solution.py:185
  2.3 1.5 %second.1 = (f32[256,256]{1,0:T(8,128)S(1)}, f32[264,256]{1,0:T(8,128)S(1)}, f32[256,256]{1,0:T(8,128)S(1)}, f32[256,256]{1,0:T(8,128)S(1)}, f32[256,256]{1,0:T(...) custom-call(f32[16,520,128]{2,1,0:T(8,128)S(1)} %get-tuple-element.3, ...), custom_call_target="tpu_custom_call" | custom-call | tf_op jit(solution)/shard_map/second/pallas_call | solution.py:199
  3.8 3.9 %collective-permute-start.2 = (f32[1,256]{1,0:T(1,128)S(1)}, f32[1,256]{1,0:T(1,128)S(1)}, u32[]{:S(2)}, u32[]{:S(2)}) collective-permute-start(f32[1,256]{1,0:T(1,128)S(1)} %get-tuple-element.37.refs_0_), channel_id=1, source_target_pairs={{0,24},{4,28},{8,16},{12,20},{16,8},{20,12},{24,0},{28,4},{1,25},{... | collective-permute-start | bytes 3080 | tf_op jit(solution)/shard_map/ppermute | solution.py:399
  7.7 0.5 collective-permute-start.1
  8.2 0.1 collective-permute-start
  8.3 1.0 %collective-permute-done.2.refs_3_ = f32[1,256]{1,0:T(1,128)S(1)} collective-permute-done((f32[1,256]{1,0:T(1,128)S(1)}, f32[1,256]{1,0:T(1,128)S(1)}, u32[]{:S(2)}, u32[]{:S(2)}) %collective-permute-start.2) | collective-permute-done | bytes 1056 | tf_op jit(solution)/shard_map/ppermute | solution.py:399
  9.3 2.0 %collective-permute-done.1.refs_2_ = f32[1,256]{1,0:T(1,128)S(1)} collective-permute-done((f32[1,256]{1,0:T(1,128)S(1)}, f32[1,256]{1,0:T(1,128)S(1)}, u32[]{:S(2)}, u32[]{:S(2)}) %collective-permute-start.1) | collective-permute-done | bytes 1056 | tf_op jit(solution)/shard_map/ppermute | solution.py:399
  11.3 0.5 collective-permute-done.refs_1_
  11.8 0.0 collective-permute-start.3
  11.8 1.6 %collective-permute-start.9 = (f32[256,256]{1,0:T(8,128)S(1)}, f32[256,256]{1,0:T(8,128)S(1)}, u32[]{:S(2)}, u32[]{:S(2)}) collective-permute-start(f32[256,256]{1,0:T(8,128)S(1)} %get-tuple-element.41), channel_id=1, source_target_pairs={{0,24},{4,28},{8,16},{12,20},{16,8},{20,12},{24,0},{28,4},{1,25},{... | collective-permute-start | bytes 786440 | tf_op jit(solution)/shard_map/ppermute | solution.py:399
  13.4 1.5 %collective-permute-start.7 = (f32[256,256]{1,0:T(8,128)S(1)}, f32[256,256]{1,0:T(8,128)S(1)}, u32[]{:S(2)}, u32[]{:S(2)}) collective-permute-start(f32[256,256]{1,0:T(8,128)S(1)} %get-tuple-element.39), channel_id=1, source_target_pairs={{0,8},{4,12},{8,0},{12,4},{16,24},{20,28},{24,16},{28,20},{1,9},{5... | collective-permute-start | bytes 786440 | tf_op jit(solution)/shard_map/ppermute | solution.py:399
  14.8 0.5 collective-permute-start.8
  15.3 0.7 %collective-permute-start.10 = (f32[256,256]{1,0:T(8,128)S(1)}, f32[256,256]{1,0:T(8,128)S(1)}, u32[]{:S(2)}, u32[]{:S(2)}) collective-permute-start(f32[256,256]{1,0:T(8,128)S(1)} %get-tuple-element.42), channel_id=1, source_target_pairs={{0,28},{4,24},{8,20},{12,16},{16,12},{20,8},{24,4},{28,0},{1,29},{... | collective-permute-start | bytes 786440 | tf_op jit(solution)/shard_map/ppermute | solution.py:399
  16.1 5.9 %collective-permute-done.9.refs_8_ = f32[256,256]{1,0:T(8,128)S(1)} collective-permute-done((f32[256,256]{1,0:T(8,128)S(1)}, f32[256,256]{1,0:T(8,128)S(1)}, u32[]{:S(2)}, u32[]{:S(2)}) %collective-permute-start.9) | collective-permute-done | bytes 262176 | tf_op jit(solution)/shard_map/ppermute | solution.py:399
  22.0 0.0 collective-permute-start.13
  22.0 5.7 %collective-permute-done.7.refs_6_ = f32[256,256]{1,0:T(8,128)S(1)} collective-permute-done((f32[256,256]{1,0:T(8,128)S(1)}, f32[256,256]{1,0:T(8,128)S(1)}, u32[]{:S(2)}, u32[]{:S(2)}) %collective-permute-start.7) | collective-permute-done | bytes 262176 | tf_op jit(solution)/shard_map/ppermute | solution.py:399
  27.7 0.0 collective-permute-start.14
  27.7 0.0 collective-permute-done.8.refs_7_
  27.7 0.3 collective-permute-start.11
  28.0 0.0 collective-permute-done.3.refs_1_.refs_5_
  28.0 1.5 %collective-permute-start.12 = (f32[256,128]{1,0:T(8,128)S(1)}, f32[256,128]{1,0:T(8,128)S(1)}, u32[]{:S(2)}, u32[]{:S(2)}) collective-permute-start(f32[256,128]{1,0:T(8,128)S(1)} %get-tuple-element.48), channel_id=1, source_target_pairs={{0,20},{4,16},{8,28},{12,24},{16,4},{20,0},{24,12},{28,8},{1,21},{... | collective-permute-start | bytes 393224 | tf_op jit(solution)/shard_map/ppermute | solution.py:399
  29.5 2.8 %collective-permute-done.10.refs_9_ = f32[256,256]{1,0:T(8,128)S(1)} collective-permute-done((f32[256,256]{1,0:T(8,128)S(1)}, f32[256,256]{1,0:T(8,128)S(1)}, u32[]{:S(2)}, u32[]{:S(2)}) %collective-permute-start.10) | collective-permute-done | bytes 262176 | tf_op jit(solution)/shard_map/ppermute | solution.py:399
  32.3 3.6 %collective-permute-start.6 = (f32[8,256]{1,0:T(8,128)S(1)}, f32[8,256]{1,0:T(8,128)S(1)}, u32[]{:S(2)}, u32[]{:S(2)}) collective-permute-start(f32[8,256]{1,0:T(8,128)S(1)} %stack.1.refs_0_), channel_id=1, source_target_pairs={{0,3},{1,0},{2,1},{3,2},{4,7},{5,4},{6,5},{7,6},{8,11},{9,8},{10,9... | collective-permute-start | bytes 24584 | tf_op jit(solution)/shard_map/ppermute | solution.py:410
  35.9 1.4 %collective-permute-done.6.refs_3_ = f32[8,256]{1,0:T(8,128)S(1)} collective-permute-done((f32[8,256]{1,0:T(8,128)S(1)}, f32[8,256]{1,0:T(8,128)S(1)}, u32[]{:S(2)}, u32[]{:S(2)}) %collective-permute-start.6) | collective-permute-done | bytes 8224 | tf_op jit(solution)/shard_map/ppermute | solution.py:410
  37.2 1.3 %collective-permute-start.5 = (f32[8,256]{1,0:T(8,128)S(1)}, f32[8,256]{1,0:T(8,128)S(1)}, u32[]{:S(2)}, u32[]{:S(2)}) collective-permute-start(f32[8,256]{1,0:T(8,128)S(1)} %stack.1.refs_0_), channel_id=1, source_target_pairs={{0,2},{1,3},{2,0},{3,1},{4,6},{5,7},{6,4},{7,5},{8,10},{9,11},{10,... | collective-permute-start | bytes 24584 | tf_op jit(solution)/shard_map/ppermute | solution.py:410
  38.5 3.3 %collective-permute-done.5.refs_2_ = f32[8,256]{1,0:T(8,128)S(1)} collective-permute-done((f32[8,256]{1,0:T(8,128)S(1)}, f32[8,256]{1,0:T(8,128)S(1)}, u32[]{:S(2)}, u32[]{:S(2)}) %collective-permute-start.5) | collective-permute-done | bytes 8224 | tf_op jit(solution)/shard_map/ppermute | solution.py:410
  41.8 1.7 %collective-permute-start.4 = (f32[8,256]{1,0:T(8,128)S(1)}, f32[8,256]{1,0:T(8,128)S(1)}, u32[]{:S(2)}, u32[]{:S(2)}) collective-permute-start(f32[8,256]{1,0:T(8,128)S(1)} %stack.1.refs_0_), channel_id=1, source_target_pairs={{0,1},{1,2},{2,3},{3,0},{4,5},{5,6},{6,7},{7,4},{8,9},{9,10},{10,1... | collective-permute-start | bytes 24584 | tf_op jit(solution)/shard_map/ppermute | solution.py:410
  43.5 4.0 %collective-permute-done.4.refs_1_ = f32[8,256]{1,0:T(8,128)S(1)} collective-permute-done((f32[8,256]{1,0:T(8,128)S(1)}, f32[8,256]{1,0:T(8,128)S(1)}, u32[]{:S(2)}, u32[]{:S(2)}) %collective-permute-start.4) | collective-permute-done | bytes 8224 | tf_op jit(solution)/shard_map/ppermute | solution.py:410
  47.5 1.9 %early.1 = (f32[4096,128]{1,0:T(8,128)S(1)}, f32[4096,128]{1,0:T(8,128)S(1)}, f32[8,128]{1,0:T(8,128)S(1)}, f32[8,128]{1,0:T(8,128)S(1)}, f32[256,128]{1,0:T(8,1...) custom-call(s32[512]{0:T(512)S(4)} %get-tuple-element.31.assign_ref, ...), custom_call_target="tpu_custom_call" | custom-call | tf_op jit(solution)/shard_map/early/pallas_call | solution.py:362
  49.4 0.0 collective-permute-done.13.refs_4_
  49.4 0.0 collective-permute-done.14.refs_5_
  49.4 1.5 %shard_map.37 = (f32[1,256,4096]{2,1,0:T(8,128)}, f32[128,4096]{1,0:T(8,128)S(1)}) custom-call(s32[512]{0:T(512)S(4)} %get-tuple-element.31.assign_ref, f32[256,128]{1,0:T(8,128)S(1)} %get-tuple-element.43.refs_0_, bf16[512,256]{1,0:T(8,128)(2,1)S(1)} %get-tuple-element.44.refs_1_, f32[256,128]{1,0:T(8,128)S(1)} %get-tuple-element.45.refs_2_, ...), custom_call_target="tpu_custom_call" | custom-call | tf_op jit(solution)/shard_map/pallas_call | solution.py:378
  50.9 0.0 collective-permute-done.11.refs_4_
  50.9 0.0 collective-permute-done.12.refs_5_
  50.9 1.8 %shard_map.38 = f32[1,256,4096]{2,1,0:T(8,128)} custom-call(s32[512]{0:T(512)S(4)} %get-tuple-element.31.assign_ref, f32[256,128]{1,0:T(8,128)S(1)} %get-tuple-element.43.refs_0_, bf16[512,256]{1,0:T(8,128)(2,1)S(1)} %get-tuple-element.44.refs_1_, f32[256,128]{1,0:T(8,128)S(1)} %get-tuple-element.45.refs_2_, ...), custom_call_target="tpu_custom_call", output_to_operand_aliasing={{}: (10, {})} | custom-call | tf_op jit(solution)/shard_map/pallas_call | solution.py:378
  (2 shorter events, 0.0 us)
Async XLA Ops:
  3.8 5.5 %collective-permute-start.2 = (f32[1,256]{1,0:T(1,128)S(1)}, f32[1,256]{1,0:T(1,128)S(1)}, u32[]{:S(2)}, u32[]{:S(2)}) collective-permute-start(f32[1,256]{1,0:T(1,128)S(1)} %get-tuple-element.37.refs_0_), channel_id=1, source_target_pairs={{0,24},{4,28},{8,16},{12,20},{16,8},{20,12},{24,0},{28,4},{1,25},{... | collective-permute-start | bytes 3080 | tf_op jit(solution)/shard_map/ppermute | solution.py:399
  7.7 3.6 %collective-permute-start.1 = (f32[1,256]{1,0:T(1,128)S(1)}, f32[1,256]{1,0:T(1,128)S(1)}, u32[]{:S(2)}, u32[]{:S(2)}) collective-permute-start(f32[1,256]{1,0:T(1,128)S(1)} %get-tuple-element.37.refs_0_), channel_id=1, source_target_pairs={{0,16},{4,20},{8,24},{12,28},{16,0},{20,4},{24,8},{28,12},{1,17},{... | collective-permute-start | bytes 3080 | tf_op jit(solution)/shard_map/ppermute | solution.py:399
  8.2 3.6 %collective-permute-start = (f32[1,256]{1,0:T(1,128)S(1)}, f32[1,256]{1,0:T(1,128)S(1)}, u32[]{:S(2)}, u32[]{:S(2)}) collective-permute-start(f32[1,256]{1,0:T(1,128)S(1)} %get-tuple-element.37.refs_0_), channel_id=1, source_target_pairs={{0,8},{4,12},{8,0},{12,4},{16,24},{20,28},{24,16},{28,20},{1,9},{5... | collective-permute-start | bytes 3080 | tf_op jit(solution)/shard_map/ppermute | solution.py:399
  11.8 16.2 %collective-permute-start.3 = (f32[264,256]{1,0:T(8,128)S(1)}, f32[264,256]{1,0:T(8,128)S(1)}, u32[]{:S(2)}, u32[]{:S(2)}) collective-permute-start(f32[264,256]{1,0:T(8,128)S(1)} %join.1.refs_0_), channel_id=1, source_target_pairs={{0,4},{4,0},{8,12},{12,8},{16,20},{20,16},{24,28},{28,24},{1,5},{5... | collective-permute-start | bytes 811016 | tf_op jit(solution)/shard_map/ppermute | solution.py:399
  11.8 10.2 %collective-permute-start.9 = (f32[256,256]{1,0:T(8,128)S(1)}, f32[256,256]{1,0:T(8,128)S(1)}, u32[]{:S(2)}, u32[]{:S(2)}) collective-permute-start(f32[256,256]{1,0:T(8,128)S(1)} %get-tuple-element.41), channel_id=1, source_target_pairs={{0,24},{4,28},{8,16},{12,20},{16,8},{20,12},{24,0},{28,4},{1,25},{... | collective-permute-start | bytes 786440 | tf_op jit(solution)/shard_map/ppermute | solution.py:399
  13.4 14.3 %collective-permute-start.7 = (f32[256,256]{1,0:T(8,128)S(1)}, f32[256,256]{1,0:T(8,128)S(1)}, u32[]{:S(2)}, u32[]{:S(2)}) collective-permute-start(f32[256,256]{1,0:T(8,128)S(1)} %get-tuple-element.39), channel_id=1, source_target_pairs={{0,8},{4,12},{8,0},{12,4},{16,24},{20,28},{24,16},{28,20},{1,9},{5... | collective-permute-start | bytes 786440 | tf_op jit(solution)/shard_map/ppermute | solution.py:399
  14.8 12.8 %collective-permute-start.8 = (f32[256,256]{1,0:T(8,128)S(1)}, f32[256,256]{1,0:T(8,128)S(1)}, u32[]{:S(2)}, u32[]{:S(2)}) collective-permute-start(f32[256,256]{1,0:T(8,128)S(1)} %get-tuple-element.40), channel_id=1, source_target_pairs={{0,16},{4,20},{8,24},{12,28},{16,0},{20,4},{24,8},{28,12},{1,17},{... | collective-permute-start | bytes 786440 | tf_op jit(solution)/shard_map/ppermute | solution.py:399
  15.3 16.9 %collective-permute-start.10 = (f32[256,256]{1,0:T(8,128)S(1)}, f32[256,256]{1,0:T(8,128)S(1)}, u32[]{:S(2)}, u32[]{:S(2)}) collective-permute-start(f32[256,256]{1,0:T(8,128)S(1)} %get-tuple-element.42), channel_id=1, source_target_pairs={{0,28},{4,24},{8,20},{12,16},{16,12},{20,8},{24,4},{28,0},{1,29},{... | collective-permute-start | bytes 786440 | tf_op jit(solution)/shard_map/ppermute | solution.py:399
  22.0 27.4 %collective-permute-start.13 = (f32[256,128]{1,0:T(8,128)S(1)}, f32[256,128]{1,0:T(8,128)S(1)}, u32[]{:S(2)}, u32[]{:S(2)}) collective-permute-start(f32[256,128]{1,0:T(8,128)S(1)} %get-tuple-element.51), channel_id=1, source_target_pairs={{0,12},{4,8},{8,4},{12,0},{16,28},{20,24},{24,20},{28,16},{1,13},{... | collective-permute-start | bytes 393224 | tf_op jit(solution)/shard_map/ppermute | solution.py:399
  27.7 21.7 %collective-permute-start.14 = (f32[256,128]{1,0:T(8,128)S(1)}, f32[256,128]{1,0:T(8,128)S(1)}, u32[]{:S(2)}, u32[]{:S(2)}) collective-permute-start(f32[256,128]{1,0:T(8,128)S(1)} %get-tuple-element.52), channel_id=1, source_target_pairs={{0,20},{4,16},{8,28},{12,24},{16,4},{20,0},{24,12},{28,8},{1,21},{... | collective-permute-start | bytes 393224 | tf_op jit(solution)/shard_map/ppermute | solution.py:399
  27.7 23.3 %collective-permute-start.11 = (f32[256,128]{1,0:T(8,128)S(1)}, f32[256,128]{1,0:T(8,128)S(1)}, u32[]{:S(2)}, u32[]{:S(2)}) collective-permute-start(f32[256,128]{1,0:T(8,128)S(1)} %get-tuple-element.47), channel_id=1, source_target_pairs={{0,12},{4,8},{8,4},{12,0},{16,28},{20,24},{24,20},{28,16},{1,13},{... | collective-permute-start | bytes 393224 | tf_op jit(solution)/shard_map/ppermute | solution.py:399
  28.0 22.9 %collective-permute-start.12 = (f32[256,128]{1,0:T(8,128)S(1)}, f32[256,128]{1,0:T(8,128)S(1)}, u32[]{:S(2)}, u32[]{:S(2)}) collective-permute-start(f32[256,128]{1,0:T(8,128)S(1)} %get-tuple-element.48), channel_id=1, source_target_pairs={{0,20},{4,16},{8,28},{12,24},{16,4},{20,0},{24,12},{28,8},{1,21},{... | collective-permute-start | bytes 393224 | tf_op jit(solution)/shard_map/ppermute | solution.py:399
  32.3 5.0 %collective-permute-start.6 = (f32[8,256]{1,0:T(8,128)S(1)}, f32[8,256]{1,0:T(8,128)S(1)}, u32[]{:S(2)}, u32[]{:S(2)}) collective-permute-start(f32[8,256]{1,0:T(8,128)S(1)} %stack.1.refs_0_), channel_id=1, source_target_pairs={{0,3},{1,0},{2,1},{3,2},{4,7},{5,4},{6,5},{7,6},{8,11},{9,8},{10,9... | collective-permute-start | bytes 24584 | tf_op jit(solution)/shard_map/ppermute | solution.py:410
  37.2 4.5 %collective-permute-start.5 = (f32[8,256]{1,0:T(8,128)S(1)}, f32[8,256]{1,0:T(8,128)S(1)}, u32[]{:S(2)}, u32[]{:S(2)}) collective-permute-start(f32[8,256]{1,0:T(8,128)S(1)} %stack.1.refs_0_), channel_id=1, source_target_pairs={{0,2},{1,3},{2,0},{3,1},{4,6},{5,7},{6,4},{7,5},{8,10},{9,11},{10,... | collective-permute-start | bytes 24584 | tf_op jit(solution)/shard_map/ppermute | solution.py:410
  41.8 5.7 %collective-permute-start.4 = (f32[8,256]{1,0:T(8,128)S(1)}, f32[8,256]{1,0:T(8,128)S(1)}, u32[]{:S(2)}, u32[]{:S(2)}) collective-permute-start(f32[8,256]{1,0:T(8,128)S(1)} %stack.1.refs_0_), channel_id=1, source_target_pairs={{0,1},{1,2},{2,3},{3,0},{4,5},{5,6},{6,7},{7,4},{8,9},{9,10},{10,1... | collective-permute-start | bytes 24584 | tf_op jit(solution)/shard_map/ppermute | solution.py:410

commit v5 on v4

--- a/solution.py
+++ b/solution.py
@@ -158,12 +158,7 @@
         return carry
 
     lax.fori_loop(0, ACT_DEV // SUBLANES, gather, 0)
-    total = lax.dot_general(
-        jnp.ones((SUBLANES, LANES), jnp.float32), squares[...],
-        (((1,), (1,)), ((), ())),
-        precision=lax.Precision.HIGHEST, preferred_element_type=jnp.float32,
-    )
-    part_ref[...] = total[:1]
+    part_ref[...] = jnp.sum(squares[...].T, axis=0, keepdims=True)
 
 
 def pick(mask, assign, coef, groups, rows, tiles):
@@ -275,10 +270,10 @@
     return jnp.sum((value * value).reshape(ACT_DEV // SUBLANES, SUBLANES, -1), axis=0)
 
 
-def early_kernel(lines, rest, assign_ref, key_ref, *refs):
+def early_kernel(lines, rest, columns, assign_ref, key_ref, *refs):
     n = len(lines)
-    totals, got = refs[:4], refs[4 : 4 + n]
-    outs = refs[4 + n :]
+    totals, got = refs[:columns], refs[columns : columns + n]
+    outs = refs[columns + n :]
     flats, (squares_a, squares_b) = outs[:2], outs[2:4]
     scale = inverse_norms(totals)
     for n, (k, line) in enumerate(rest):
@@ -361,7 +356,10 @@
     tables = [pltpu.VMEM((ACT_DEV, half), jnp.float32), pltpu.VMEM((rows, ACT_DEV), jnp.bfloat16)]
     flat_a, flat_b, squares_a, squares_b, *tables = pl.pallas_call(
         functools.partial(
-            early_kernel, [(k, lines_of[k]) for k in early], [(k, lines_of[k]) for k in last]
+            early_kernel,
+            [(k, lines_of[k]) for k in early],
+            [(k, lines_of[k]) for k in last],
+            len(totals),
         ),
         out_shape=[flat, flat, squares, squares] + tables * len(last),
         in_specs=[SMEM] + [VMEM] * (1 + len(totals) + len(early)),
@@ -458,7 +456,7 @@
     out_specs = P("col", "scen", None)
     groups, columns = mesh.shape["scen"], mesh.shape["col"]
     slice_width = NV // (groups * columns)
-    fits = groups == 8 and columns == 4 and slice_width % (2 * LANES) == 0
+    fits = groups == 8 and slice_width % (2 * LANES) == 0
     shard = functools.partial(
         jax.shard_map, mesh=mesh, in_specs=in_specs, out_specs=out_specs, check_vma=False
     )

time: 52.9 us -> 52.9 us (level)
  no operation moved by 1% of the time
where the time goes in v5:
time: 52.9 us; the launch traced here: 52.7 us
  waiting for transfers between devices  26.5 us (50%)
  starting transfers between devices  17.3 us (33%)
  Pallas kernels  8.91 us (17%)
    ppermute x12, waiting for transfers between devices, swap(): return lax.ppermute(value, 'scen', [(i, i ^ k) for i in range(groups)])  17.8 us
    ppermute x12, starting transfers between devices, swap(): return lax.ppermute(value, 'scen', [(i, i ^ k) for i in range(groups)])  10.7 us
    ppermute x3, waiting for transfers between devices, turn(): lax.ppermute(lines, 'col', [(i, (i + z) % columns) for i in range(columns)])  8.63 us
    ppermute x3, starting transfers between devices, turn(): lax.ppermute(lines, 'col', [(i, (i + z) % columns) for i in range(columns)])  6.6 us
    pallas_call x2, Pallas kernels, late(): pl.pallas_call(functools.partial(late_kernel, last, ACT_DEV * groups, n),...  3.36 us
    pallas_call x1, Pallas kernels, pick(): pl.pallas_call(functools.partial(first_kernel, groups, rows, tiles, ahead...  2.27 us
    pallas_call x1, Pallas kernels, finish(): pl.pallas_call(functools.partial(early_kernel, [(k, lines_of[k]) for k in...  1.88 us
    pallas_call x1, Pallas kernels, pick(): pl.pallas_call(functools.partial(second_kernel, tiles, behind), out_shape...  1.4 us
  transfers between devices with their start and end apart: 15, of which 9 were waited for; matrix products, arithmetic and copies ran while one was open for 0% of the time, Pallas kernels for 6%

profile of v5, /device:TPU:0, one launch (start us, length us, event | category | flops | bytes accessed | tf_op | source)
XLA Modules:
  0.0 52.7 jit_solution(17164997847691809880)
XLA Ops:
  0.0 2.3 %first.1 = (f32[256,256]{1,0:T(8,128)S(1)}, f32[16,520,128]{2,1,0:T(8,128)S(1)}, f32[256,128]{1,0:T(8,128)S(1)}, f32[512,8]{1,0:T(8,128)S(1)}, s32[512]{0:T(512)S(4)}, /*index=5*/s32[512]{0:T(512)S(4)}) custom-call(s32[4096]{0:T(1024)} %mask_ref.1, s32[512]{0:T(512)} %assign_ref.1, f32[512,2048]{1,0:T(8,128)} %coef_ref.1), custom_call_target="tpu_custom_call" | custom-call | tf_op jit(solution)/shard_map/first/pallas_call | solution.py:180
  2.3 1.4 %second.1 = (f32[256,256]{1,0:T(8,128)S(1)}, f32[264,256]{1,0:T(8,128)S(1)}, f32[256,256]{1,0:T(8,128)S(1)}, f32[256,256]{1,0:T(8,128)S(1)}, f32[256,256]{1,0:T(...) custom-call(f32[16,520,128]{2,1,0:T(8,128)S(1)} %get-tuple-element.3, ...), custom_call_target="tpu_custom_call" | custom-call | tf_op jit(solution)/shard_map/second/pallas_call | solution.py:194
  3.7 4.0 %collective-permute-start.2 = (f32[1,256]{1,0:T(1,128)S(1)}, f32[1,256]{1,0:T(1,128)S(1)}, u32[]{:S(2)}, u32[]{:S(2)}) collective-permute-start(f32[1,256]{1,0:T(1,128)S(1)} %get-tuple-element.37.refs_0_), channel_id=1, source_target_pairs={{0,24},{4,28},{8,16},{12,20},{16,8},{20,12},{24,0},{28,4},{1,25},{... | collective-permute-start | bytes 3080 | tf_op jit(solution)/shard_map/ppermute | solution.py:397
  7.7 0.5 collective-permute-start.1
  8.2 0.1 collective-permute-start
  8.3 0.9 %collective-permute-done.2.refs_3_ = f32[1,256]{1,0:T(1,128)S(1)} collective-permute-done((f32[1,256]{1,0:T(1,128)S(1)}, f32[1,256]{1,0:T(1,128)S(1)}, u32[]{:S(2)}, u32[]{:S(2)}) %collective-permute-start.2) | collective-permute-done | bytes 1056 | tf_op jit(solution)/shard_map/ppermute | solution.py:397
  9.2 2.0 %collective-permute-done.1.refs_2_ = f32[1,256]{1,0:T(1,128)S(1)} collective-permute-done((f32[1,256]{1,0:T(1,128)S(1)}, f32[1,256]{1,0:T(1,128)S(1)}, u32[]{:S(2)}, u32[]{:S(2)}) %collective-permute-start.1) | collective-permute-done | bytes 1056 | tf_op jit(solution)/shard_map/ppermute | solution.py:397
  11.2 0.5 collective-permute-done.refs_1_
  11.8 0.0 collective-permute-start.3
  11.8 1.6 %collective-permute-start.9 = (f32[256,256]{1,0:T(8,128)S(1)}, f32[256,256]{1,0:T(8,128)S(1)}, u32[]{:S(2)}, u32[]{:S(2)}) collective-permute-start(f32[256,256]{1,0:T(8,128)S(1)} %get-tuple-element.41), channel_id=1, source_target_pairs={{0,24},{4,28},{8,16},{12,20},{16,8},{20,12},{24,0},{28,4},{1,25},{... | collective-permute-start | bytes 786440 | tf_op jit(solution)/shard_map/ppermute | solution.py:397
  13.3 1.5 %collective-permute-start.7 = (f32[256,256]{1,0:T(8,128)S(1)}, f32[256,256]{1,0:T(8,128)S(1)}, u32[]{:S(2)}, u32[]{:S(2)}) collective-permute-start(f32[256,256]{1,0:T(8,128)S(1)} %get-tuple-element.39), channel_id=1, source_target_pairs={{0,8},{4,12},{8,0},{12,4},{16,24},{20,28},{24,16},{28,20},{1,9},{5... | collective-permute-start | bytes 786440 | tf_op jit(solution)/shard_map/ppermute | solution.py:397
  14.8 0.5 collective-permute-start.8
  15.3 0.7 %collective-permute-start.10 = (f32[256,256]{1,0:T(8,128)S(1)}, f32[256,256]{1,0:T(8,128)S(1)}, u32[]{:S(2)}, u32[]{:S(2)}) collective-permute-start(f32[256,256]{1,0:T(8,128)S(1)} %get-tuple-element.42), channel_id=1, source_target_pairs={{0,28},{4,24},{8,20},{12,16},{16,12},{20,8},{24,4},{28,0},{1,29},{... | collective-permute-start | bytes 786440 | tf_op jit(solution)/shard_map/ppermute | solution.py:397
  16.0 5.9 %collective-permute-done.9.refs_8_ = f32[256,256]{1,0:T(8,128)S(1)} collective-permute-done((f32[256,256]{1,0:T(8,128)S(1)}, f32[256,256]{1,0:T(8,128)S(1)}, u32[]{:S(2)}, u32[]{:S(2)}) %collective-permute-start.9) | collective-permute-done | bytes 262176 | tf_op jit(solution)/shard_map/ppermute | solution.py:397
  21.9 0.0 collective-permute-start.13
  21.9 5.7 %collective-permute-done.7.refs_6_ = f32[256,256]{1,0:T(8,128)S(1)} collective-permute-done((f32[256,256]{1,0:T(8,128)S(1)}, f32[256,256]{1,0:T(8,128)S(1)}, u32[]{:S(2)}, u32[]{:S(2)}) %collective-permute-start.7) | collective-permute-done | bytes 262176 | tf_op jit(solution)/shard_map/ppermute | solution.py:397
  27.6 0.0 collective-permute-start.14
  27.6 0.0 collective-permute-done.8.refs_7_
  27.6 0.4 collective-permute-start.11
  28.0 0.0 collective-permute-done.3.refs_1_.refs_5_
  28.0 1.5 %collective-permute-start.12 = (f32[256,128]{1,0:T(8,128)S(1)}, f32[256,128]{1,0:T(8,128)S(1)}, u32[]{:S(2)}, u32[]{:S(2)}) collective-permute-start(f32[256,128]{1,0:T(8,128)S(1)} %get-tuple-element.48), channel_id=1, source_target_pairs={{0,20},{4,16},{8,28},{12,24},{16,4},{20,0},{24,12},{28,8},{1,21},{... | collective-permute-start | bytes 393224 | tf_op jit(solution)/shard_map/ppermute | solution.py:397
  29.4 2.8 %collective-permute-done.10.refs_9_ = f32[256,256]{1,0:T(8,128)S(1)} collective-permute-done((f32[256,256]{1,0:T(8,128)S(1)}, f32[256,256]{1,0:T(8,128)S(1)}, u32[]{:S(2)}, u32[]{:S(2)}) %collective-permute-start.10) | collective-permute-done | bytes 262176 | tf_op jit(solution)/shard_map/ppermute | solution.py:397
  32.2 3.6 %collective-permute-start.6 = (f32[8,256]{1,0:T(8,128)S(1)}, f32[8,256]{1,0:T(8,128)S(1)}, u32[]{:S(2)}, u32[]{:S(2)}) collective-permute-start(f32[8,256]{1,0:T(8,128)S(1)} %stack.1.refs_0_), channel_id=1, source_target_pairs={{0,3},{1,0},{2,1},{3,2},{4,7},{5,4},{6,5},{7,6},{8,11},{9,8},{10,9... | collective-permute-start | bytes 24584 | tf_op jit(solution)/shard_map/ppermute | solution.py:408
  35.8 1.4 %collective-permute-done.6.refs_3_ = f32[8,256]{1,0:T(8,128)S(1)} collective-permute-done((f32[8,256]{1,0:T(8,128)S(1)}, f32[8,256]{1,0:T(8,128)S(1)}, u32[]{:S(2)}, u32[]{:S(2)}) %collective-permute-start.6) | collective-permute-done | bytes 8224 | tf_op jit(solution)/shard_map/ppermute | solution.py:408
  37.2 1.3 %collective-permute-start.5 = (f32[8,256]{1,0:T(8,128)S(1)}, f32[8,256]{1,0:T(8,128)S(1)}, u32[]{:S(2)}, u32[]{:S(2)}) collective-permute-start(f32[8,256]{1,0:T(8,128)S(1)} %stack.1.refs_0_), channel_id=1, source_target_pairs={{0,2},{1,3},{2,0},{3,1},{4,6},{5,7},{6,4},{7,5},{8,10},{9,11},{10,... | collective-permute-start | bytes 24584 | tf_op jit(solution)/shard_map/ppermute | solution.py:408
  38.5 3.3 %collective-permute-done.5.refs_2_ = f32[8,256]{1,0:T(8,128)S(1)} collective-permute-done((f32[8,256]{1,0:T(8,128)S(1)}, f32[8,256]{1,0:T(8,128)S(1)}, u32[]{:S(2)}, u32[]{:S(2)}) %collective-permute-start.5) | collective-permute-done | bytes 8224 | tf_op jit(solution)/shard_map/ppermute | solution.py:408
  41.7 1.7 %collective-permute-start.4 = (f32[8,256]{1,0:T(8,128)S(1)}, f32[8,256]{1,0:T(8,128)S(1)}, u32[]{:S(2)}, u32[]{:S(2)}) collective-permute-start(f32[8,256]{1,0:T(8,128)S(1)} %stack.1.refs_0_), channel_id=1, source_target_pairs={{0,1},{1,2},{2,3},{3,0},{4,5},{5,6},{6,7},{7,4},{8,9},{9,10},{10,1... | collective-permute-start | bytes 24584 | tf_op jit(solution)/shard_map/ppermute | solution.py:408
  43.5 4.0 %collective-permute-done.4.refs_1_ = f32[8,256]{1,0:T(8,128)S(1)} collective-permute-done((f32[8,256]{1,0:T(8,128)S(1)}, f32[8,256]{1,0:T(8,128)S(1)}, u32[]{:S(2)}, u32[]{:S(2)}) %collective-permute-start.4) | collective-permute-done | bytes 8224 | tf_op jit(solution)/shard_map/ppermute | solution.py:408
  47.5 1.9 %early.1 = (f32[4096,128]{1,0:T(8,128)S(1)}, f32[4096,128]{1,0:T(8,128)S(1)}, f32[8,128]{1,0:T(8,128)S(1)}, f32[8,128]{1,0:T(8,128)S(1)}, f32[256,128]{1,0:T(8,1...) custom-call(s32[512]{0:T(512)S(4)} %get-tuple-element.31.assign_ref, ...), custom_call_target="tpu_custom_call" | custom-call | tf_op jit(solution)/shard_map/early/pallas_call | solution.py:357
  49.3 0.0 collective-permute-done.13.refs_4_
  49.3 0.0 collective-permute-done.14.refs_5_
  49.4 1.5 %shard_map.37 = (f32[1,256,4096]{2,1,0:T(8,128)}, f32[128,4096]{1,0:T(8,128)S(1)}) custom-call(s32[512]{0:T(512)S(4)} %get-tuple-element.31.assign_ref, f32[256,128]{1,0:T(8,128)S(1)} %get-tuple-element.43.refs_0_, bf16[512,256]{1,0:T(8,128)(2,1)S(1)} %get-tuple-element.44.refs_1_, f32[256,128]{1,0:T(8,128)S(1)} %get-tuple-element.45.refs_2_, ...), custom_call_target="tpu_custom_call" | custom-call | tf_op jit(solution)/shard_map/pallas_call | solution.py:376
  50.9 0.0 collective-permute-done.11.refs_4_
  50.9 0.0 collective-permute-done.12.refs_5_
  50.9 1.8 %shard_map.38 = f32[1,256,4096]{2,1,0:T(8,128)} custom-call(s32[512]{0:T(512)S(4)} %get-tuple-element.31.assign_ref, f32[256,128]{1,0:T(8,128)S(1)} %get-tuple-element.43.refs_0_, bf16[512,256]{1,0:T(8,128)(2,1)S(1)} %get-tuple-element.44.refs_1_, f32[256,128]{1,0:T(8,128)S(1)} %get-tuple-element.45.refs_2_, ...), custom_call_target="tpu_custom_call", output_to_operand_aliasing={{}: (10, {})} | custom-call | tf_op jit(solution)/shard_map/pallas_call | solution.py:376
  (2 shorter events, 0.0 us)
Async XLA Ops:
  3.7 5.5 %collective-permute-start.2 = (f32[1,256]{1,0:T(1,128)S(1)}, f32[1,256]{1,0:T(1,128)S(1)}, u32[]{:S(2)}, u32[]{:S(2)}) collective-permute-start(f32[1,256]{1,0:T(1,128)S(1)} %get-tuple-element.37.refs_0_), channel_id=1, source_target_pairs={{0,24},{4,28},{8,16},{12,20},{16,8},{20,12},{24,0},{28,4},{1,25},{... | collective-permute-start | bytes 3080 | tf_op jit(solution)/shard_map/ppermute | solution.py:397
  7.7 3.6 %collective-permute-start.1 = (f32[1,256]{1,0:T(1,128)S(1)}, f32[1,256]{1,0:T(1,128)S(1)}, u32[]{:S(2)}, u32[]{:S(2)}) collective-permute-start(f32[1,256]{1,0:T(1,128)S(1)} %get-tuple-element.37.refs_0_), channel_id=1, source_target_pairs={{0,16},{4,20},{8,24},{12,28},{16,0},{20,4},{24,8},{28,12},{1,17},{... | collective-permute-start | bytes 3080 | tf_op jit(solution)/shard_map/ppermute | solution.py:397
  8.2 3.6 %collective-permute-start = (f32[1,256]{1,0:T(1,128)S(1)}, f32[1,256]{1,0:T(1,128)S(1)}, u32[]{:S(2)}, u32[]{:S(2)}) collective-permute-start(f32[1,256]{1,0:T(1,128)S(1)} %get-tuple-element.37.refs_0_), channel_id=1, source_target_pairs={{0,8},{4,12},{8,0},{12,4},{16,24},{20,28},{24,16},{28,20},{1,9},{5... | collective-permute-start | bytes 3080 | tf_op jit(solution)/shard_map/ppermute | solution.py:397
  11.8 16.2 %collective-permute-start.3 = (f32[264,256]{1,0:T(8,128)S(1)}, f32[264,256]{1,0:T(8,128)S(1)}, u32[]{:S(2)}, u32[]{:S(2)}) collective-permute-start(f32[264,256]{1,0:T(8,128)S(1)} %join.1.refs_0_), channel_id=1, source_target_pairs={{0,4},{4,0},{8,12},{12,8},{16,20},{20,16},{24,28},{28,24},{1,5},{5... | collective-permute-start | bytes 811016 | tf_op jit(solution)/shard_map/ppermute | solution.py:397
  11.8 10.2 %collective-permute-start.9 = (f32[256,256]{1,0:T(8,128)S(1)}, f32[256,256]{1,0:T(8,128)S(1)}, u32[]{:S(2)}, u32[]{:S(2)}) collective-permute-start(f32[256,256]{1,0:T(8,128)S(1)} %get-tuple-element.41), channel_id=1, source_target_pairs={{0,24},{4,28},{8,16},{12,20},{16,8},{20,12},{24,0},{28,4},{1,25},{... | collective-permute-start | bytes 786440 | tf_op jit(solution)/shard_map/ppermute | solution.py:397
  13.3 14.3 %collective-permute-start.7 = (f32[256,256]{1,0:T(8,128)S(1)}, f32[256,256]{1,0:T(8,128)S(1)}, u32[]{:S(2)}, u32[]{:S(2)}) collective-permute-start(f32[256,256]{1,0:T(8,128)S(1)} %get-tuple-element.39), channel_id=1, source_target_pairs={{0,8},{4,12},{8,0},{12,4},{16,24},{20,28},{24,16},{28,20},{1,9},{5... | collective-permute-start | bytes 786440 | tf_op jit(solution)/shard_map/ppermute | solution.py:397
  14.8 12.8 %collective-permute-start.8 = (f32[256,256]{1,0:T(8,128)S(1)}, f32[256,256]{1,0:T(8,128)S(1)}, u32[]{:S(2)}, u32[]{:S(2)}) collective-permute-start(f32[256,256]{1,0:T(8,128)S(1)} %get-tuple-element.40), channel_id=1, source_target_pairs={{0,16},{4,20},{8,24},{12,28},{16,0},{20,4},{24,8},{28,12},{1,17},{... | collective-permute-start | bytes 786440 | tf_op jit(solution)/shard_map/ppermute | solution.py:397
  15.3 16.9 %collective-permute-start.10 = (f32[256,256]{1,0:T(8,128)S(1)}, f32[256,256]{1,0:T(8,128)S(1)}, u32[]{:S(2)}, u32[]{:S(2)}) collective-permute-start(f32[256,256]{1,0:T(8,128)S(1)} %get-tuple-element.42), channel_id=1, source_target_pairs={{0,28},{4,24},{8,20},{12,16},{16,12},{20,8},{24,4},{28,0},{1,29},{... | collective-permute-start | bytes 786440 | tf_op jit(solution)/shard_map/ppermute | solution.py:397
  21.9 27.4 %collective-permute-start.13 = (f32[256,128]{1,0:T(8,128)S(1)}, f32[256,128]{1,0:T(8,128)S(1)}, u32[]{:S(2)}, u32[]{:S(2)}) collective-permute-start(f32[256,128]{1,0:T(8,128)S(1)} %get-tuple-element.51), channel_id=1, source_target_pairs={{0,12},{4,8},{8,4},{12,0},{16,28},{20,24},{24,20},{28,16},{1,13},{... | collective-permute-start | bytes 393224 | tf_op jit(solution)/shard_map/ppermute | solution.py:397
  27.6 21.7 %collective-permute-start.14 = (f32[256,128]{1,0:T(8,128)S(1)}, f32[256,128]{1,0:T(8,128)S(1)}, u32[]{:S(2)}, u32[]{:S(2)}) collective-permute-start(f32[256,128]{1,0:T(8,128)S(1)} %get-tuple-element.52), channel_id=1, source_target_pairs={{0,20},{4,16},{8,28},{12,24},{16,4},{20,0},{24,12},{28,8},{1,21},{... | collective-permute-start | bytes 393224 | tf_op jit(solution)/shard_map/ppermute | solution.py:397
  27.6 23.3 %collective-permute-start.11 = (f32[256,128]{1,0:T(8,128)S(1)}, f32[256,128]{1,0:T(8,128)S(1)}, u32[]{:S(2)}, u32[]{:S(2)}) collective-permute-start(f32[256,128]{1,0:T(8,128)S(1)} %get-tuple-element.47), channel_id=1, source_target_pairs={{0,12},{4,8},{8,4},{12,0},{16,28},{20,24},{24,20},{28,16},{1,13},{... | collective-permute-start | bytes 393224 | tf_op jit(solution)/shard_map/ppermute | solution.py:397
  28.0 22.9 %collective-permute-start.12 = (f32[256,128]{1,0:T(8,128)S(1)}, f32[256,128]{1,0:T(8,128)S(1)}, u32[]{:S(2)}, u32[]{:S(2)}) collective-permute-start(f32[256,128]{1,0:T(8,128)S(1)} %get-tuple-element.48), channel_id=1, source_target_pairs={{0,20},{4,16},{8,28},{12,24},{16,4},{20,0},{24,12},{28,8},{1,21},{... | collective-permute-start | bytes 393224 | tf_op jit(solution)/shard_map/ppermute | solution.py:397
  32.2 5.0 %collective-permute-start.6 = (f32[8,256]{1,0:T(8,128)S(1)}, f32[8,256]{1,0:T(8,128)S(1)}, u32[]{:S(2)}, u32[]{:S(2)}) collective-permute-start(f32[8,256]{1,0:T(8,128)S(1)} %stack.1.refs_0_), channel_id=1, source_target_pairs={{0,3},{1,0},{2,1},{3,2},{4,7},{5,4},{6,5},{7,6},{8,11},{9,8},{10,9... | collective-permute-start | bytes 24584 | tf_op jit(solution)/shard_map/ppermute | solution.py:408
  37.2 4.5 %collective-permute-start.5 = (f32[8,256]{1,0:T(8,128)S(1)}, f32[8,256]{1,0:T(8,128)S(1)}, u32[]{:S(2)}, u32[]{:S(2)}) collective-permute-start(f32[8,256]{1,0:T(8,128)S(1)} %stack.1.refs_0_), channel_id=1, source_target_pairs={{0,2},{1,3},{2,0},{3,1},{4,6},{5,7},{6,4},{7,5},{8,10},{9,11},{10,... | collective-permute-start | bytes 24584 | tf_op jit(solution)/shard_map/ppermute | solution.py:408
  41.7 5.7 %collective-permute-start.4 = (f32[8,256]{1,0:T(8,128)S(1)}, f32[8,256]{1,0:T(8,128)S(1)}, u32[]{:S(2)}, u32[]{:S(2)}) collective-permute-start(f32[8,256]{1,0:T(8,128)S(1)} %stack.1.refs_0_), channel_id=1, source_target_pairs={{0,1},{1,2},{2,3},{3,0},{4,5},{5,6},{6,7},{7,4},{8,9},{9,10},{10,1... | collective-permute-start | bytes 24584 | tf_op jit(solution)/shard_map/ppermute | solution.py:408

commit v6 on v5

--- a/solution.py
+++ b/solution.py
@@ -77,24 +77,20 @@
 
 def first_kernel(groups, rows, tiles, parts, mask_ref, assign_ref, coef_ref, *refs):
     outs = refs[: len(parts)]
-    window, squares, key_ref, order, slots, live, masks, sems, mask_sems = refs[len(parts) :]
+    squares, key_ref, order, slots, window, live, masks, sems, mask_sems = refs[len(parts) :]
     me = lax.axis_index("scen")
     cells = cells_of(parts, outs, tiles)
-    ahead = [t for t, _, _ in cells]
-    every = groups * tiles
-    runs = [(ahead[0], ahead[-1] + 1), (0, ahead[0]), (ahead[-1] + 1, every)]
-
-    def copy(run, t):
+    ahead = sorted({t for t, _, _ in cells})
+    cells = [(t - ahead[0], out, lane) for t, out, lane in cells]
+
+    def copy(t):
         k, h = divmod(t, tiles)
         column = pl.multiple_of((jnp.bitwise_xor(me, k) * tiles + h) * LANES, LANES)
         return pltpu.make_async_copy(
-            coef_ref.at[:, pl.ds(column, LANES)], window.at[t, pl.ds(0, rows)], sems.at[run]
+            coef_ref.at[:, pl.ds(column, LANES)],
+            window.at[t - ahead[0], pl.ds(0, rows)],
+            sems.at[t - ahead[0]],
         )
-
-    def wait(run):
-        start, end = runs[run]
-        landed = window.at[pl.ds(start, end - start), pl.ds(0, rows)]
-        pltpu.make_async_copy(landed, landed, sems.at[run]).wait()
 
     small = [
         pltpu.make_async_copy(mask_ref.at[pl.ds(me * rows, rows)], live, mask_sems.at[0]),
@@ -108,9 +104,8 @@
         return carry
 
     ahead_of_all(begin)
-    for run, (start, end) in enumerate(runs):
-        for t in range(start, end):
-            copy(run, t).start()
+    for t in ahead:
+        copy(t).start()
 
     def gather(i, carry):
         first = pl.multiple_of(i * SUBLANES, SUBLANES)
@@ -138,23 +133,34 @@
         order[n] = r
         n = n + live[r]
     key_ref[...] = jnp.where(marks > 0, rank, -1.0).T
-    wait(0)
+    for t in ahead:
+        copy(t).wait()
     lax.fori_loop(0, ACT_DEV // SUBLANES, gather, 0, unroll=2)
-    wait(1)
-    wait(2)
     small[2].wait()
 
 
-def second_kernel(tiles, parts, window, before, order, *refs):
+def second_kernel(tiles, parts, coef_ref, before, order, *refs):
     outs = refs[: len(parts)]
     part_ref, squares = refs[len(parts) :]
-    cells = cells_of(parts, outs, tiles)
+    me = lax.axis_index("scen")
+    across = lax.axis_size("scen") * tiles * SUBLANES
+    lane_row = lax.broadcasted_iota(jnp.int32, (SUBLANES, LANES), 0)
 
     def gather(i, carry):
         first = pl.multiple_of(i * SUBLANES, SUBLANES)
-        picks = [order[first + j] - j for j in range(SUBLANES)]
+        rows_at = [order[first + j] for j in range(SUBLANES)]
+        picks = [lax.shift_right_logical(r, 3) * across + jnp.bitwise_and(r, SUBLANES - 1) - j for j, r in enumerate(rows_at)]
         total = before[pl.ds(first, SUBLANES), :]
-        squares[pl.ds(first, SUBLANES), :] = pack(first, picks, window, cells, total)
+        for t, out, lane in cells_of(parts, outs, tiles):
+            k, h = divmod(t, tiles)
+            column = (jnp.bitwise_xor(me, k) * tiles + h) * SUBLANES
+            tile = jnp.zeros((SUBLANES, LANES), jnp.float32)
+            for j in range(SUBLANES):
+                line = coef_ref[pl.ds(picks[j] + column, SUBLANES), :]
+                tile = jnp.where(lane_row == j, line, tile)
+            out[pl.ds(first, SUBLANES), lane : lane + LANES] = tile
+            total = total + tile * tile
+        squares[pl.ds(first, SUBLANES), :] = total
         return carry
 
     lax.fori_loop(0, ACT_DEV // SUBLANES, gather, 0)
@@ -174,15 +180,16 @@
         ]
 
     squares = pltpu.VMEM((ACT_DEV, LANES), jnp.float32)
-    window = pltpu.VMEM((groups * tiles, rows + SUBLANES, LANES), jnp.float32)
+    window = pltpu.VMEM((tiles * len(ahead), rows + SUBLANES, LANES), jnp.float32)
     key = pltpu.VMEM((rows, groups), jnp.float32)
     listed = [pltpu.SMEM((rows,), jnp.int32), pltpu.SMEM(assign.shape, jnp.int32)]
-    *one, window, before, key, order, slots = pl.pallas_call(
+    *one, before, key, order, slots = pl.pallas_call(
         functools.partial(first_kernel, groups, rows, tiles, ahead),
-        out_shape=blocks(ahead) + [window, squares, key] + listed,
+        out_shape=blocks(ahead) + [squares, key] + listed,
         in_specs=[HBM, HBM, HBM],
-        out_specs=[VMEM] * (len(ahead) + 3) + [SMEM, SMEM],
+        out_specs=[VMEM] * (len(ahead) + 2) + [SMEM, SMEM],
         scratch_shapes=[
+            window,
             pltpu.SMEM((rows,), jnp.int32),
             pltpu.VMEM(mask.shape, jnp.int32),
             pltpu.SemaphoreType.DMA((3,)),
@@ -191,6 +198,8 @@
         name="first",
         compiler_params=PARAMS,
     )(*in_hbm(mask, assign, coef))
+    lined = coef.reshape(rows // SUBLANES, SUBLANES, groups * tiles, LANES)
+    lined = lined.transpose(0, 2, 1, 3).reshape(-1, LANES)
     *two, part = pl.pallas_call(
         functools.partial(second_kernel, tiles, behind),
         out_shape=blocks(behind) + [pltpu.VMEM((1, ACT_DEV), jnp.float32)],
@@ -199,7 +208,7 @@
         scratch_shapes=[squares],
         name="second",
         compiler_params=PARAMS,
-    )(*on_chip(window, before), scalars(order))
+    )(*on_chip(lined, before), scalars(order))
     found = zip(ahead + behind, one + two)
     return {(k, h0): block for (k, h0, _), block in found}, part, key, slots
 

time: 52.9 us -> 53.7 us (1.015)
    pallas_call x1, Pallas kernels: 1.4 us -> 2.14 us  [pick(): pl.pallas_call(functools.partial(second_kernel, tiles, behind), out_shape...]
where the time goes in v6:
time: 53.7 us; the launch traced here: 53.6 us
  waiting for transfers between devices  26.5 us (49%)
  starting transfers between devices  17.3 us (32%)
  Pallas kernels  9.37 us (17%)
    ppermute x12, waiting for transfers between devices, swap(): return lax.ppermute(value, 'scen', [(i, i ^ k) for i in range(groups)])  17.8 us
    ppermute x12, starting transfers between devices, swap(): return lax.ppermute(value, 'scen', [(i, i ^ k) for i in range(groups)])  10.7 us
    ppermute x3, waiting for transfers between devices, turn(): lax.ppermute(lines, 'col', [(i, (i + z) % columns) for i in range(columns)])  8.63 us
    ppermute x3, starting transfers between devices, turn(): lax.ppermute(lines, 'col', [(i, (i + z) % columns) for i in range(columns)])  6.6 us
    pallas_call x2, Pallas kernels, late(): pl.pallas_call(functools.partial(late_kernel, last, ACT_DEV * groups, n),...  3.36 us
    pallas_call x1, Pallas kernels, pick(): pl.pallas_call(functools.partial(second_kernel, tiles, behind), out_shape...  2.14 us
    pallas_call x1, Pallas kernels, pick(): pl.pallas_call(functools.partial(first_kernel, groups, rows, tiles, ahead...  1.99 us
    pallas_call x1, Pallas kernels, finish(): pl.pallas_call(functools.partial(early_kernel, [(k, lines_of[k]) for k in...  1.88 us
  transfers between devices with their start and end apart: 15, of which 9 were waited for; matrix products, arithmetic and copies ran while one was open for 0% of the time, Pallas kernels for 6%

profile of v6, /device:TPU:0, one launch (start us, length us, event | category | flops | bytes accessed | tf_op | source)
XLA Modules:
  0.0 53.6 jit_solution(10802657924763862840)
XLA Ops:
  0.0 0.0 copy-start
  0.0 2.0 %first.1 = (f32[256,256]{1,0:T(8,128)S(1)}, f32[256,128]{1,0:T(8,128)S(1)}, f32[512,8]{1,0:T(8,128)S(1)}, s32[512]{0:T(512)S(4)}, s32[512]{0:T(512)S(4)}) custom-call(s32[4096]{0:T(1024)} %mask_ref.1, s32[512]{0:T(512)} %assign_ref.1, f32[512,2048]{1,0:T(8,128)} %coef_ref.1), custom_call_target="tpu_custom_call" | custom-call | tf_op jit(solution)/shard_map/first/pallas_call | solution.py:186
  2.0 0.4 copy-done
  2.4 2.1 %second.1 = (f32[256,256]{1,0:T(8,128)S(1)}, f32[264,256]{1,0:T(8,128)S(1)}, f32[256,256]{1,0:T(8,128)S(1)}, f32[256,256]{1,0:T(8,128)S(1)}, f32[256,256]{1,0:T(...) custom-call(f32[8192,128]{1,0:T(8,128)S(1)} %bitcast.5, ...), custom_call_target="tpu_custom_call" | custom-call | tf_op jit(solution)/shard_map/second/pallas_call | solution.py:203
  4.5 4.0 %collective-permute-start.2 = (f32[1,256]{1,0:T(1,128)S(1)}, f32[1,256]{1,0:T(1,128)S(1)}, u32[]{:S(2)}, u32[]{:S(2)}) collective-permute-start(f32[1,256]{1,0:T(1,128)S(1)} %get-tuple-element.35.refs_0_), channel_id=1, source_target_pairs={{0,24},{4,28},{8,16},{12,20},{16,8},{20,12},{24,0},{28,4},{1,25},{... | collective-permute-start | bytes 3080 | tf_op jit(solution)/shard_map/ppermute | solution.py:406
  8.5 0.5 collective-permute-start.1
  9.0 0.1 collective-permute-start
  9.1 0.9 %collective-permute-done.2.refs_3_ = f32[1,256]{1,0:T(1,128)S(1)} collective-permute-done((f32[1,256]{1,0:T(1,128)S(1)}, f32[1,256]{1,0:T(1,128)S(1)}, u32[]{:S(2)}, u32[]{:S(2)}) %collective-permute-start.2) | collective-permute-done | bytes 1056 | tf_op jit(solution)/shard_map/ppermute | solution.py:406
  10.1 2.0 %collective-permute-done.1.refs_2_ = f32[1,256]{1,0:T(1,128)S(1)} collective-permute-done((f32[1,256]{1,0:T(1,128)S(1)}, f32[1,256]{1,0:T(1,128)S(1)}, u32[]{:S(2)}, u32[]{:S(2)}) %collective-permute-start.1) | collective-permute-done | bytes 1056 | tf_op jit(solution)/shard_map/ppermute | solution.py:406
  12.1 0.5 collective-permute-done.refs_1_
  12.6 0.0 collective-permute-start.3
  12.6 1.6 %collective-permute-start.9 = (f32[256,256]{1,0:T(8,128)S(1)}, f32[256,256]{1,0:T(8,128)S(1)}, u32[]{:S(2)}, u32[]{:S(2)}) collective-permute-start(f32[256,256]{1,0:T(8,128)S(1)} %get-tuple-element.39), channel_id=1, source_target_pairs={{0,24},{4,28},{8,16},{12,20},{16,8},{20,12},{24,0},{28,4},{1,25},{... | collective-permute-start | bytes 786440 | tf_op jit(solution)/shard_map/ppermute | solution.py:406
  14.1 1.5 %collective-permute-start.7 = (f32[256,256]{1,0:T(8,128)S(1)}, f32[256,256]{1,0:T(8,128)S(1)}, u32[]{:S(2)}, u32[]{:S(2)}) collective-permute-start(f32[256,256]{1,0:T(8,128)S(1)} %get-tuple-element.37), channel_id=1, source_target_pairs={{0,8},{4,12},{8,0},{12,4},{16,24},{20,28},{24,16},{28,20},{1,9},{5... | collective-permute-start | bytes 786440 | tf_op jit(solution)/shard_map/ppermute | solution.py:406
  15.6 0.5 collective-permute-start.8
  16.1 0.7 %collective-permute-start.10 = (f32[256,256]{1,0:T(8,128)S(1)}, f32[256,256]{1,0:T(8,128)S(1)}, u32[]{:S(2)}, u32[]{:S(2)}) collective-permute-start(f32[256,256]{1,0:T(8,128)S(1)} %get-tuple-element.40), channel_id=1, source_target_pairs={{0,28},{4,24},{8,20},{12,16},{16,12},{20,8},{24,4},{28,0},{1,29},{... | collective-permute-start | bytes 786440 | tf_op jit(solution)/shard_map/ppermute | solution.py:406
  16.8 5.9 %collective-permute-done.9.refs_8_ = f32[256,256]{1,0:T(8,128)S(1)} collective-permute-done((f32[256,256]{1,0:T(8,128)S(1)}, f32[256,256]{1,0:T(8,128)S(1)}, u32[]{:S(2)}, u32[]{:S(2)}) %collective-permute-start.9) | collective-permute-done | bytes 262176 | tf_op jit(solution)/shard_map/ppermute | solution.py:406
  22.8 0.0 collective-permute-start.13
  22.8 5.7 %collective-permute-done.7.refs_6_ = f32[256,256]{1,0:T(8,128)S(1)} collective-permute-done((f32[256,256]{1,0:T(8,128)S(1)}, f32[256,256]{1,0:T(8,128)S(1)}, u32[]{:S(2)}, u32[]{:S(2)}) %collective-permute-start.7) | collective-permute-done | bytes 262176 | tf_op jit(solution)/shard_map/ppermute | solution.py:406
  28.4 0.0 collective-permute-start.14
  28.5 0.0 collective-permute-done.8.refs_7_
  28.5 0.4 collective-permute-start.11
  28.8 0.0 collective-permute-done.3.refs_1_.refs_5_
  28.8 1.5 %collective-permute-start.12 = (f32[256,128]{1,0:T(8,128)S(1)}, f32[256,128]{1,0:T(8,128)S(1)}, u32[]{:S(2)}, u32[]{:S(2)}) collective-permute-start(f32[256,128]{1,0:T(8,128)S(1)} %get-tuple-element.46), channel_id=1, source_target_pairs={{0,20},{4,16},{8,28},{12,24},{16,4},{20,0},{24,12},{28,8},{1,21},{... | collective-permute-start | bytes 393224 | tf_op jit(solution)/shard_map/ppermute | solution.py:406
  30.3 2.8 %collective-permute-done.10.refs_9_ = f32[256,256]{1,0:T(8,128)S(1)} collective-permute-done((f32[256,256]{1,0:T(8,128)S(1)}, f32[256,256]{1,0:T(8,128)S(1)}, u32[]{:S(2)}, u32[]{:S(2)}) %collective-permute-start.10) | collective-permute-done | bytes 262176 | tf_op jit(solution)/shard_map/ppermute | solution.py:406
  33.1 3.6 %collective-permute-start.6 = (f32[8,256]{1,0:T(8,128)S(1)}, f32[8,256]{1,0:T(8,128)S(1)}, u32[]{:S(2)}, u32[]{:S(2)}) collective-permute-start(f32[8,256]{1,0:T(8,128)S(1)} %stack.1.refs_0_), channel_id=1, source_target_pairs={{0,3},{1,0},{2,1},{3,2},{4,7},{5,4},{6,5},{7,6},{8,11},{9,8},{10,9... | collective-permute-start | bytes 24584 | tf_op jit(solution)/shard_map/ppermute | solution.py:417
  36.7 1.4 %collective-permute-done.6.refs_3_ = f32[8,256]{1,0:T(8,128)S(1)} collective-permute-done((f32[8,256]{1,0:T(8,128)S(1)}, f32[8,256]{1,0:T(8,128)S(1)}, u32[]{:S(2)}, u32[]{:S(2)}) %collective-permute-start.6) | collective-permute-done | bytes 8224 | tf_op jit(solution)/shard_map/ppermute | solution.py:417
  38.0 1.3 %collective-permute-start.5 = (f32[8,256]{1,0:T(8,128)S(1)}, f32[8,256]{1,0:T(8,128)S(1)}, u32[]{:S(2)}, u32[]{:S(2)}) collective-permute-start(f32[8,256]{1,0:T(8,128)S(1)} %stack.1.refs_0_), channel_id=1, source_target_pairs={{0,2},{1,3},{2,0},{3,1},{4,6},{5,7},{6,4},{7,5},{8,10},{9,11},{10,... | collective-permute-start | bytes 24584 | tf_op jit(solution)/shard_map/ppermute | solution.py:417
  39.3 3.3 %collective-permute-done.5.refs_2_ = f32[8,256]{1,0:T(8,128)S(1)} collective-permute-done((f32[8,256]{1,0:T(8,128)S(1)}, f32[8,256]{1,0:T(8,128)S(1)}, u32[]{:S(2)}, u32[]{:S(2)}) %collective-permute-start.5) | collective-permute-done | bytes 8224 | tf_op jit(solution)/shard_map/ppermute | solution.py:417
  42.6 1.7 %collective-permute-start.4 = (f32[8,256]{1,0:T(8,128)S(1)}, f32[8,256]{1,0:T(8,128)S(1)}, u32[]{:S(2)}, u32[]{:S(2)}) collective-permute-start(f32[8,256]{1,0:T(8,128)S(1)} %stack.1.refs_0_), channel_id=1, source_target_pairs={{0,1},{1,2},{2,3},{3,0},{4,5},{5,6},{6,7},{7,4},{8,9},{9,10},{10,1... | collective-permute-start | bytes 24584 | tf_op jit(solution)/shard_map/ppermute | solution.py:417
  44.3 4.0 %collective-permute-done.4.refs_1_ = f32[8,256]{1,0:T(8,128)S(1)} collective-permute-done((f32[8,256]{1,0:T(8,128)S(1)}, f32[8,256]{1,0:T(8,128)S(1)}, u32[]{:S(2)}, u32[]{:S(2)}) %collective-permute-start.4) | collective-permute-done | bytes 8224 | tf_op jit(solution)/shard_map/ppermute | solution.py:417
  48.3 1.9 %early.1 = (f32[4096,128]{1,0:T(8,128)S(1)}, f32[4096,128]{1,0:T(8,128)S(1)}, f32[8,128]{1,0:T(8,128)S(1)}, f32[8,128]{1,0:T(8,128)S(1)}, f32[256,128]{1,0:T(8,1...) custom-call(s32[512]{0:T(512)S(4)} %get-tuple-element.30.assign_ref, ...), custom_call_target="tpu_custom_call" | custom-call | tf_op jit(solution)/shard_map/early/pallas_call | solution.py:366
  50.2 0.0 collective-permute-done.13.refs_4_
  50.2 0.0 collective-permute-done.14.refs_5_
  50.2 1.5 %shard_map.37 = (f32[1,256,4096]{2,1,0:T(8,128)}, f32[128,4096]{1,0:T(8,128)S(1)}) custom-call(s32[512]{0:T(512)S(4)} %get-tuple-element.30.assign_ref, f32[256,128]{1,0:T(8,128)S(1)} %get-tuple-element.41.refs_0_, bf16[512,256]{1,0:T(8,128)(2,1)S(1)} %get-tuple-element.42.refs_1_, f32[256,128]{1,0:T(8,128)S(1)} %get-tuple-element.43.refs_2_, ...), custom_call_target="tpu_custom_call" | custom-call | tf_op jit(solution)/shard_map/pallas_call | solution.py:385
  51.7 0.0 collective-permute-done.11.refs_4_
  51.7 0.0 collective-permute-done.12.refs_5_
  51.7 1.8 %shard_map.38 = f32[1,256,4096]{2,1,0:T(8,128)} custom-call(s32[512]{0:T(512)S(4)} %get-tuple-element.30.assign_ref, f32[256,128]{1,0:T(8,128)S(1)} %get-tuple-element.41.refs_0_, bf16[512,256]{1,0:T(8,128)(2,1)S(1)} %get-tuple-element.42.refs_1_, f32[256,128]{1,0:T(8,128)S(1)} %get-tuple-element.43.refs_2_, ...), custom_call_target="tpu_custom_call", output_to_operand_aliasing={{}: (10, {})} | custom-call | tf_op jit(solution)/shard_map/pallas_call | solution.py:385
  (2 shorter events, 0.0 us)
Async XLA Ops:
  0.0 2.4 %copy-start = (f32[512,2048]{1,0:T(8,128)S(1)}, f32[512,2048]{1,0:T(8,128)}, u32[]{:S(2)}) copy-start(f32[512,2048]{1,0:T(8,128)} %coef_ref.1) | copy-start | bytes 12582916
  4.5 5.5 %collective-permute-start.2 = (f32[1,256]{1,0:T(1,128)S(1)}, f32[1,256]{1,0:T(1,128)S(1)}, u32[]{:S(2)}, u32[]{:S(2)}) collective-permute-start(f32[1,256]{1,0:T(1,128)S(1)} %get-tuple-element.35.refs_0_), channel_id=1, source_target_pairs={{0,24},{4,28},{8,16},{12,20},{16,8},{20,12},{24,0},{28,4},{1,25},{... | collective-permute-start | bytes 3080 | tf_op jit(solution)/shard_map/ppermute | solution.py:406
  8.5 3.6 %collective-permute-start.1 = (f32[1,256]{1,0:T(1,128)S(1)}, f32[1,256]{1,0:T(1,128)S(1)}, u32[]{:S(2)}, u32[]{:S(2)}) collective-permute-start(f32[1,256]{1,0:T(1,128)S(1)} %get-tuple-element.35.refs_0_), channel_id=1, source_target_pairs={{0,16},{4,20},{8,24},{12,28},{16,0},{20,4},{24,8},{28,12},{1,17},{... | collective-permute-start | bytes 3080 | tf_op jit(solution)/shard_map/ppermute | solution.py:406
  9.0 3.6 %collective-permute-start = (f32[1,256]{1,0:T(1,128)S(1)}, f32[1,256]{1,0:T(1,128)S(1)}, u32[]{:S(2)}, u32[]{:S(2)}) collective-permute-start(f32[1,256]{1,0:T(1,128)S(1)} %get-tuple-element.35.refs_0_), channel_id=1, source_target_pairs={{0,8},{4,12},{8,0},{12,4},{16,24},{20,28},{24,16},{28,20},{1,9},{5... | collective-permute-start | bytes 3080 | tf_op jit(solution)/shard_map/ppermute | solution.py:406
  12.6 16.2 %collective-permute-start.3 = (f32[264,256]{1,0:T(8,128)S(1)}, f32[264,256]{1,0:T(8,128)S(1)}, u32[]{:S(2)}, u32[]{:S(2)}) collective-permute-start(f32[264,256]{1,0:T(8,128)S(1)} %join.1.refs_0_), channel_id=1, source_target_pairs={{0,4},{4,0},{8,12},{12,8},{16,20},{20,16},{24,28},{28,24},{1,5},{5... | collective-permute-start | bytes 811016 | tf_op jit(solution)/shard_map/ppermute | solution.py:406
  12.6 10.2 %collective-permute-start.9 = (f32[256,256]{1,0:T(8,128)S(1)}, f32[256,256]{1,0:T(8,128)S(1)}, u32[]{:S(2)}, u32[]{:S(2)}) collective-permute-start(f32[256,256]{1,0:T(8,128)S(1)} %get-tuple-element.39), channel_id=1, source_target_pairs={{0,24},{4,28},{8,16},{12,20},{16,8},{20,12},{24,0},{28,4},{1,25},{... | collective-permute-start | bytes 786440 | tf_op jit(solution)/shard_map/ppermute | solution.py:406
  14.1 14.3 %collective-permute-start.7 = (f32[256,256]{1,0:T(8,128)S(1)}, f32[256,256]{1,0:T(8,128)S(1)}, u32[]{:S(2)}, u32[]{:S(2)}) collective-permute-start(f32[256,256]{1,0:T(8,128)S(1)} %get-tuple-element.37), channel_id=1, source_target_pairs={{0,8},{4,12},{8,0},{12,4},{16,24},{20,28},{24,16},{28,20},{1,9},{5... | collective-permute-start | bytes 786440 | tf_op jit(solution)/shard_map/ppermute | solution.py:406
  15.6 12.8 %collective-permute-start.8 = (f32[256,256]{1,0:T(8,128)S(1)}, f32[256,256]{1,0:T(8,128)S(1)}, u32[]{:S(2)}, u32[]{:S(2)}) collective-permute-start(f32[256,256]{1,0:T(8,128)S(1)} %get-tuple-element.38), channel_id=1, source_target_pairs={{0,16},{4,20},{8,24},{12,28},{16,0},{20,4},{24,8},{28,12},{1,17},{... | collective-permute-start | bytes 786440 | tf_op jit(solution)/shard_map/ppermute | solution.py:406
  16.1 16.9 %collective-permute-start.10 = (f32[256,256]{1,0:T(8,128)S(1)}, f32[256,256]{1,0:T(8,128)S(1)}, u32[]{:S(2)}, u32[]{:S(2)}) collective-permute-start(f32[256,256]{1,0:T(8,128)S(1)} %get-tuple-element.40), channel_id=1, source_target_pairs={{0,28},{4,24},{8,20},{12,16},{16,12},{20,8},{24,4},{28,0},{1,29},{... | collective-permute-start | bytes 786440 | tf_op jit(solution)/shard_map/ppermute | solution.py:406
  22.8 27.4 %collective-permute-start.13 = (f32[256,128]{1,0:T(8,128)S(1)}, f32[256,128]{1,0:T(8,128)S(1)}, u32[]{:S(2)}, u32[]{:S(2)}) collective-permute-start(f32[256,128]{1,0:T(8,128)S(1)} %get-tuple-element.49), channel_id=1, source_target_pairs={{0,12},{4,8},{8,4},{12,0},{16,28},{20,24},{24,20},{28,16},{1,13},{... | collective-permute-start | bytes 393224 | tf_op jit(solution)/shard_map/ppermute | solution.py:406
  28.4 21.7 %collective-permute-start.14 = (f32[256,128]{1,0:T(8,128)S(1)}, f32[256,128]{1,0:T(8,128)S(1)}, u32[]{:S(2)}, u32[]{:S(2)}) collective-permute-start(f32[256,128]{1,0:T(8,128)S(1)} %get-tuple-element.50), channel_id=1, source_target_pairs={{0,20},{4,16},{8,28},{12,24},{16,4},{20,0},{24,12},{28,8},{1,21},{... | collective-permute-start | bytes 393224 | tf_op jit(solution)/shard_map/ppermute | solution.py:406
  28.5 23.3 %collective-permute-start.11 = (f32[256,128]{1,0:T(8,128)S(1)}, f32[256,128]{1,0:T(8,128)S(1)}, u32[]{:S(2)}, u32[]{:S(2)}) collective-permute-start(f32[256,128]{1,0:T(8,128)S(1)} %get-tuple-element.45), channel_id=1, source_target_pairs={{0,12},{4,8},{8,4},{12,0},{16,28},{20,24},{24,20},{28,16},{1,13},{... | collective-permute-start | bytes 393224 | tf_op jit(solution)/shard_map/ppermute | solution.py:406
  28.8 22.9 %collective-permute-start.12 = (f32[256,128]{1,0:T(8,128)S(1)}, f32[256,128]{1,0:T(8,128)S(1)}, u32[]{:S(2)}, u32[]{:S(2)}) collective-permute-start(f32[256,128]{1,0:T(8,128)S(1)} %get-tuple-element.46), channel_id=1, source_target_pairs={{0,20},{4,16},{8,28},{12,24},{16,4},{20,0},{24,12},{28,8},{1,21},{... | collective-permute-start | bytes 393224 | tf_op jit(solution)/shard_map/ppermute | solution.py:406
  33.1 5.0 %collective-permute-start.6 = (f32[8,256]{1,0:T(8,128)S(1)}, f32[8,256]{1,0:T(8,128)S(1)}, u32[]{:S(2)}, u32[]{:S(2)}) collective-permute-start(f32[8,256]{1,0:T(8,128)S(1)} %stack.1.refs_0_), channel_id=1, source_target_pairs={{0,3},{1,0},{2,1},{3,2},{4,7},{5,4},{6,5},{7,6},{8,11},{9,8},{10,9... | collective-permute-start | bytes 24584 | tf_op jit(solution)/shard_map/ppermute | solution.py:417
  38.0 4.5 %collective-permute-start.5 = (f32[8,256]{1,0:T(8,128)S(1)}, f32[8,256]{1,0:T(8,128)S(1)}, u32[]{:S(2)}, u32[]{:S(2)}) collective-permute-start(f32[8,256]{1,0:T(8,128)S(1)} %stack.1.refs_0_), channel_id=1, source_target_pairs={{0,2},{1,3},{2,0},{3,1},{4,6},{5,7},{6,4},{7,5},{8,10},{9,11},{10,... | collective-permute-start | bytes 24584 | tf_op jit(solution)/shard_map/ppermute | solution.py:417
  42.6 5.7 %collective-permute-start.4 = (f32[8,256]{1,0:T(8,128)S(1)}, f32[8,256]{1,0:T(8,128)S(1)}, u32[]{:S(2)}, u32[]{:S(2)}) collective-permute-start(f32[8,256]{1,0:T(8,128)S(1)} %stack.1.refs_0_), channel_id=1, source_target_pairs={{0,1},{1,2},{2,3},{3,0},{4,5},{5,6},{6,7},{7,4},{8,9},{9,10},{10,1... | collective-permute-start | bytes 24584 | tf_op jit(solution)/shard_map/ppermute | solution.py:417
